TPU v7x, 16 devices: a 4x2x1 block of a 4x4x8 slice. The times are simulated.
16 devices in a mesh: dp: 2 (over y, z), sp: 8 (over x, core).
Axes of the slice: x: 4, y: 2, z: 1, core: 2. Of those that a mesh axis runs over, the one named last changes fastest.
The devices are a block of a 4x4x8 slice.
Arguments:
- u_in: bfloat16 [2, 16384, 1024], P('dp', 'sp'), parts along dimension 0
- w_in: bfloat16 [1024, 3072], replicated
- b_in: float32 [3072], replicated
- conv_taps: float32 [3, 3072], replicated
- w_out: bfloat16 [1024, 1024], replicated
- skip_one: float32 [1024], replicated
- skip_two: float32 [1024], replicated
- filt_one: float32 [16384, 1024], P('sp')
- filt_two: float32 [16384, 1024], P('sp')
Outputs:
- output: bfloat16 [2, 16384, 1024], P('dp', 'sp'), parts along dimension 0
There are 2 independent parts. A program takes and returns all parts, laid end to end along the dimension named above; an argument that names none is the same for every part.
All inputs are finite; a program needn't handle non-finite values.
Results may differ from a plain program's by a relative error of at most 0.0149239.
Values sent between devices are 32-bit elements.
A program may use at most 768 MiB of HBM per device.

v0:
```python
import math
import jax
import jax.numpy as jnp
from jax import lax
from jax.sharding import PartitionSpec as P


def phase_table(row_idx, col_idx, fft_len, phase_sign):
    phase_angle = (phase_sign * 2.0 * math.pi / fft_len) * (row_idx[:, None] * col_idx[None, :]).astype(jnp.float32)
    return lax.complex(jnp.cos(phase_angle), jnp.sin(phase_angle))


def to_spectrum(signal, n_dev, dev_rank):
    groups, seq_len, channels = signal.shape
    piece_len = seq_len // n_dev
    fft_len = 2 * n_dev * seq_len
    by_block = lax.all_to_all(signal.reshape(groups, n_dev, piece_len, channels), 'sp', 1, 1, tiled=True)
    coarse = jnp.fft.fft(by_block, n=2 * n_dev, axis=1)
    pos_local = dev_rank * piece_len + jnp.arange(piece_len)
    coarse = coarse * phase_table(jnp.arange(2 * n_dev), pos_local, fft_len, -1.0)[None, :, :, None]
    pair_parts = lax.all_to_all(jnp.stack([coarse.real, coarse.imag]), 'sp', 2, 3, tiled=True)
    return jnp.fft.fft(lax.complex(pair_parts[0], pair_parts[1]), axis=2)


def from_spectrum(spectrum_in, n_dev, dev_rank):
    groups, seq_len, channels = spectrum_in.shape[0], spectrum_in.shape[2], spectrum_in.shape[3]
    fft_len = 2 * n_dev * seq_len
    fine_part = jnp.fft.ifft(spectrum_in, axis=2)
    own_freq = 2 * dev_rank + jnp.arange(2)
    fine_part = fine_part * phase_table(own_freq, jnp.arange(seq_len), fft_len, 1.0)[None, :, :, None]
    pair_parts = lax.all_to_all(jnp.stack([fine_part.real, fine_part.imag]), 'sp', 3, 2, tiled=True)
    coarse = jnp.fft.ifft(lax.complex(pair_parts[0], pair_parts[1]), axis=1)[:, :n_dev].real
    restored = lax.all_to_all(coarse, 'sp', 1, 1, tiled=True)
    return restored.reshape(groups, seq_len, channels)


def solution(mesh):
    n_dev = mesh.shape['sp']
    halo_perm = list(zip(range(n_dev - 1), range(1, n_dev)))

    def local_step(u_in, w_in, b_in, conv_taps, w_out, skip_one, skip_two, filt_one, filt_two):
        dev_rank = lax.axis_index('sp')
        model_width = u_in.shape[2]
        projected = (jnp.einsum('bsd,de->bse', u_in, w_in, preferred_element_type=jnp.float32) + b_in).astype(jnp.bfloat16).astype(jnp.float32)
        tail_rows = lax.ppermute(projected[:, -2:], 'sp', halo_perm)
        extended = jnp.concatenate([tail_rows, projected], axis=1)
        mixed = (conv_taps[0] * extended[:, 2:] + conv_taps[1] * extended[:, 1:-1] + conv_taps[2] * extended[:, :-2]).astype(jnp.bfloat16).astype(jnp.float32)
        gate_one = mixed[..., :model_width]
        gate_two = mixed[..., model_width:2 * model_width]
        values = mixed[..., 2 * model_width:]
        spec_one = to_spectrum(filt_one[None], n_dev, dev_rank)
        spec_two = to_spectrum(filt_two[None], n_dev, dev_rank)
        conv_one = from_spectrum(to_spectrum(values, n_dev, dev_rank) * spec_one, n_dev, dev_rank)
        z_one = gate_one * (conv_one + skip_one * values)
        conv_two = from_spectrum(to_spectrum(z_one, n_dev, dev_rank) * spec_two, n_dev, dev_rank)
        gated = gate_two * (conv_two + skip_two * z_one)
        out_sum = u_in.astype(jnp.float32) + jnp.einsum('bsd,de->bse', gated.astype(jnp.bfloat16), w_out, preferred_element_type=jnp.float32)
        return out_sum.astype(jnp.bfloat16)

    seq_spec = P('dp', 'sp', None)
    filt_spec = P('sp', None)
    return jax.shard_map(local_step, mesh=mesh, in_specs=(seq_spec, P(), P(), P(), P(), P(), P(), filt_spec, filt_spec), out_specs=seq_spec, check_vma=False)
```

profile of v0, /device:TPU:113, one launch (start us, length us, event | category | flops | bytes accessed | tf_op | source)
XLA Modules:
  0.0 5411.3 jit_solution(2477212058570943851)
XLA Ops:
  36.4 60.6 %collective-permute-done = f32[1,2,3072]{2,1,0:T(2,128)S(1)} collective-permute-done((f32[1,2,3072]{2,1,0:T(2,128)S(1)}, f32[1,2,3072]{2,1,0:T(2,128)S(1)}, u32[]{:S(2)}, u32[]{:S(2)}) %collective-permute-start) | collective-permute-done | bytes 24608 | tf_op jit(solution)/shard_map/ppermute | solution.py:45
  175.9 44.9 all-to-all-done
  283.8 60.2 %fusion.76 = (f32[1,1,16,256,1024]{4,2,3,1,0:T(8,128)}, f32[1,1,16,256,1024]{4,2,3,1,0:T(8,128)}, f32[1,1,16,256,1024]{4,2,3,1,0:T(8,128)}, f32[1,1,16,256,1024]{4,2,3,1,0:T(8,128)}) fusion(f32[256,1024,16]{1,2,0:T(8,128)} %fusion.162, f32[16,256]{0,1:T(8,128)S(1)} %copy.341, f32[16,256]{0,1:T(8,128)S(1)} %copy.340, f32[256,1024,16]{1,2,0:T(8,128)} %fusion.81, ...), kind=kOutput, calls=%fused_computation.154 | convolution fusion | flops 868222208 | bytes 142639104 | tf_op jit(solution)/shard_map/jit(fft) | solution.py:18
  356.2 35.7 copy.356
  412.2 35.7 copy.342
  447.9 315.4 %all-to-all-done.3 = f32[2,1,16,256,1024]{4,3,1,0,2:T(8,128)} async-done(((f32[2,1,16,256,1024]{4,3,1,0,2:T(8,128)}), f32[2,1,16,256,1024]{4,3,1,0,2:T(8,128)}, u32[]{:S(2)}, u32[]{:S(2)}) %all-to-all-start.3) | async-done | bytes 33554464 | tf_op jit(solution)/shard_map/all_to_all | solution.py:21
  850.5 34.6 fusion.141
  885.1 40.4 fusion.143
  925.5 209.6 %all-to-all-done.1 = f32[2,1,16,256,1024]{4,3,1,0,2:T(8,128)} async-done(((f32[2,1,16,256,1024]{4,3,1,0,2:T(8,128)}), f32[2,1,16,256,1024]{4,3,1,0,2:T(8,128)}, u32[]{:S(2)}, u32[]{:S(2)}) %all-to-all-start.1) | async-done | bytes 33554464 | tf_op jit(solution)/shard_map/all_to_all | solution.py:21
  1199.0 34.8 fusion.151
  1247.8 40.8 fusion.153
  1288.6 34.5 fusion.145
  1323.1 74.4 %add_bitcast_fusion.9 = (f32[2,1024,128,16]{2,1,3,0:T(8,128)}, f32[1,2,1024,128,16]{3,2,4,1,0:T(8,128)}, f32[1,2,1024,128,16]{3,2,4,1,0:T(8,128)}, f32[2,1024,12...) fusion(f32[128,16]{0,1:T(8,128)S(1)} %copy-done.17, ...), kind=kOutput, calls=%fused_computation.254 | convolution fusion | flops 6518013952 | bytes 201342976 | tf_op jit(solution)/shard_map/jit(fft)/dot.27 | solution.py:22
  1430.3 35.8 subtract_bitcast_fusion.3
  1515.2 35.7 subtract_bitcast_fusion.2
  1567.2 35.9 add_bitcast_fusion.8
  1619.5 36.0 add_bitcast_fusion.6
  1706.2 40.3 fusion.127
  1759.1 34.5 fusion.129
  1793.5 47.8 add_bitcast_fusion.5
  1906.2 37.6 multiply_bitcast_fusion.3
  2015.7 49.4 copy.387
  2065.2 375.7 %all_to_all.114 = f32[2,1,2,2048,1024]{4,2,1,0,3:T(2,128)} all-to-all(f32[2,1,2,2048,1024]{4,2,1,0,3:T(2,128)} %copy.387), channel_id=1, replica_groups=mesh['dp'=2,'sp'=8] {'sp'}, dimensions={3} | all-to-all | bytes 67108864 | tf_op jit(solution)/shard_map/all_to_all | solution.py:31
  2610.3 98.0 %all_to_all.115 = f32[1,8,256,1024]{3,2,0,1:T(8,128)} all-to-all(f32[1,8,256,1024]{3,2,0,1:T(8,128)S(1)} %copy.389), channel_id=1, replica_groups=mesh['dp'=2,'sp'=8] {'sp'}, dimensions={1} | all-to-all | bytes 16777216 | tf_op jit(solution)/shard_map/all_to_all | solution.py:33
  2727.7 80.2 %all-to-all-done.8 = f32[1,8,256,1024]{3,2,0,1:T(8,128)} async-done(((f32[1,8,256,1024]{3,2,0,1:T(8,128)}), f32[1,8,256,1024]{3,2,0,1:T(8,128)}, u32[]{:S(2)}, u32[]{:S(2)}) %all-to-all-start.8) | async-done | bytes 8388640 | tf_op jit(solution)/shard_map/all_to_all | solution.py:17
  2850.5 57.4 %all-to-all-done.6 = f32[1,8,256,1024]{3,2,0,1:T(8,128)} async-done(((f32[1,8,256,1024]{3,2,0,1:T(8,128)}), f32[1,8,256,1024]{3,2,0,1:T(8,128)}, u32[]{:S(2)}, u32[]{:S(2)}) %all-to-all-start.6) | async-done | bytes 8388640 | tf_op jit(solution)/shard_map/all_to_all | solution.py:17
  2970.5 60.5 %fusion.43 = (f32[1,1,16,256,1024]{4,2,3,1,0:T(8,128)}, f32[1,1,16,256,1024]{4,2,3,1,0:T(8,128)}, f32[1,1,16,256,1024]{4,2,3,1,0:T(8,128)}, f32[1,1,16,256,1024]{4,2,3,1,0:T(8,128)}) fusion(f32[256,1024,16]{1,2,0:T(8,128)} %fusion.168, f32[16,256]{0,1:T(8,128)S(1)} %copy-done.10, f32[16,256]{0,1:T(8,128)S(1)} %copy-done.8, f32[256,1024,16]{1,2,0:T(8,128)} %fusion.48, ...), kind=kOutput, calls=%fused_computation.92 | convolution fusion | flops 868222208 | bytes 142639104 | tf_op jit(solution)/shard_map/jit(fft) | solution.py:18
  3043.1 35.7 copy.406
  3099.0 35.7 copy.392
  3134.7 315.5 %all-to-all-done.9 = f32[2,1,16,256,1024]{4,3,1,0,2:T(8,128)} async-done(((f32[2,1,16,256,1024]{4,3,1,0,2:T(8,128)}), f32[2,1,16,256,1024]{4,3,1,0,2:T(8,128)}, u32[]{:S(2)}, u32[]{:S(2)}) %all-to-all-start.9) | async-done | bytes 33554464 | tf_op jit(solution)/shard_map/all_to_all | solution.py:21
  3534.9 34.6 fusion.105
  3569.5 40.4 fusion.107
  3609.9 211.8 %all-to-all-done.7 = f32[2,1,16,256,1024]{4,3,1,0,2:T(8,128)} async-done(((f32[2,1,16,256,1024]{4,3,1,0,2:T(8,128)}), f32[2,1,16,256,1024]{4,3,1,0,2:T(8,128)}, u32[]{:S(2)}, u32[]{:S(2)}) %all-to-all-start.7) | async-done | bytes 33554464 | tf_op jit(solution)/shard_map/all_to_all | solution.py:21
  3885.6 35.0 fusion.115
  3934.6 40.5 fusion.117
  3975.2 34.8 fusion.109
  4009.9 74.4 %add_bitcast_fusion.4 = (f32[2,1024,128,16]{2,1,3,0:T(8,128)}, f32[1,2,1024,128,16]{3,2,4,1,0:T(8,128)}, f32[1,2,1024,128,16]{3,2,4,1,0:T(8,128)}, f32[2,1024,12...) fusion(f32[128,16]{0,1:T(8,128)S(1)} %copy-done.18, ...), kind=kOutput, calls=%fused_computation.245 | convolution fusion | flops 6518013952 | bytes 201342976 | tf_op jit(solution)/shard_map/jit(fft)/dot.27 | solution.py:22
  4117.1 35.8 subtract_bitcast_fusion.1
  4201.7 35.7 subtract_bitcast_fusion
  4253.8 36.1 add_bitcast_fusion.3
  4306.3 36.0 add_bitcast_fusion.1
  4392.7 40.4 fusion.91
  4446.0 34.5 fusion.93
  4480.5 47.9 add_bitcast_fusion
  4593.1 37.4 multiply_bitcast_fusion.1
  4702.4 49.4 copy.437
  4751.9 375.7 %all_to_all.116 = f32[2,1,2,2048,1024]{4,2,1,0,3:T(2,128)} all-to-all(f32[2,1,2,2048,1024]{4,2,1,0,3:T(2,128)} %copy.437), channel_id=1, replica_groups=mesh['dp'=2,'sp'=8] {'sp'}, dimensions={3} | all-to-all | bytes 67108864 | tf_op jit(solution)/shard_map/all_to_all | solution.py:31
  5297.0 98.4 %all_to_all.117 = f32[1,8,256,1024]{3,2,0,1:T(8,128)} all-to-all(f32[1,8,256,1024]{3,2,0,1:T(8,128)S(1)} %copy.439), channel_id=1, replica_groups=mesh['dp'=2,'sp'=8] {'sp'}, dimensions={1} | all-to-all | bytes 16777216 | tf_op jit(solution)/shard_map/all_to_all | solution.py:33
  (181 shorter events, 1678.4 us)
Async XLA Ops:
  0.0 5395.3 %copy-start = (bf16[1024,1024]{1,0:T(8,128)(2,1)S(1)}, bf16[1024,1024]{1,0:T(8,128)(2,1)}, u32[]{:S(2)}) copy-start(bf16[1024,1024]{1,0:T(8,128)(2,1)} %param.19) | copy-start | bytes 6291460
  0.0 6.2 copy-start.25
  0.0 121.7 %all-to-all-start.2 = ((f32[1,8,256,1024]{3,2,0,1:T(8,128)}), f32[1,8,256,1024]{3,2,0,1:T(8,128)}, u32[]{:S(2)}, u32[]{:S(2)}) async-start(f32[1,8,256,1024]{3,2,0,1:T(8,128)} %bitcast.988), calls=%async_computation.2 | async-start | bytes 16777216 | tf_op jit(solution)/shard_map/all_to_all | solution.py:17
  25.5 10.8 copy-start.23
  32.7 64.3 %collective-permute-start = (f32[1,2,3072]{2,1,0:T(2,128)S(1)}, f32[1,2,3072]{2,1,0:T(2,128)S(1)}, u32[]{:S(2)}, u32[]{:S(2)}) collective-permute-start(f32[1,2,3072]{2,1,0:T(2,128)S(1)} %slice.106), channel_id=1, source_target_pairs={{0,1},{1,2},{2,3},{3,4},{4,5},{5,6},{6,7},{8,9},{9,10},{10,11},{11... | collective-permute-start | bytes 73736 | tf_op jit(solution)/shard_map/ppermute | solution.py:45
  121.7 99.1 %all-to-all-start = ((f32[1,8,256,1024]{3,2,0,1:T(8,128)}), f32[1,8,256,1024]{3,2,0,1:T(8,128)}, u32[]{:S(2)}, u32[]{:S(2)}) async-start(f32[1,8,256,1024]{3,2,0,1:T(8,128)} %bitcast.987), calls=%async_computation | async-start | bytes 16777216 | tf_op jit(solution)/shard_map/all_to_all | solution.py:17
  127.7 156.1 %copy-start.7 = (f32[16,256]{0,1:T(8,128)}, f32[16,256]{0,1:T(8,128)S(1)}, u32[]{:S(2)}) copy-start(f32[16,256]{0,1:T(8,128)S(1)} %copy.340) | copy-start | bytes 49156
  127.8 156.0 %copy-start.9 = (f32[16,256]{0,1:T(8,128)}, f32[16,256]{0,1:T(8,128)S(1)}, u32[]{:S(2)}) copy-start(f32[16,256]{0,1:T(8,128)S(1)} %copy.341) | copy-start | bytes 49156
  147.8 3.4 copy-start.4
  229.1 3.3 copy-start.5
  391.8 371.5 %all-to-all-start.3 = ((f32[2,1,16,256,1024]{4,3,1,0,2:T(8,128)}), f32[2,1,16,256,1024]{4,3,1,0,2:T(8,128)}, u32[]{:S(2)}, u32[]{:S(2)}) async-start(f32[2,1,16,256,1024]{4,3,1,0,2:T(8,128)} %copy.356), calls=%async_computation.3 | async-start | bytes 67108864 | tf_op jit(solution)/shard_map/all_to_all | solution.py:21
  763.3 371.8 %all-to-all-start.1 = ((f32[2,1,16,256,1024]{4,3,1,0,2:T(8,128)}), f32[2,1,16,256,1024]{4,3,1,0,2:T(8,128)}, u32[]{:S(2)}, u32[]{:S(2)}) async-start(f32[2,1,16,256,1024]{4,3,1,0,2:T(8,128)} %copy.342), calls=%async_computation.1 | async-start | bytes 67108864 | tf_op jit(solution)/shard_map/all_to_all | solution.py:21
  1233.8 54.8 %slice-start = ((s8[16777216]{0:T(1024)(128)(4,1)}), s8[4194304]{0:T(1024)(128)(4,1)S(1)}, s32[]{:S(2)}) async-start(s8[16777216]{0:T(1024)(128)(4,1)} %bitcast.969), calls=%async_computation.12 | async-start | bytes 8388608
  1233.8 54.8 %slice-start.1 = ((s8[16777216]{0:T(1024)(128)(4,1)}), s8[4194304]{0:T(1024)(128)(4,1)S(1)}, s32[]{:S(2)}) async-start(s8[16777216]{0:T(1024)(128)(4,1)} %bitcast.969), calls=%async_computation.13 | async-start | bytes 8388608
  1247.7 40.8 slice-start.2
  1247.7 40.8 slice-start.3
  1288.6 34.6 copy-start.15
  1288.6 34.5 copy-start.17
  1706.2 40.4 copy-start.1
  1759.1 34.5 copy-start.11
  1759.1 34.5 copy-start.13
  1961.9 18.0 copy-start.19
  1961.9 18.0 copy-start.21
  2602.0 3.4 slice-start.8
  2610.3 104.0 %copy-start.24 = (f32[1024]{0:T(1024)S(1)}, f32[1024]{0:T(1024)}, u32[]{:S(2)}) copy-start(f32[1024]{0:T(1024)} %param.20) | copy-start | bytes 12292
  2708.3 99.6 %all-to-all-start.8 = ((f32[1,8,256,1024]{3,2,0,1:T(8,128)}), f32[1,8,256,1024]{3,2,0,1:T(8,128)}, u32[]{:S(2)}, u32[]{:S(2)}) async-start(f32[1,8,256,1024]{3,2,0,1:T(8,128)} %bitcast.989), calls=%async_computation.8 | async-start | bytes 16777216 | tf_op jit(solution)/shard_map/all_to_all | solution.py:17
  2807.9 99.9 %all-to-all-start.6 = ((f32[1,8,256,1024]{3,2,0,1:T(8,128)}), f32[1,8,256,1024]{3,2,0,1:T(8,128)}, u32[]{:S(2)}, u32[]{:S(2)}) async-start(f32[1,8,256,1024]{3,2,0,1:T(8,128)} %bitcast.985), calls=%async_computation.6 | async-start | bytes 16777216 | tf_op jit(solution)/shard_map/all_to_all | solution.py:17
  2822.5 3.3 copy-start.3
  2916.1 3.2 copy-start.6
  2943.9 26.7 copy-start.8
  2943.9 26.7 copy-start.10
  3078.8 371.4 %all-to-all-start.9 = ((f32[2,1,16,256,1024]{4,3,1,0,2:T(8,128)}), f32[2,1,16,256,1024]{4,3,1,0,2:T(8,128)}, u32[]{:S(2)}, u32[]{:S(2)}) async-start(f32[2,1,16,256,1024]{4,3,1,0,2:T(8,128)} %copy.406), calls=%async_computation.9 | async-start | bytes 67108864 | tf_op jit(solution)/shard_map/all_to_all | solution.py:21
  3450.2 371.6 %all-to-all-start.7 = ((f32[2,1,16,256,1024]{4,3,1,0,2:T(8,128)}), f32[2,1,16,256,1024]{4,3,1,0,2:T(8,128)}, u32[]{:S(2)}, u32[]{:S(2)}) async-start(f32[2,1,16,256,1024]{4,3,1,0,2:T(8,128)} %copy.392), calls=%async_computation.7 | async-start | bytes 67108864 | tf_op jit(solution)/shard_map/all_to_all | solution.py:21
  3920.6 54.5 %slice-start.4 = ((s8[16777216]{0:T(1024)(128)(4,1)}), s8[4194304]{0:T(1024)(128)(4,1)S(1)}, s32[]{:S(2)}) async-start(s8[16777216]{0:T(1024)(128)(4,1)} %bitcast.971), calls=%async_computation.16 | async-start | bytes 8388608
  3920.6 54.5 %slice-start.5 = ((s8[16777216]{0:T(1024)(128)(4,1)}), s8[4194304]{0:T(1024)(128)(4,1)S(1)}, s32[]{:S(2)}) async-start(s8[16777216]{0:T(1024)(128)(4,1)} %bitcast.971), calls=%async_computation.17 | async-start | bytes 8388608
  3934.6 40.5 slice-start.6
  3934.6 40.5 slice-start.7
  3975.2 34.8 copy-start.16
  3975.2 34.8 copy-start.18
  4392.7 40.4 copy-start.2
  4446.0 34.5 copy-start.12
  4446.0 34.5 copy-start.14
  4648.6 18.0 copy-start.20
  4648.6 18.0 copy-start.22
  5288.7 3.4 slice-start.9
  5292.1 103.2 %copy-start.26 = (f32[1024]{0:T(1024)S(1)}, f32[1024]{0:T(1024)}, u32[]{:S(2)}) copy-start(f32[1024]{0:T(1024)} %param.21) | copy-start | bytes 12292
where the time goes:
time: 5430 us; the launch traced here: 5410 us
  matrix products  1850 us (34%)
  waiting for transfers between devices  1300 us (24%)
  blocking collectives  948 us (17%)
  local copies, waits for them, and re-layouts  946 us (17%)
  other arithmetic  306 us (6%)
  starting transfers between devices  61.3 us (1%)
    all_to_all x4, waiting for transfers between devices, to_spectrum(): lax.all_to_all(jnp.stack([coarse.real, coarse.imag]), 'sp', 2, 3, tiled=T...  1050 us
    another operation x24, matrix products, to_spectrum(): return jnp.fft.fft(lax.complex(pair_parts[0], pair_parts[1]), axis=2)  937 us
    all_to_all x2, blocking collectives, from_spectrum(): lax.all_to_all(jnp.stack([fine_part.real, fine_part.imag]), 'sp', 3, 2, t...  751 us
    another operation x12, matrix products, from_spectrum(): fine_part = jnp.fft.ifft(spectrum_in, axis=2)  450 us
    another operation x9, matrix products, to_spectrum(): coarse = jnp.fft.fft(by_block, n=2 * n_dev, axis=1)  285 us
    all_to_all x2, blocking collectives, from_spectrum(): restored = lax.all_to_all(coarse, 'sp', 1, 1, tiled=True)  196 us
    all_to_all x4, waiting for transfers between devices, to_spectrum(): lax.all_to_all(signal.reshape(groups, n_dev, piece_len, channels), 'sp',...  182 us
    slice x12, local copies, waits for them, and re-layouts, to_spectrum(): return jnp.fft.fft(lax.complex(pair_parts[0], pair_parts[1]), axis=2)  162 us
  transfers between devices with their start and end apart: 9, of which 8 were waited for; matrix products, arithmetic and copies ran while one was open for 10% of the time, Pallas kernels for 0%

commit v1 on v0

v1 whole, which is shorter than its diff:
```python
import functools
import jax
import jax.numpy as jnp
import numpy as np
from jax import lax
from jax.experimental import pallas as pl
from jax.experimental.pallas import tpu as pltpu
from jax.sharding import PartitionSpec as P

LANES = 128
F32 = jnp.float32
BF16 = jnp.bfloat16


def split_table(table, n_parts=3):
    parts, rest = [], np.asarray(table, np.float64)
    for _ in range(n_parts):
        part = rest.astype(jnp.bfloat16)
        parts.append(part)
        rest = rest - part.astype(np.float64)
    return parts


def transform_tables(seq_len):
    n_high = seq_len // LANES
    quarter = np.arange(n_high)[:, None] + 0.25
    high = 2.0 * np.pi * quarter * np.arange(n_high)[None, :] / n_high
    twist = 2.0 * np.pi * quarter * np.arange(LANES)[None, :] / seq_len
    low = 2.0 * np.pi * np.outer(np.arange(LANES), np.arange(LANES)) / LANES
    first = np.concatenate([np.cos(high), -np.sin(high)], axis=0)
    last = np.concatenate([np.cos(high.T), -np.sin(high.T)], axis=1)
    er, ei = np.cos(low), -np.sin(low)
    fwd = np.block([[er, ei], [-ei, er]])
    inv = np.block([[er, -ei], [ei, er]])
    a, b, c = split_table(first)
    first_wide = np.concatenate([a, a, a, b, b, c], axis=1)
    first_thin = np.concatenate([a, b, c], axis=1)
    fwd_parts = np.concatenate(split_table(fwd), axis=0)
    inv_parts = np.concatenate(split_table(inv), axis=0)
    last_parts = np.concatenate(split_table(last), axis=0)
    twist_tab = np.stack([np.cos(twist), -np.sin(twist)]).astype(np.float32)
    return first_wide, first_thin, fwd_parts, inv_parts, last_parts, twist_tab


def split3(x):
    hi = x.astype(BF16)
    rest = x - hi.astype(F32)
    mid = rest.astype(BF16)
    low = (rest - mid.astype(F32)).astype(BF16)
    return hi, mid, low


def dot32(a, b):
    return jnp.dot(a, b, preferred_element_type=F32)


def turn_filters_body(one_ref, two_ref, out_ref):
    n_rows = one_ref.shape[0] // LANES
    for which, ref in enumerate((one_ref, two_ref)):

        @pl.loop(0, n_rows)
        def _(r):
            block = ref[pl.ds(pl.multiple_of(r * LANES, LANES), LANES), :]
            out_ref[0, which, pl.ds(r, LANES, stride=n_rows), :] = block.T


def turn_filters(filt_one, filt_two, n_dev):
    rows = filt_one.shape[0]
    n_rows = rows // LANES
    spec = pl.BlockSpec((rows, LANES), lambda d: (0, d))
    return pl.pallas_call(
        turn_filters_body,
        grid=(n_dev,),
        in_specs=[spec, spec],
        out_specs=pl.BlockSpec((1, 2, LANES * n_rows, LANES), lambda d: (d, 0, 0, 0)),
        out_shape=jax.ShapeDtypeStruct((n_dev, 2, LANES * n_rows, LANES), F32),
        cost_estimate=pl.CostEstimate(flops=10**9, bytes_accessed=4 * 4 * rows * LANES * n_dev, transcendentals=0),
        compiler_params=pltpu.CompilerParams(dimension_semantics=("arbitrary",)),
        name="turn_filters",
    )(filt_one, filt_two)


def project_body(n_chunks, flag_ref, u_ref, halo_ref, *refs):
    w_refs, b_refs, tap_refs = refs[:3], refs[3:6], refs[6:9]
    sent_ref, gate_ref, p_ref = refs[9:]
    rows = u_ref.shape[0]
    n_rows = rows // LANES
    width = w_refs[0].shape[1]
    per_chunk = LANES // n_chunks
    for which in range(3):
        w = w_refs[which][...]
        bias = b_refs[which][...]
        halo = (dot32(halo_ref[...].astype(BF16), w) + bias).astype(BF16).astype(F32)
        p_ref[0:8, :] = jnp.where(flag_ref[0] > 0, halo, 0.0)
        step = 2 * LANES

        @pl.loop(0, rows // step)
        def _(i):
            start = pl.multiple_of(i * step, step)
            proj = dot32(u_ref[pl.ds(start, step), :], w) + bias
            p_ref[pl.ds(start + 8, step), :] = proj.astype(BF16).astype(F32)

        c0, c1, c2 = (tap_refs[which][t : t + 1, :] for t in range(3))

        @pl.loop(0, n_rows)
        def _(r):
            start = pl.multiple_of(r * LANES, LANES)
            window = p_ref[pl.ds(start, LANES + 8), :]
            mixed = c0 * window[8:] + c1 * window[7:-1] + c2 * window[6:-2]
            mixed = mixed.astype(BF16)
            if which == 1:
                gate_ref[pl.ds(start, LANES), :] = mixed
            else:
                slot = 1 if which == 0 else 0
                for d in range(width // LANES):
                    turned = mixed[:, d * LANES : (d + 1) * LANES].astype(F32).T
                    for k in range(n_chunks):
                        sent_ref[k, d, slot, pl.ds(r, per_chunk, stride=n_rows), :] = turned[k * per_chunk : (k + 1) * per_chunk]


def project(has_prev, u, halo, w_in, b_in, taps, n_dev, n_chunks):
    rows, depth = u.shape
    model = w_in.shape[1] // 3
    width = 2 * LANES
    steps = model // width
    n_rows = rows // LANES
    per_chunk = LANES // n_chunks
    chunk_rows = per_chunk * n_rows
    w_specs = [pl.BlockSpec((depth, width), functools.partial(lambda off, j: (0, off + j), t * steps)) for t in range(3)]
    b_specs = [pl.BlockSpec((1, width), functools.partial(lambda off, j: (0, off + j), t * steps)) for t in range(3)]
    t_specs = [pl.BlockSpec((3, width), functools.partial(lambda off, j: (0, off + j), t * steps)) for t in range(3)]
    return pl.pallas_call(
        functools.partial(project_body, n_chunks),
        grid=(steps,),
        in_specs=[
            pl.BlockSpec(memory_space=pltpu.SMEM),
            pl.BlockSpec((rows, depth), lambda j: (0, 0)),
            pl.BlockSpec((8, depth), lambda j: (0, 0)),
            *w_specs,
            *b_specs,
            *t_specs,
        ],
        out_specs=[
            pl.BlockSpec((n_chunks, 2, 2, chunk_rows, LANES), lambda j: (0, j, 0, 0, 0)),
            pl.BlockSpec((rows, width), lambda j: (0, j)),
        ],
        out_shape=[
            jax.ShapeDtypeStruct((n_chunks, n_dev, 2, chunk_rows, LANES), F32),
            jax.ShapeDtypeStruct((rows, model), BF16),
        ],
        scratch_shapes=[pltpu.VMEM((rows + 8, width), F32)],
        cost_estimate=pl.CostEstimate(flops=2 * rows * depth * 3 * model, bytes_accessed=30 * 2**20, transcendentals=0),
        compiler_params=pltpu.CompilerParams(dimension_semantics=("arbitrary",), vmem_limit_bytes=60 * 2**20),
        name="project",
    )(has_prev, u, halo, w_in, w_in, w_in, b_in, b_in, b_in, taps, taps, taps)


def spectrum_tools(group, n_high, tables, parts_ref):
    wide_ref, thin_ref, fwd_ref, inv_ref, last_ref, twist_ref = tables
    wide = 2 * LANES
    scale = 1.0 / (n_high * LANES)

    def complex_dot(tab_ref):
        return (
            dot32(parts_ref[:, 2 * wide :], tab_ref[:wide])
            + dot32(parts_ref[:, wide : 2 * wide], tab_ref[:wide])
            + dot32(parts_ref[:, :wide], tab_ref[wide : 2 * wide])
            + dot32(parts_ref[:, wide : 2 * wide], tab_ref[wide : 2 * wide])
            + dot32(parts_ref[:, :wide], tab_ref[2 * wide :])
            + dot32(parts_ref[:, :wide], tab_ref[:wide])
        )

    def store_parts(g, real, imag):
        for t, (re, im) in enumerate(zip(split3(real), split3(imag))):
            parts_ref[g * n_high : (g + 1) * n_high, 2 * t * LANES : (2 * t + 1) * LANES] = re
            parts_ref[g * n_high : (g + 1) * n_high, (2 * t + 1) * LANES : (2 * t + 2) * LANES] = im

    def spectrum(signals, exact):
        tr, ti = twist_ref[0], twist_ref[1]
        for g in range(0, group, 2):
            pair = jnp.concatenate([signals[g], signals[g + 1]], axis=1)
            if exact:
                short = pair.astype(BF16)
                coarse = dot32(thin_ref[...], jnp.concatenate([short, short, short], axis=0))
            else:
                hi, mid, low = split3(pair)
                coarse = dot32(wide_ref[...], jnp.concatenate([hi, mid, low, hi, mid, hi], axis=0))
            for j in range(2):
                re = coarse[:n_high, j * LANES : (j + 1) * LANES]
                im = coarse[n_high:, j * LANES : (j + 1) * LANES]
                store_parts(g + j, re * tr - im * ti, re * ti + im * tr)
        return complex_dot(fwd_ref)

    def signal(spec_a, spec_b):
        tr, ti = twist_ref[0], twist_ref[1]
        for g in range(group):
            rows = slice(g * n_high, (g + 1) * n_high)
            ar, ai = spec_a[rows, :LANES], spec_a[rows, LANES:]
            br, bi = spec_b[rows, :LANES], spec_b[rows, LANES:]
            store_parts(g, ar * br - ai * bi, ar * bi + ai * br)
        fine = complex_dot(inv_ref)
        results = []
        for g in range(0, group, 2):
            halves = []
            for j in range(2):
                rows = slice((g + j) * n_high, (g + j + 1) * n_high)
                re, im = fine[rows, :LANES] * scale, fine[rows, LANES:] * scale
                halves.append(jnp.concatenate([re * tr + im * ti, im * tr - re * ti], axis=0))
            hi, mid, low = split3(jnp.concatenate(halves, axis=1))
            d_hi = dot32(last_ref[...], hi)
            d_mid = dot32(last_ref[: 2 * n_high], mid)
            d_low = dot32(last_ref[:n_high], low)
            small = d_hi[2 * n_high :] + d_mid[n_high:] + d_low
            total = d_hi[:n_high] + ((d_hi[n_high : 2 * n_high] + d_mid[:n_high]) + small)
            results += [total[:, :LANES], total[:, LANES:]]
        return results

    return spectrum, signal


def exchange_body(n_dev, group, ahead, skip_ref, filt_ref, sent_ref, wide_ref, thin_ref, fwd_ref, inv_ref, last_ref, twist_ref, back_ref, got_ref, h_ref, done_ref, parts_ref, spec_one_ref, spec_two_ref, sent_sem, got_sem, h_sem, back_sem, done_sem):
    n_chunks, _, _, chunk_rows, _ = sent_ref.shape
    n_high = twist_ref.shape[1]
    per_src = n_high // n_dev
    n_chan = chunk_rows // per_src
    me = lax.axis_index("sp")
    spectrum, signal = spectrum_tools(group, n_high, (wide_ref, thin_ref, fwd_ref, inv_ref, last_ref, twist_ref), parts_ref)

    barrier = pltpu.get_barrier_semaphore()
    for off in range(1, n_dev):
        pl.semaphore_signal(barrier, inc=1, device_id={"sp": lax.rem(me + off, n_dev)}, device_id_type=pl.DeviceIdType.MESH)
    pl.semaphore_wait(barrier, n_dev - 1)

    def sending(k, off):
        dest = lax.rem(me + off, n_dev)
        return pltpu.make_async_remote_copy(
            src_ref=sent_ref.at[k, dest],
            dst_ref=got_ref.at[k, me],
            send_sem=sent_sem.at[k, off],
            recv_sem=got_sem.at[k, off],
            device_id={"sp": dest},
            device_id_type=pl.DeviceIdType.MESH,
        )

    def keeping(k):
        return pltpu.make_async_copy(sent_ref.at[k, me], got_ref.at[k, me], got_sem.at[k, 0])

    def fetching(k, slot):
        return pltpu.make_async_copy(
            filt_ref.at[:, :, pl.ds(pl.multiple_of(k * chunk_rows, chunk_rows), chunk_rows), :], h_ref.at[slot], h_sem.at[slot]
        )

    block = per_src * n_chan

    def part_of(slot, dest):
        return done_ref.at[slot, pl.ds(pl.multiple_of(dest * block, block), block), :]

    def returning(k, slot, off):
        dest = lax.rem(me + off, n_dev)
        return pltpu.make_async_remote_copy(
            src_ref=part_of(slot, dest),
            dst_ref=back_ref.at[k, me],
            send_sem=done_sem.at[slot, off],
            recv_sem=back_sem.at[k, off],
            device_id={"sp": dest},
            device_id_type=pl.DeviceIdType.MESH,
        )

    def storing(k, slot):
        return pltpu.make_async_copy(part_of(slot, me), back_ref.at[k, me], done_sem.at[slot, 0])

    def launch(k):
        keeping(k).start()
        for off in range(1, n_dev):
            sending(k, off).start()

    for k in range(ahead):
        launch(k)
    fetching(0, 0).start()

    @pl.loop(0, n_chunks)
    def _(k):
        slot = lax.rem(k, 2)

        @pl.when(k + ahead < n_chunks)
        def _():
            launch(k + ahead)

        @pl.when(k + 1 < n_chunks)
        def _():
            fetching(k + 1, 1 - slot).start()

        fetching(k, slot).wait()
        keeping(k).wait()
        for off in range(1, n_dev):
            sending(k, off).wait_recv()

        @pl.when(k >= 2)
        def _():
            storing(k - 2, slot).wait()
            for off in range(1, n_dev):
                returning(k - 2, slot, off).wait_send()

        @pl.loop(0, n_chan // group)
        def _(i):
            first = i * group

            def load_h(which, g):
                start = pl.multiple_of((first + g) * per_src, per_src)
                return h_ref[slot, :, which, pl.ds(start, per_src), :].reshape(n_high, LANES)

            def load_x(which, g):
                start = pl.multiple_of((first + g) * per_src, per_src)
                return got_ref[k, :, which, pl.ds(start, per_src), :].reshape(n_high, LANES)

            chan = k * n_chan + first
            spec_one_ref[...] = spectrum([load_h(0, g) for g in range(group)], False)
            spec_two_ref[...] = spectrum([load_h(1, g) for g in range(group)], False)
            values = [load_x(0, g) for g in range(group)]
            conv = signal(spectrum(values, True), spec_one_ref)
            gated = [load_x(1, g) * (conv[g] + skip_ref[0, chan + g] * values[g]) for g in range(group)]
            conv = signal(spectrum(gated, False), spec_two_ref)
            for g in range(group):
                done_ref[slot, pl.ds(first + g, n_high, stride=n_chan), :] = conv[g] + skip_ref[1, chan + g] * gated[g]

        storing(k, slot).start()
        for off in range(1, n_dev):
            returning(k, slot, off).start()

    for k in range(max(0, n_chunks - 2), n_chunks):
        storing(k, k % 2).wait()
        for off in range(1, n_dev):
            returning(k, k % 2, off).wait_send()

    @pl.loop(0, n_chunks)
    def _(k):
        for off in range(1, n_dev):
            sending(k, off).wait_send()
            returning(k, 0, off).wait_recv()


def exchange(skips, filters, sent, tables, n_dev, group=4, ahead=3):
    n_chunks, _, _, chunk_rows, _ = sent.shape
    n_high = tables[-1].shape[1]
    n_chan = chunk_rows // (n_high // n_dev)
    any_spec = pl.BlockSpec(memory_space=pl.ANY)
    vmem_spec = pl.BlockSpec(memory_space=pltpu.VMEM)
    return pl.pallas_call(
        functools.partial(exchange_body, n_dev, group, ahead),
        in_specs=[pl.BlockSpec(memory_space=pltpu.SMEM), any_spec, any_spec] + [vmem_spec] * len(tables),
        out_specs=any_spec,
        out_shape=jax.ShapeDtypeStruct((n_chunks, n_dev, chunk_rows, LANES), F32),
        scratch_shapes=[
            pltpu.VMEM((n_chunks, n_dev, 2, chunk_rows, LANES), F32),
            pltpu.VMEM((2, n_dev, 2, chunk_rows, LANES), F32),
            pltpu.VMEM((2, n_high * n_chan, LANES), F32),
            pltpu.VMEM((group * n_high, 6 * LANES), BF16),
            pltpu.VMEM((group * n_high, 2 * LANES), F32),
            pltpu.VMEM((group * n_high, 2 * LANES), F32),
            pltpu.SemaphoreType.DMA((n_chunks, n_dev)),
            pltpu.SemaphoreType.DMA((n_chunks, n_dev)),
            pltpu.SemaphoreType.DMA((2,)),
            pltpu.SemaphoreType.DMA((n_chunks, n_dev)),
            pltpu.SemaphoreType.DMA((2, n_dev)),
        ],
        cost_estimate=pl.CostEstimate(flops=10**11, bytes_accessed=40 * 2**20, transcendentals=0),
        compiler_params=pltpu.CompilerParams(collective_id=0, has_side_effects=True, vmem_limit_bytes=60 * 2**20),
        name="exchange",
    )(skips, filters, sent, *tables)


def finish_body(gate_ref, u_ref, w_ref, back_ref, out_ref, y_ref):
    n_chunks, n_src, n_rows, _, _ = back_ref.shape
    for r in range(n_rows):
        for s in range(n_src):
            full = jnp.concatenate([back_ref[k, s, r] for k in range(n_chunks)], axis=0)
            rows, cols = slice(r * LANES, (r + 1) * LANES), slice(s * LANES, (s + 1) * LANES)
            y_ref[rows, cols] = (gate_ref[rows, cols].astype(F32) * full.T).astype(BF16)
    out_ref[...] = (u_ref[...].astype(F32) + dot32(y_ref[...], w_ref[...])).astype(BF16)


def finish(gate, u, w_out, back, n_rows=2):
    rows, model = u.shape
    n_chunks, n_src, _, per_chunk, _ = back.shape
    tile = n_rows * LANES
    return pl.pallas_call(
        finish_body,
        grid=(rows // tile,),
        in_specs=[
            pl.BlockSpec((tile, model), lambda i: (i, 0)),
            pl.BlockSpec((tile, model), lambda i: (i, 0)),
            pl.BlockSpec(w_out.shape, lambda i: (0, 0)),
            pl.BlockSpec((n_chunks, n_src, n_rows, per_chunk, LANES), lambda i: (0, 0, i, 0, 0)),
        ],
        out_specs=pl.BlockSpec((tile, model), lambda i: (i, 0)),
        out_shape=jax.ShapeDtypeStruct((rows, model), BF16),
        scratch_shapes=[pltpu.VMEM((tile, model), BF16)],
        cost_estimate=pl.CostEstimate(flops=2 * rows * model * model, bytes_accessed=20 * 2**20, transcendentals=0),
        compiler_params=pltpu.CompilerParams(dimension_semantics=("arbitrary",), vmem_limit_bytes=48 * 2**20),
        name="finish",
    )(gate, u, w_out, back)


def solution(mesh):
    n_dev = mesh.shape["sp"]
    n_chunks = 8
    halo_perm = list(zip(range(n_dev - 1), range(1, n_dev)))

    def local_step(u_in, w_in, b_in, conv_taps, w_out, skip_one, skip_two, filt_one, filt_two):
        rank = lax.axis_index("sp")
        u = u_in[0]
        rows = u.shape[0]
        tables = [jnp.asarray(t) for t in transform_tables(rows * n_dev)]

        def swap(x):
            return lax.all_to_all(x, "sp", 0, 0, tiled=True)

        halo = lax.ppermute(u[-8:].astype(F32), "sp", halo_perm)
        has_prev = (rank > 0).astype(jnp.int32)[None]
        filters = swap(turn_filters(filt_one, filt_two, n_dev))
        sent, gate = project(has_prev, u, halo, w_in, b_in[None], conv_taps, n_dev, n_chunks)
        skips = lax.dynamic_slice_in_dim(jnp.stack([skip_one, skip_two]), rank * LANES, LANES, axis=1)
        back = exchange(skips, filters, sent, tables, n_dev)
        back = back.reshape(n_chunks, n_dev, rows // LANES, LANES // n_chunks, LANES)
        return finish(gate, u, w_out, back)[None]

    seq_spec = P("dp", "sp", None)
    filt_spec = P("sp", None)
    return jax.shard_map(
        local_step,
        mesh=mesh,
        in_specs=(seq_spec, P(), P(), P(), P(), P(), P(), filt_spec, filt_spec),
        out_specs=seq_spec,
        check_vma=False,
    )
```

time: 5430 us -> 598 us (0.11)
  matrix products: 1850 us -> 0 us
  waiting for transfers between devices: 1300 us -> 175 us
  blocking collectives: 948 us -> 0 us
  local copies, waits for them, and re-layouts: 946 us -> 0.63 us
  Pallas kernels: 0 us -> 410 us
  other arithmetic: 306 us -> 1.37 us
    another operation x51 -> x0, matrix products: 1820 us -> none  [the longest x24 937 us: to_spectrum(): return jnp.fft.fft(lax.complex(pair_parts[0], pair_parts[1]), axis=2)]
    all_to_all x8 -> x1, waiting for transfers between devices: 1230 us -> 0.01 us  [swap(): return lax.all_to_all(x, 'sp', 0, 0, tiled=True)]
    all_to_all x4 -> x0, blocking collectives: 948 us -> none  [the longest x2 751 us: from_spectrum(): lax.all_to_all(jnp.stack([fine_part.real, fine_part.imag]), 'sp', 3, 2, t...]
    another operation x18 -> x0, local copies, waits for them, and re-layouts: 445 us -> none  [the longest x4 143 us: to_spectrum(): jnp.stack([coarse.real, coarse.imag])]
    pallas_call x0 -> x4, Pallas kernels: none -> 410 us  [the longest x1 309 us: exchange(): pl.pallas_call(functools.partial(exchange_body, n_dev, group, ahead), in_...]
    slice x23 -> x0, local copies, waits for them, and re-layouts: 234 us -> none  [the longest x12 162 us: to_spectrum(): return jnp.fft.fft(lax.complex(pair_parts[0], pair_parts[1]), axis=2)]
    another operation x16 -> x1, other arithmetic: 200 us -> 0.65 us  [local_step(): jnp.stack([skip_one, skip_two])]
    all_to_all x10 -> x0, local copies, waits for them, and re-layouts: 173 us -> none  [the longest x4 93.4 us: to_spectrum(): lax.all_to_all(jnp.stack([coarse.real, coarse.imag]), 'sp', 2, 3, tiled=T...]
  transfers between devices with their start and end apart: 9 -> 2, of which waited for: 8 -> 1; matrix products, arithmetic and copies ran while one was open for 10% -> 0% of each run, Pallas kernels for 0% -> 10%
where the time goes in v1:
time: 598 us
  Pallas kernels  410 us (69%)
  waiting for transfers between devices  175 us (29%)
  starting transfers between devices  10.5 us (2%)
    pallas_call x1, Pallas kernels, exchange(): pl.pallas_call(functools.partial(exchange_body, n_dev, group, ahead), in_...  309 us
    ppermute x1, waiting for transfers between devices, local_step(): halo = lax.ppermute(u[-8:].astype(F32), 'sp', halo_perm)  175 us
    pallas_call x1, Pallas kernels, project(): pl.pallas_call(functools.partial(project_body, n_chunks), grid=(steps,),...  59.4 us
    pallas_call x1, Pallas kernels, turn_filters(): pl.pallas_call(turn_filters_body, grid=(n_dev,), in_specs=[spec, spec], o...  28.9 us
    pallas_call x1, Pallas kernels, finish(): pl.pallas_call(finish_body, grid=(rows // tile,), in_specs=[pl.BlockSpec(...  12.3 us
  transfers between devices with their start and end apart: 2, of which 1 were waited for; matrix products, arithmetic and copies ran while one was open for 0% of the time, Pallas kernels for 10%

profile of v1, /device:TPU:113, one launch (start us, length us, event | category | flops | bytes accessed | tf_op | source)
XLA Modules:
  0.0 597.8 jit_solution(17133003505688154669)
XLA Ops:
  0.0 28.9 %turn_filters.1 = f32[8,2,2048,128]{3,2,1,0:T(8,128)} custom-call(f32[2048,1024]{1,0:T(8,128)} %one_ref.1, f32[2048,1024]{1,0:T(8,128)} %two_ref.1), custom_call_target="tpu_custom_call" | custom-call | flops 1000000000 | bytes 33554432 | tf_op jit(solution)/shard_map/turn_filters/pallas_call | solution.py:71
  28.9 0.0 copy-start.1
  28.9 0.0 copy-start.2
  28.9 6.5 %all-to-all-start = ((f32[8,2,2048,128]{3,2,1,0:T(8,128)}), f32[8,2,2048,128]{3,2,1,0:T(8,128)}, u32[]{:S(2)}, u32[]{:S(2)}) async-start(f32[8,2,2048,128]{3,2,1,0:T(8,128)} %turn_filters.1), calls=%async_computation | async-start | bytes 33554432 | tf_op jit(solution)/shard_map/all_to_all | solution.py:416
  35.4 0.7 bitcast_convert_fusion
  36.1 4.0 collective-permute-start
  40.1 0.0 copy-done.1
  40.1 0.0 copy-done.2
  40.1 0.7 fusion.skip_ref
  40.8 175.3 %collective-permute-done.halo_ref = f32[8,1024]{1,0:T(8,128)S(1)} collective-permute-done((f32[8,1024]{1,0:T(8,128)S(1)}, f32[8,1024]{1,0:T(8,128)S(1)}, u32[]{:S(2)}, u32[]{:S(2)}) %collective-permute-start) | collective-permute-done | bytes 32800 | tf_op jit(solution)/shard_map/ppermute | solution.py:418
  216.1 0.0 copy-start.3
  216.1 0.6 copy-done.3
  216.8 59.4 %project.1 = (f32[8,8,2,256,128]{4,3,2,1,0:T(8,128)}, bf16[2048,1024]{1,0:T(8,128)(2,1)}) custom-call(s32[1]{0:T(128)} %bitcast.flag_ref, bf16[2048,1024]{1,0:T(8,128)(2,1)} %bitcast.11, f32[8,1024]{1,0:T(8,128)} %copy-done.3, bf16[1024,3072]{1,0:T(8,128)(2,1)} %refs_2_.1, bf16[1024,3072]{1,0:T(8,128)(2,1)} %refs_2_.1, bf16[1024,3072]{1,0:T(8,128)(2,1)} %refs_2_.1, ...), custom_call_target="tpu_custom_call" | custom-call | flops 12884901888 | bytes 31457280 | tf_op jit(solution)/shard_map/project/pallas_call | solution.py:132
  276.1 0.0 all-to-all-done.filt_ref
  276.1 0.0 copy-start
  276.1 309.3 %exchange.1 = f32[8,8,256,128]{3,2,1,0:T(8,128)} custom-call(f32[2,128]{1,0:T(2,128)} %fusion.skip_ref, f32[8,2,2048,128]{3,2,1,0:T(8,128)} %all-to-all-done.filt_ref, f32[8,8,2,256,128]{4,3,2,1,0:T(8,128)} %get-tuple-element.8.sent_ref, bf16[256,768]{1,0:T(8,128)(2,1)} %constant.22.clone.wide_ref, bf16[256,384]{1,0:T(8,128)(2,1)} %constant.23.clone.thin_ref, ...), custom_call_target="tpu_custom_call" | custom-call | flops 99999997952 | bytes 41943040 | tf_op jit(solution)/shard_map/exchange/pallas_call | solution.py:348
  585.4 0.0 copy-done
  585.5 12.3 %finish.1 = bf16[2048,1024]{1,0:T(8,128)(2,1)} custom-call(bf16[2048,1024]{1,0:T(8,128)(2,1)} %get-tuple-element.7.gate_ref, bf16[2048,1024]{1,0:T(8,128)(2,1)} %bitcast.12, bf16[1024,1024]{1,0:T(8,128)(2,1)S(1)} %copy-done, f32[8,8,16,16,128]{4,3,2,1,0:T(8,128)} %bitcast.10), custom_call_target="tpu_custom_call" | custom-call | flops 4294967296 | bytes 20971520 | tf_op jit(solution)/shard_map/finish/pallas_call | solution.py:386
Async XLA Ops:
  28.9 11.3 %copy-start.1 = (f32[1024]{0:T(1024)S(1)}, f32[1024]{0:T(1024)}, u32[]{:S(2)}) copy-start(f32[1024]{0:T(1024)} %param.20) | copy-start | bytes 12292
  28.9 11.3 %copy-start.2 = (f32[1024]{0:T(1024)S(1)}, f32[1024]{0:T(1024)}, u32[]{:S(2)}) copy-start(f32[1024]{0:T(1024)} %param.21) | copy-start | bytes 12292
  28.9 247.2 %all-to-all-start = ((f32[8,2,2048,128]{3,2,1,0:T(8,128)}), f32[8,2,2048,128]{3,2,1,0:T(8,128)}, u32[]{:S(2)}, u32[]{:S(2)}) async-start(f32[8,2,2048,128]{3,2,1,0:T(8,128)} %turn_filters.1), calls=%async_computation | async-start | bytes 33554432 | tf_op jit(solution)/shard_map/all_to_all | solution.py:416
  36.1 180.1 %collective-permute-start = (f32[8,1024]{1,0:T(8,128)S(1)}, f32[8,1024]{1,0:T(8,128)S(1)}, u32[]{:S(2)}, u32[]{:S(2)}) collective-permute-start(f32[8,1024]{1,0:T(8,128)S(1)} %bitcast_convert_fusion), channel_id=1, source_target_pairs={{0,1},{1,2},{2,3},{3,4},{4,5},{5,6},{6,7},{8,9},{9,10},{10,11},{11... | collective-permute-start | bytes 98312 | tf_op jit(solution)/shard_map/ppermute | solution.py:418
  216.1 0.6 copy-start.3
  276.1 309.3 %copy-start = (bf16[1024,1024]{1,0:T(8,128)(2,1)S(1)}, bf16[1024,1024]{1,0:T(8,128)(2,1)}, u32[]{:S(2)}) copy-start(bf16[1024,1024]{1,0:T(8,128)(2,1)} %w_ref.1) | copy-start | bytes 6291460

commit v2 on v1

--- a/solution.py
+++ b/solution.py
@@ -54,30 +54,59 @@
     return jnp.dot(a, b, preferred_element_type=F32)
 
 
-def turn_filters_body(one_ref, two_ref, out_ref):
+def turn_share_body(n_chunks, units, place_ref, one_ref, two_ref, out_ref, *scratch):
     n_rows = one_ref.shape[0] // LANES
-    for which, ref in enumerate((one_ref, two_ref)):
-
+    n_chan = LANES // n_chunks
+
+    def turn(ref, into_ref, base):
         @pl.loop(0, n_rows)
         def _(r):
-            block = ref[pl.ds(pl.multiple_of(r * LANES, LANES), LANES), :]
-            out_ref[0, which, pl.ds(r, LANES, stride=n_rows), :] = block.T
-
-
-def turn_filters(filt_one, filt_two, n_dev):
+            block = ref[pl.ds(pl.multiple_of(r * LANES, LANES), LANES), :].T
+            for k in range(n_chunks):
+                into_ref[k, pl.ds(base + r, n_chan, stride=n_rows), :] = block[k * n_chan : (k + 1) * n_chan]
+
+    if units == 2 * n_chan:
+        turn(one_ref, out_ref.at[0], 0)
+        turn(two_ref, out_ref.at[0], n_chan * n_rows)
+    else:
+        into_ref = out_ref.at[0] if units == n_chan else scratch[0]
+        for which, ref in enumerate((one_ref, two_ref)):
+
+            @pl.when(place_ref[0] == which)
+            def _():
+                turn(ref, into_ref, 0)
+
+        if units < n_chan:
+            start = pl.multiple_of(place_ref[1] * n_rows, n_rows)
+            out_ref[0] = scratch[0][:, pl.ds(start, units * n_rows), :]
+
+
+def turn_share(place, filt_one, filt_two, n_dev, n_chunks, units):
     rows = filt_one.shape[0]
     n_rows = rows // LANES
-    spec = pl.BlockSpec((rows, LANES), lambda d: (0, d))
+    n_chan = LANES // n_chunks
+    both = units == 2 * n_chan
+
+    def pick(which):
+        def index(d, place_ref):
+            return 0, (d if both else jnp.where(place_ref[0] == which, d, 0))
+
+        return pl.BlockSpec((rows, LANES), index)
+
     return pl.pallas_call(
-        turn_filters_body,
-        grid=(n_dev,),
-        in_specs=[spec, spec],
-        out_specs=pl.BlockSpec((1, 2, LANES * n_rows, LANES), lambda d: (d, 0, 0, 0)),
-        out_shape=jax.ShapeDtypeStruct((n_dev, 2, LANES * n_rows, LANES), F32),
-        cost_estimate=pl.CostEstimate(flops=10**9, bytes_accessed=4 * 4 * rows * LANES * n_dev, transcendentals=0),
+        functools.partial(turn_share_body, n_chunks, units),
+        grid_spec=pltpu.PrefetchScalarGridSpec(
+            num_scalar_prefetch=1,
+            grid=(n_dev,),
+            in_specs=[pick(0), pick(1)],
+            out_specs=pl.BlockSpec((1, n_chunks, units * n_rows, LANES), lambda d, place_ref: (d, 0, 0, 0)),
+            scratch_shapes=[] if units >= n_chan else [pltpu.VMEM((n_chunks, n_chan * n_rows, LANES), F32)],
+        ),
+        out_shape=jax.ShapeDtypeStruct((n_dev, n_chunks, units * n_rows, LANES), F32),
+        cost_estimate=pl.CostEstimate(flops=10**9, bytes_accessed=16 * rows * units * n_chunks * n_dev, transcendentals=0),
         compiler_params=pltpu.CompilerParams(dimension_semantics=("arbitrary",)),
-        name="turn_filters",
-    )(filt_one, filt_two)
+        name="turn_share",
+    )(place, filt_one, filt_two)
 
 
 def project_body(n_chunks, flag_ref, u_ref, halo_ref, *refs):
@@ -218,18 +247,40 @@
     return spectrum, signal
 
 
-def exchange_body(n_dev, group, ahead, skip_ref, filt_ref, sent_ref, wide_ref, thin_ref, fwd_ref, inv_ref, last_ref, twist_ref, back_ref, got_ref, h_ref, done_ref, parts_ref, spec_one_ref, spec_two_ref, sent_sem, got_sem, h_sem, back_sem, done_sem):
+def exchange_body(n_dev, n_groups, group, skip_ref, share_ref, sent_ref, wide_ref, thin_ref, fwd_ref, inv_ref, last_ref, twist_ref, back_ref, got_ref, filt_ref, done_ref, parts_ref, spec_one_ref, spec_two_ref, sent_sem, got_sem, share_sem, filt_sem, back_sem, done_sem):
     n_chunks, _, _, chunk_rows, _ = sent_ref.shape
     n_high = twist_ref.shape[1]
     per_src = n_high // n_dev
     n_chan = chunk_rows // per_src
-    me = lax.axis_index("sp")
+    me, my_group = lax.axis_index("sp"), lax.axis_index("dp")
+    share_rows = share_ref.shape[2]
     spectrum, signal = spectrum_tools(group, n_high, (wide_ref, thin_ref, fwd_ref, inv_ref, last_ref, twist_ref), parts_ref)
 
     barrier = pltpu.get_barrier_semaphore()
     for off in range(1, n_dev):
         pl.semaphore_signal(barrier, inc=1, device_id={"sp": lax.rem(me + off, n_dev)}, device_id_type=pl.DeviceIdType.MESH)
-    pl.semaphore_wait(barrier, n_dev - 1)
+    for off in range(1, n_groups):
+        pl.semaphore_signal(barrier, inc=1, device_id={"dp": lax.rem(my_group + off, n_groups)}, device_id_type=pl.DeviceIdType.MESH)
+    pl.semaphore_wait(barrier, n_dev + n_groups - 2)
+
+    def sharing(k, off):
+        return pltpu.make_async_remote_copy(
+            src_ref=share_ref.at[:, k],
+            dst_ref=share_of(k),
+            send_sem=share_sem.at[k],
+            recv_sem=filt_sem.at[k],
+            device_id={"dp": lax.rem(my_group + off, n_groups)},
+            device_id_type=pl.DeviceIdType.MESH,
+        )
+
+    def share_of(k):
+        return filt_ref.at[k, :, pl.ds(pl.multiple_of(my_group * share_rows, share_rows), share_rows), :]
+
+    def own_share(k):
+        return pltpu.make_async_copy(share_ref.at[:, k], share_of(k), filt_sem.at[k])
+
+    def all_shares(k):
+        return pltpu.make_async_copy(filt_ref.at[k], filt_ref.at[k], filt_sem.at[k])
 
     def sending(k, off):
         dest = lax.rem(me + off, n_dev)
@@ -245,11 +296,6 @@
     def keeping(k):
         return pltpu.make_async_copy(sent_ref.at[k, me], got_ref.at[k, me], got_sem.at[k, 0])
 
-    def fetching(k, slot):
-        return pltpu.make_async_copy(
-            filt_ref.at[:, :, pl.ds(pl.multiple_of(k * chunk_rows, chunk_rows), chunk_rows), :], h_ref.at[slot], h_sem.at[slot]
-        )
-
     block = per_src * n_chan
 
     def part_of(slot, dest):
@@ -269,28 +315,19 @@
     def storing(k, slot):
         return pltpu.make_async_copy(part_of(slot, me), back_ref.at[k, me], done_sem.at[slot, 0])
 
-    def launch(k):
+    @pl.loop(0, n_chunks)
+    def _(k):
+        own_share(k).start()
         keeping(k).start()
+        for off in range(1, n_groups):
+            sharing(k, off).start()
         for off in range(1, n_dev):
             sending(k, off).start()
-
-    for k in range(ahead):
-        launch(k)
-    fetching(0, 0).start()
 
     @pl.loop(0, n_chunks)
     def _(k):
         slot = lax.rem(k, 2)
-
-        @pl.when(k + ahead < n_chunks)
-        def _():
-            launch(k + ahead)
-
-        @pl.when(k + 1 < n_chunks)
-        def _():
-            fetching(k + 1, 1 - slot).start()
-
-        fetching(k, slot).wait()
+        all_shares(k).wait()
         keeping(k).wait()
         for off in range(1, n_dev):
             sending(k, off).wait_recv()
@@ -306,8 +343,8 @@
             first = i * group
 
             def load_h(which, g):
-                start = pl.multiple_of((first + g) * per_src, per_src)
-                return h_ref[slot, :, which, pl.ds(start, per_src), :].reshape(n_high, LANES)
+                start = pl.multiple_of((which * n_chan + first + g) * per_src, per_src)
+                return filt_ref[k, :, pl.ds(start, per_src), :].reshape(n_high, LANES)
 
             def load_x(which, g):
                 start = pl.multiple_of((first + g) * per_src, per_src)
@@ -337,36 +374,39 @@
         for off in range(1, n_dev):
             sending(k, off).wait_send()
             returning(k, 0, off).wait_recv()
-
-
-def exchange(skips, filters, sent, tables, n_dev, group=4, ahead=3):
+        for off in range(1, n_groups):
+            sharing(k, off).wait_send()
+
+
+def exchange(skips, share, sent, tables, n_dev, n_groups, group=4):
     n_chunks, _, _, chunk_rows, _ = sent.shape
     n_high = tables[-1].shape[1]
     n_chan = chunk_rows // (n_high // n_dev)
     any_spec = pl.BlockSpec(memory_space=pl.ANY)
     vmem_spec = pl.BlockSpec(memory_space=pltpu.VMEM)
     return pl.pallas_call(
-        functools.partial(exchange_body, n_dev, group, ahead),
+        functools.partial(exchange_body, n_dev, n_groups, group),
         in_specs=[pl.BlockSpec(memory_space=pltpu.SMEM), any_spec, any_spec] + [vmem_spec] * len(tables),
         out_specs=any_spec,
         out_shape=jax.ShapeDtypeStruct((n_chunks, n_dev, chunk_rows, LANES), F32),
         scratch_shapes=[
             pltpu.VMEM((n_chunks, n_dev, 2, chunk_rows, LANES), F32),
-            pltpu.VMEM((2, n_dev, 2, chunk_rows, LANES), F32),
+            pltpu.VMEM((n_chunks, n_dev, 2 * chunk_rows, LANES), F32),
             pltpu.VMEM((2, n_high * n_chan, LANES), F32),
             pltpu.VMEM((group * n_high, 6 * LANES), BF16),
             pltpu.VMEM((group * n_high, 2 * LANES), F32),
             pltpu.VMEM((group * n_high, 2 * LANES), F32),
             pltpu.SemaphoreType.DMA((n_chunks, n_dev)),
             pltpu.SemaphoreType.DMA((n_chunks, n_dev)),
-            pltpu.SemaphoreType.DMA((2,)),
+            pltpu.SemaphoreType.DMA((n_chunks,)),
+            pltpu.SemaphoreType.DMA((n_chunks,)),
             pltpu.SemaphoreType.DMA((n_chunks, n_dev)),
             pltpu.SemaphoreType.DMA((2, n_dev)),
         ],
         cost_estimate=pl.CostEstimate(flops=10**11, bytes_accessed=40 * 2**20, transcendentals=0),
         compiler_params=pltpu.CompilerParams(collective_id=0, has_side_effects=True, vmem_limit_bytes=60 * 2**20),
         name="exchange",
-    )(skips, filters, sent, *tables)
+    )(skips, share, sent, *tables)
 
 
 def finish_body(gate_ref, u_ref, w_ref, back_ref, out_ref, y_ref):
@@ -402,8 +442,12 @@
 
 
 def solution(mesh):
-    n_dev = mesh.shape["sp"]
+    n_dev, n_groups = mesh.shape["sp"], mesh.shape["dp"]
     n_chunks = 8
+    n_chan = LANES // n_chunks
+    if (2 * n_chan) % n_groups:
+        raise ValueError("uneven groups")
+    units = 2 * n_chan // n_groups
     halo_perm = list(zip(range(n_dev - 1), range(1, n_dev)))
 
     def local_step(u_in, w_in, b_in, conv_taps, w_out, skip_one, skip_two, filt_one, filt_two):
@@ -412,15 +456,16 @@
         rows = u.shape[0]
         tables = [jnp.asarray(t) for t in transform_tables(rows * n_dev)]
 
-        def swap(x):
-            return lax.all_to_all(x, "sp", 0, 0, tiled=True)
-
         halo = lax.ppermute(u[-8:].astype(F32), "sp", halo_perm)
         has_prev = (rank > 0).astype(jnp.int32)[None]
-        filters = swap(turn_filters(filt_one, filt_two, n_dev))
+        first_unit = lax.axis_index("dp") * units
+        place = jnp.stack([first_unit // n_chan, first_unit % n_chan])
+        share = turn_share(place, filt_one, filt_two, n_dev, n_chunks, units)
+        share, halo = lax.optimization_barrier((share, halo))
+        share = lax.all_to_all(share, "sp", 0, 0, tiled=True)
         sent, gate = project(has_prev, u, halo, w_in, b_in[None], conv_taps, n_dev, n_chunks)
         skips = lax.dynamic_slice_in_dim(jnp.stack([skip_one, skip_two]), rank * LANES, LANES, axis=1)
-        back = exchange(skips, filters, sent, tables, n_dev)
+        back = exchange(skips, share, sent, tables, n_dev, n_groups)
         back = back.reshape(n_chunks, n_dev, rows // LANES, LANES // n_chunks, LANES)
         return finish(gate, u, w_out, back)[None]
 

time: 598 us -> 502 us (0.84)
  waiting for transfers between devices: 175 us -> 33.5 us
  Pallas kernels: 410 us -> 455 us
    ppermute x1, waiting for transfers between devices: 175 us -> 0.01 us  [local_step(): halo = lax.ppermute(u[-8:].astype(F32), 'sp', halo_perm)]
    pallas_call x2, Pallas kernels: 338 us -> 384 us  [the longest x1 367 us: exchange(): pl.pallas_call(functools.partial(exchange_body, n_dev, n_groups, group),...]
    all_to_all x1, waiting for transfers between devices: 0.01 us -> 33.5 us  [local_step(): share = lax.all_to_all(share, 'sp', 0, 0, tiled=True)]
  transfers between devices with their start and end apart: 2 -> 2, of which waited for: 1 -> 1; matrix products, arithmetic and copies ran while one was open for 0% -> 0% of each run, Pallas kernels for 10% -> 15%
where the time goes in v2:
time: 502 us; the launch traced here: 501 us
  Pallas kernels  455 us (91%)
  waiting for transfers between devices  33.5 us (7%)
  starting transfers between devices  9.65 us (2%)
    pallas_call x1, Pallas kernels, exchange(): pl.pallas_call(functools.partial(exchange_body, n_dev, n_groups, group),...  367 us
    pallas_call x1, Pallas kernels, project(): pl.pallas_call(functools.partial(project_body, n_chunks), grid=(steps,),...  59.4 us
    all_to_all x1, waiting for transfers between devices, local_step(): share = lax.all_to_all(share, 'sp', 0, 0, tiled=True)  33.5 us
    pallas_call x1, Pallas kernels, turn_share(): pl.pallas_call(functools.partial(turn_share_body, n_chunks, units), grid_...  16.5 us
    pallas_call x1, Pallas kernels, finish(): pl.pallas_call(finish_body, grid=(rows // tile,), in_specs=[pl.BlockSpec(...  12.3 us
  transfers between devices with their start and end apart: 2, of which 1 were waited for; matrix products, arithmetic and copies ran while one was open for 0% of the time, Pallas kernels for 15%

profile of v2, /device:TPU:113, one launch (start us, length us, event | category | flops | bytes accessed | tf_op | source)
XLA Modules:
  0.0 501.3 jit_solution(2390609158766314328)
XLA Ops:
  0.0 0.7 bitcast_convert_fusion
  0.7 4.6 collective-permute-start
  5.3 0.6 pad_add_fusion.place_ref
  5.9 16.5 %turn_share.1 = f32[8,8,256,128]{3,2,1,0:T(8,128)} custom-call(s32[2]{0:T(128)} %pad_add_fusion.place_ref, f32[2048,1024]{1,0:T(8,128)} %one_ref.1, f32[2048,1024]{1,0:T(8,128)} %two_ref.1), custom_call_target="tpu_custom_call" | custom-call | flops 1000000000 | bytes 33554432 | tf_op jit(solution)/shard_map/turn_share/pallas_call | solution.py:96
  22.4 0.0 copy-start.1
  22.4 0.0 copy-start.2
  22.4 0.0 collective-permute-done.halo_ref
  22.4 0.0 copy-start.3
  22.4 0.6 copy-done.3
  23.0 5.1 %all-to-all-start = ((f32[8,8,256,128]{3,2,1,0:T(8,128)}), f32[8,8,256,128]{3,2,1,0:T(8,128)}, u32[]{:S(2)}, u32[]{:S(2)}) async-start(f32[8,8,256,128]{3,2,1,0:T(8,128)} %turn_share.1), calls=%async_computation | async-start | bytes 16777216 | tf_op jit(solution)/shard_map/all_to_all | solution.py:465
  28.1 0.0 copy-done.1
  28.1 0.0 copy-done.2
  28.1 0.7 fusion.skip_ref
  28.8 59.4 %project.1 = (f32[8,8,2,256,128]{4,3,2,1,0:T(8,128)}, bf16[2048,1024]{1,0:T(8,128)(2,1)}) custom-call(s32[1]{0:T(128)} %bitcast.flag_ref, bf16[2048,1024]{1,0:T(8,128)(2,1)} %bitcast.13, f32[8,1024]{1,0:T(8,128)} %copy-done.3, bf16[1024,3072]{1,0:T(8,128)(2,1)} %refs_2_.1, bf16[1024,3072]{1,0:T(8,128)(2,1)} %refs_2_.1, bf16[1024,3072]{1,0:T(8,128)(2,1)} %refs_2_.1, ...), custom_call_target="tpu_custom_call" | custom-call | flops 12884901888 | bytes 31457280 | tf_op jit(solution)/shard_map/project/pallas_call | solution.py:161
  88.2 33.5 %all-to-all-done.share_ref = f32[8,8,256,128]{3,2,1,0:T(8,128)} async-done(((f32[8,8,256,128]{3,2,1,0:T(8,128)}), f32[8,8,256,128]{3,2,1,0:T(8,128)}, u32[]{:S(2)}, u32[]{:S(2)}) %all-to-all-start) | async-done | bytes 8388640 | tf_op jit(solution)/shard_map/all_to_all | solution.py:465
  121.7 0.0 copy-start
  121.7 367.2 %exchange.1 = f32[8,8,256,128]{3,2,1,0:T(8,128)} custom-call(f32[2,128]{1,0:T(2,128)} %fusion.skip_ref, f32[8,8,256,128]{3,2,1,0:T(8,128)} %all-to-all-done.share_ref, f32[8,8,2,256,128]{4,3,2,1,0:T(8,128)} %get-tuple-element.12.sent_ref, bf16[256,768]{1,0:T(8,128)(2,1)} %constant.52.clone.wide_ref, bf16[256,384]{1,0:T(8,128)(2,1)} %constant.53.clone.thin_ref, ...), custom_call_target="tpu_custom_call" | custom-call | flops 99999997952 | bytes 41943040 | tf_op jit(solution)/shard_map/exchange/pallas_call | solution.py:387
  488.9 0.0 copy-done
  488.9 12.3 %finish.1 = bf16[2048,1024]{1,0:T(8,128)(2,1)} custom-call(bf16[2048,1024]{1,0:T(8,128)(2,1)} %get-tuple-element.10.gate_ref, bf16[2048,1024]{1,0:T(8,128)(2,1)} %bitcast.14, bf16[1024,1024]{1,0:T(8,128)(2,1)S(1)} %copy-done, f32[8,8,16,16,128]{4,3,2,1,0:T(8,128)} %bitcast.12), custom_call_target="tpu_custom_call" | custom-call | flops 4294967296 | bytes 20971520 | tf_op jit(solution)/shard_map/finish/pallas_call | solution.py:426
Async XLA Ops:
  0.7 21.7 %collective-permute-start = (f32[8,1024]{1,0:T(8,128)S(1)}, f32[8,1024]{1,0:T(8,128)S(1)}, u32[]{:S(2)}, u32[]{:S(2)}) collective-permute-start(f32[8,1024]{1,0:T(8,128)S(1)} %bitcast_convert_fusion), channel_id=1, source_target_pairs={{0,1},{1,2},{2,3},{3,4},{4,5},{5,6},{6,7},{8,9},{9,10},{10,11},{11... | collective-permute-start | bytes 98312 | tf_op jit(solution)/shard_map/ppermute | solution.py:459
  22.4 5.7 %copy-start.1 = (f32[1024]{0:T(1024)S(1)}, f32[1024]{0:T(1024)}, u32[]{:S(2)}) copy-start(f32[1024]{0:T(1024)} %param.20) | copy-start | bytes 12292
  22.4 5.7 %copy-start.2 = (f32[1024]{0:T(1024)S(1)}, f32[1024]{0:T(1024)}, u32[]{:S(2)}) copy-start(f32[1024]{0:T(1024)} %param.21) | copy-start | bytes 12292
  22.4 0.6 copy-start.3
  23.0 98.7 %all-to-all-start = ((f32[8,8,256,128]{3,2,1,0:T(8,128)}), f32[8,8,256,128]{3,2,1,0:T(8,128)}, u32[]{:S(2)}, u32[]{:S(2)}) async-start(f32[8,8,256,128]{3,2,1,0:T(8,128)} %turn_share.1), calls=%async_computation | async-start | bytes 16777216 | tf_op jit(solution)/shard_map/all_to_all | solution.py:465
  121.7 367.2 %copy-start = (bf16[1024,1024]{1,0:T(8,128)(2,1)S(1)}, bf16[1024,1024]{1,0:T(8,128)(2,1)}, u32[]{:S(2)}) copy-start(bf16[1024,1024]{1,0:T(8,128)(2,1)} %w_ref.1) | copy-start | bytes 6291460

commit v3 on v2

--- a/solution.py
+++ b/solution.py
@@ -298,22 +298,22 @@
 
     block = per_src * n_chan
 
-    def part_of(slot, dest):
-        return done_ref.at[slot, pl.ds(pl.multiple_of(dest * block, block), block), :]
-
-    def returning(k, slot, off):
+    def part_of(k, dest):
+        return done_ref.at[k, pl.ds(pl.multiple_of(dest * block, block), block), :]
+
+    def returning(k, off):
         dest = lax.rem(me + off, n_dev)
         return pltpu.make_async_remote_copy(
-            src_ref=part_of(slot, dest),
+            src_ref=part_of(k, dest),
             dst_ref=back_ref.at[k, me],
-            send_sem=done_sem.at[slot, off],
+            send_sem=done_sem.at[k, off],
             recv_sem=back_sem.at[k, off],
             device_id={"sp": dest},
             device_id_type=pl.DeviceIdType.MESH,
         )
 
-    def storing(k, slot):
-        return pltpu.make_async_copy(part_of(slot, me), back_ref.at[k, me], done_sem.at[slot, 0])
+    def storing(k):
+        return pltpu.make_async_copy(part_of(k, me), back_ref.at[k, me], done_sem.at[k, 0])
 
     @pl.loop(0, n_chunks)
     def _(k):
@@ -326,17 +326,10 @@
 
     @pl.loop(0, n_chunks)
     def _(k):
-        slot = lax.rem(k, 2)
         all_shares(k).wait()
         keeping(k).wait()
         for off in range(1, n_dev):
             sending(k, off).wait_recv()
-
-        @pl.when(k >= 2)
-        def _():
-            storing(k - 2, slot).wait()
-            for off in range(1, n_dev):
-                returning(k - 2, slot, off).wait_send()
 
         @pl.loop(0, n_chan // group)
         def _(i):
@@ -358,22 +351,18 @@
             gated = [load_x(1, g) * (conv[g] + skip_ref[0, chan + g] * values[g]) for g in range(group)]
             conv = signal(spectrum(gated, False), spec_two_ref)
             for g in range(group):
-                done_ref[slot, pl.ds(first + g, n_high, stride=n_chan), :] = conv[g] + skip_ref[1, chan + g] * gated[g]
-
-        storing(k, slot).start()
+                done_ref[k, pl.ds(first + g, n_high, stride=n_chan), :] = conv[g] + skip_ref[1, chan + g] * gated[g]
+
+        storing(k).start()
         for off in range(1, n_dev):
-            returning(k, slot, off).start()
-
-    for k in range(max(0, n_chunks - 2), n_chunks):
-        storing(k, k % 2).wait()
-        for off in range(1, n_dev):
-            returning(k, k % 2, off).wait_send()
+            returning(k, off).start()
 
     @pl.loop(0, n_chunks)
     def _(k):
         for off in range(1, n_dev):
             sending(k, off).wait_send()
-            returning(k, 0, off).wait_recv()
+            returning(k, off).wait()
+        storing(k).wait()
         for off in range(1, n_groups):
             sharing(k, off).wait_send()
 
@@ -392,7 +381,7 @@
         scratch_shapes=[
             pltpu.VMEM((n_chunks, n_dev, 2, chunk_rows, LANES), F32),
             pltpu.VMEM((n_chunks, n_dev, 2 * chunk_rows, LANES), F32),
-            pltpu.VMEM((2, n_high * n_chan, LANES), F32),
+            pltpu.VMEM((n_chunks, n_high * n_chan, LANES), F32),
             pltpu.VMEM((group * n_high, 6 * LANES), BF16),
             pltpu.VMEM((group * n_high, 2 * LANES), F32),
             pltpu.VMEM((group * n_high, 2 * LANES), F32),
@@ -401,7 +390,7 @@
             pltpu.SemaphoreType.DMA((n_chunks,)),
             pltpu.SemaphoreType.DMA((n_chunks,)),
             pltpu.SemaphoreType.DMA((n_chunks, n_dev)),
-            pltpu.SemaphoreType.DMA((2, n_dev)),
+            pltpu.SemaphoreType.DMA((n_chunks, n_dev)),
         ],
         cost_estimate=pl.CostEstimate(flops=10**11, bytes_accessed=40 * 2**20, transcendentals=0),
         compiler_params=pltpu.CompilerParams(collective_id=0, has_side_effects=True, vmem_limit_bytes=60 * 2**20),

time: 502 us -> 413 us (0.82)
  Pallas kernels: 455 us -> 367 us
    pallas_call x1, Pallas kernels: 367 us -> 279 us  [exchange(): pl.pallas_call(functools.partial(exchange_body, n_dev, n_groups, group),...]
  transfers between devices with their start and end apart: 2 -> 2, of which waited for: 1 -> 1; matrix products, arithmetic and copies ran while one was open for 0% -> 0% of each run, Pallas kernels for 15% -> 18%
where the time goes in v3:
time: 413 us
  Pallas kernels  367 us (89%)
  waiting for transfers between devices  33.5 us (8%)
  starting transfers between devices  9.65 us (2%)
    pallas_call x1, Pallas kernels, exchange(): pl.pallas_call(functools.partial(exchange_body, n_dev, n_groups, group),...  279 us
    pallas_call x1, Pallas kernels, project(): pl.pallas_call(functools.partial(project_body, n_chunks), grid=(steps,),...  59.4 us
    all_to_all x1, waiting for transfers between devices, local_step(): share = lax.all_to_all(share, 'sp', 0, 0, tiled=True)  33.5 us
    pallas_call x1, Pallas kernels, turn_share(): pl.pallas_call(functools.partial(turn_share_body, n_chunks, units), grid_...  16.5 us
    pallas_call x1, Pallas kernels, finish(): pl.pallas_call(finish_body, grid=(rows // tile,), in_specs=[pl.BlockSpec(...  12.4 us
  transfers between devices with their start and end apart: 2, of which 1 were waited for; matrix products, arithmetic and copies ran while one was open for 0% of the time, Pallas kernels for 18%

profile of v3, /device:TPU:113, one launch (start us, length us, event | category | flops | bytes accessed | tf_op | source)
XLA Modules:
  0.0 413.0 jit_solution(15954145960239876069)
XLA Ops:
  0.0 0.7 bitcast_convert_fusion
  0.7 4.6 %collective-permute-start = (f32[8,1024]{1,0:T(8,128)S(1)}, f32[8,1024]{1,0:T(8,128)S(1)}, u32[]{:S(2)}, u32[]{:S(2)}) collective-permute-start(f32[8,1024]{1,0:T(8,128)S(1)} %bitcast_convert_fusion), channel_id=1, source_target_pairs={{0,1},{1,2},{2,3},{3,4},{4,5},{5,6},{6,7},{8,9},{9,10},{10,11},{11... | collective-permute-start | bytes 98312 | tf_op jit(solution)/shard_map/ppermute | solution.py:448
  5.3 0.6 pad_add_fusion.place_ref
  5.9 16.5 %turn_share.1 = f32[8,8,256,128]{3,2,1,0:T(8,128)} custom-call(s32[2]{0:T(128)} %pad_add_fusion.place_ref, f32[2048,1024]{1,0:T(8,128)} %one_ref.1, f32[2048,1024]{1,0:T(8,128)} %two_ref.1), custom_call_target="tpu_custom_call" | custom-call | flops 1000000000 | bytes 33554432 | tf_op jit(solution)/shard_map/turn_share/pallas_call | solution.py:96
  22.4 0.0 copy-start.1
  22.4 0.0 copy-start.2
  22.4 0.0 collective-permute-done.halo_ref
  22.4 0.0 copy-start.3
  22.4 0.6 copy-done.3
  23.0 5.1 %all-to-all-start = ((f32[8,8,256,128]{3,2,1,0:T(8,128)}), f32[8,8,256,128]{3,2,1,0:T(8,128)}, u32[]{:S(2)}, u32[]{:S(2)}) async-start(f32[8,8,256,128]{3,2,1,0:T(8,128)} %turn_share.1), calls=%async_computation | async-start | bytes 16777216 | tf_op jit(solution)/shard_map/all_to_all | solution.py:454
  28.1 0.0 copy-done.1
  28.1 0.0 copy-done.2
  28.1 0.7 fusion.skip_ref
  28.8 59.4 %project.1 = (f32[8,8,2,256,128]{4,3,2,1,0:T(8,128)}, bf16[2048,1024]{1,0:T(8,128)(2,1)}) custom-call(s32[1]{0:T(128)} %bitcast.flag_ref, bf16[2048,1024]{1,0:T(8,128)(2,1)} %bitcast.13, f32[8,1024]{1,0:T(8,128)} %copy-done.3, bf16[1024,3072]{1,0:T(8,128)(2,1)} %refs_2_.1, bf16[1024,3072]{1,0:T(8,128)(2,1)} %refs_2_.1, bf16[1024,3072]{1,0:T(8,128)(2,1)} %refs_2_.1, ...), custom_call_target="tpu_custom_call" | custom-call | flops 12884901888 | bytes 31457280 | tf_op jit(solution)/shard_map/project/pallas_call | solution.py:161
  88.2 33.5 %all-to-all-done.share_ref = f32[8,8,256,128]{3,2,1,0:T(8,128)} async-done(((f32[8,8,256,128]{3,2,1,0:T(8,128)}), f32[8,8,256,128]{3,2,1,0:T(8,128)}, u32[]{:S(2)}, u32[]{:S(2)}) %all-to-all-start) | async-done | bytes 8388640 | tf_op jit(solution)/shard_map/all_to_all | solution.py:454
  121.7 0.0 copy-start
  121.7 278.9 %exchange.1 = f32[8,8,256,128]{3,2,1,0:T(8,128)} custom-call(f32[2,128]{1,0:T(2,128)} %fusion.skip_ref, f32[8,8,256,128]{3,2,1,0:T(8,128)} %all-to-all-done.share_ref, f32[8,8,2,256,128]{4,3,2,1,0:T(8,128)} %get-tuple-element.12.sent_ref, bf16[256,768]{1,0:T(8,128)(2,1)} %constant.52.clone.wide_ref, bf16[256,384]{1,0:T(8,128)(2,1)} %constant.53.clone.thin_ref, ...), custom_call_target="tpu_custom_call" | custom-call | flops 99999997952 | bytes 41943040 | tf_op jit(solution)/shard_map/exchange/pallas_call | solution.py:376
  400.6 0.0 copy-done
  400.6 12.4 %finish.1 = bf16[2048,1024]{1,0:T(8,128)(2,1)} custom-call(bf16[2048,1024]{1,0:T(8,128)(2,1)} %get-tuple-element.10.gate_ref, bf16[2048,1024]{1,0:T(8,128)(2,1)} %bitcast.14, bf16[1024,1024]{1,0:T(8,128)(2,1)S(1)} %copy-done, f32[8,8,16,16,128]{4,3,2,1,0:T(8,128)} %bitcast.12), custom_call_target="tpu_custom_call" | custom-call | flops 4294967296 | bytes 20971520 | tf_op jit(solution)/shard_map/finish/pallas_call | solution.py:415
Async XLA Ops:
  0.7 21.7 %collective-permute-start = (f32[8,1024]{1,0:T(8,128)S(1)}, f32[8,1024]{1,0:T(8,128)S(1)}, u32[]{:S(2)}, u32[]{:S(2)}) collective-permute-start(f32[8,1024]{1,0:T(8,128)S(1)} %bitcast_convert_fusion), channel_id=1, source_target_pairs={{0,1},{1,2},{2,3},{3,4},{4,5},{5,6},{6,7},{8,9},{9,10},{10,11},{11... | collective-permute-start | bytes 98312 | tf_op jit(solution)/shard_map/ppermute | solution.py:448
  22.4 5.7 %copy-start.1 = (f32[1024]{0:T(1024)S(1)}, f32[1024]{0:T(1024)}, u32[]{:S(2)}) copy-start(f32[1024]{0:T(1024)} %param.20) | copy-start | bytes 12292
  22.4 5.7 %copy-start.2 = (f32[1024]{0:T(1024)S(1)}, f32[1024]{0:T(1024)}, u32[]{:S(2)}) copy-start(f32[1024]{0:T(1024)} %param.21) | copy-start | bytes 12292
  22.4 0.6 copy-start.3
  23.0 98.7 %all-to-all-start = ((f32[8,8,256,128]{3,2,1,0:T(8,128)}), f32[8,8,256,128]{3,2,1,0:T(8,128)}, u32[]{:S(2)}, u32[]{:S(2)}) async-start(f32[8,8,256,128]{3,2,1,0:T(8,128)} %turn_share.1), calls=%async_computation | async-start | bytes 16777216 | tf_op jit(solution)/shard_map/all_to_all | solution.py:454
  121.7 278.9 %copy-start = (bf16[1024,1024]{1,0:T(8,128)(2,1)S(1)}, bf16[1024,1024]{1,0:T(8,128)(2,1)}, u32[]{:S(2)}) copy-start(bf16[1024,1024]{1,0:T(8,128)(2,1)} %w_ref.1) | copy-start | bytes 6291460

commit v4 on v3

--- a/solution.py
+++ b/solution.py
@@ -54,73 +54,129 @@
     return jnp.dot(a, b, preferred_element_type=F32)
 
 
-def turn_share_body(n_chunks, units, place_ref, one_ref, two_ref, out_ref, *scratch):
-    n_rows = one_ref.shape[0] // LANES
+def turn_rows(block, into_ref, n_chunks, row, n_rows):
+    turned = block.T
     n_chan = LANES // n_chunks
-
-    def turn(ref, into_ref, base):
+    for k in range(n_chunks):
+        into_ref[k, pl.ds(row, n_chan, stride=n_rows), :] = turned[k * n_chan : (k + 1) * n_chan]
+
+
+def share_filters(n_dev, n_groups, n_chunks, units, filt_refs, u_ref, share_ref, halo_ref, tail_ref, stage_ref, hold_ref, full_ref, sems):
+    stage_sem, sent_sem, share_sem, halo_sem = sems
+    me, my_group = lax.axis_index("sp"), lax.axis_index("dp")
+    rows = stage_ref.shape[1]
+    n_rows = rows // LANES
+    n_chan = LANES // n_chunks
+    first_unit = my_group * units
+    which_mine = first_unit // n_chan
+    per_dest = 2 if units == 2 * n_chan else 1
+    n_items = n_dev * per_dest
+
+    def target(off):
+        return lax.rem(me + off, n_dev)
+
+    def load(item, start):
+        slot = lax.rem(item, 2)
+        dest = target(item // per_dest + 1)
+        cols = pl.ds(pl.multiple_of(dest * LANES, LANES), LANES)
+
+        def copy(ref):
+            return pltpu.make_async_copy(ref.at[:, cols], stage_ref.at[slot], stage_sem.at[slot])
+
+        if not start:
+            copy(filt_refs[0]).wait()
+            return
+        which = lax.rem(item, 2) if per_dest == 2 else which_mine
+        for w, ref in enumerate(filt_refs):
+
+            @pl.when(which == w)
+            def _():
+                copy(ref).start()
+
+    load(0, True)
+    tail_ref[...] = u_ref[u_ref.shape[0] - tail_ref.shape[0] :, :].astype(F32)
+
+    barrier = pltpu.get_barrier_semaphore()
+    for off in range(1, n_dev):
+        pl.semaphore_signal(barrier, inc=1, device_id={"sp": target(off)}, device_id_type=pl.DeviceIdType.MESH)
+    pl.semaphore_wait(barrier, n_dev - 1)
+    halo_send(target, tail_ref, halo_ref, halo_sem).start()
+
+    @pl.loop(0, n_items)
+    def _(item):
+        slot = lax.rem(item, 2)
+        off = item // per_dest + 1
+        dest = target(off)
+
+        @pl.when(item + 1 < n_items)
+        def _():
+            load(item + 1, True)
+
+        load(item, False)
+        into = hold_ref.at[dest] if units >= n_chan else full_ref
+        base = lax.rem(item, per_dest) * (n_chan * n_rows)
+
         @pl.loop(0, n_rows)
         def _(r):
-            block = ref[pl.ds(pl.multiple_of(r * LANES, LANES), LANES), :].T
-            for k in range(n_chunks):
-                into_ref[k, pl.ds(base + r, n_chan, stride=n_rows), :] = block[k * n_chan : (k + 1) * n_chan]
-
-    if units == 2 * n_chan:
-        turn(one_ref, out_ref.at[0], 0)
-        turn(two_ref, out_ref.at[0], n_chan * n_rows)
-    else:
-        into_ref = out_ref.at[0] if units == n_chan else scratch[0]
-        for which, ref in enumerate((one_ref, two_ref)):
-
-            @pl.when(place_ref[0] == which)
-            def _():
-                turn(ref, into_ref, 0)
+            turn_rows(stage_ref[slot, pl.ds(pl.multiple_of(r * LANES, LANES), LANES), :], into, n_chunks, base + r, n_rows)
 
         if units < n_chan:
-            start = pl.multiple_of(place_ref[1] * n_rows, n_rows)
-            out_ref[0] = scratch[0][:, pl.ds(start, units * n_rows), :]
-
-
-def turn_share(place, filt_one, filt_two, n_dev, n_chunks, units):
-    rows = filt_one.shape[0]
-    n_rows = rows // LANES
-    n_chan = LANES // n_chunks
-    both = units == 2 * n_chan
-
-    def pick(which):
-        def index(d, place_ref):
-            return 0, (d if both else jnp.where(place_ref[0] == which, d, 0))
-
-        return pl.BlockSpec((rows, LANES), index)
-
-    return pl.pallas_call(
-        functools.partial(turn_share_body, n_chunks, units),
-        grid_spec=pltpu.PrefetchScalarGridSpec(
-            num_scalar_prefetch=1,
-            grid=(n_dev,),
-            in_specs=[pick(0), pick(1)],
-            out_specs=pl.BlockSpec((1, n_chunks, units * n_rows, LANES), lambda d, place_ref: (d, 0, 0, 0)),
-            scratch_shapes=[] if units >= n_chan else [pltpu.VMEM((n_chunks, n_chan * n_rows, LANES), F32)],
-        ),
-        out_shape=jax.ShapeDtypeStruct((n_dev, n_chunks, units * n_rows, LANES), F32),
-        cost_estimate=pl.CostEstimate(flops=10**9, bytes_accessed=16 * rows * units * n_chunks * n_dev, transcendentals=0),
-        compiler_params=pltpu.CompilerParams(dimension_semantics=("arbitrary",)),
-        name="turn_share",
-    )(place, filt_one, filt_two)
-
-
-def project_body(n_chunks, flag_ref, u_ref, halo_ref, *refs):
+            start = pl.multiple_of(lax.rem(first_unit, n_chan) * n_rows, n_rows)
+            hold_ref[dest] = full_ref[:, pl.ds(start, units * n_rows), :]
+
+        @pl.when(jnp.logical_and(lax.rem(item, per_dest) == per_dest - 1, off < n_dev))
+        def _():
+            share_send(me, target, hold_ref, share_ref, sent_sem, share_sem, off).start()
+
+    pltpu.make_async_copy(hold_ref.at[me], share_ref.at[me], sent_sem.at[0]).start()
+
+
+def share_send(me, target, hold_ref, share_ref, sent_sem, share_sem, off):
+    dest = target(off)
+    return pltpu.make_async_remote_copy(
+        src_ref=hold_ref.at[dest],
+        dst_ref=share_ref.at[me],
+        send_sem=sent_sem.at[off],
+        recv_sem=share_sem.at[off],
+        device_id={"sp": dest},
+        device_id_type=pl.DeviceIdType.MESH,
+    )
+
+
+def halo_send(target, tail_ref, halo_ref, halo_sem):
+    return pltpu.make_async_remote_copy(
+        src_ref=tail_ref,
+        dst_ref=halo_ref,
+        send_sem=halo_sem.at[0],
+        recv_sem=halo_sem.at[1],
+        device_id={"sp": target(1)},
+        device_id_type=pl.DeviceIdType.MESH,
+    )
+
+
+def project_body(n_dev, n_groups, n_chunks, units, u_ref, one_ref, two_ref, *refs):
     w_refs, b_refs, tap_refs = refs[:3], refs[3:6], refs[6:9]
-    sent_ref, gate_ref, p_ref = refs[9:]
+    sent_ref, gate_ref, share_ref, p_ref, halo_ref, tail_ref, stage_ref, hold_ref, full_ref, *sems = refs[9:]
+    stage_sem, sent_sem, share_sem, halo_sem = sems
     rows = u_ref.shape[0]
     n_rows = rows // LANES
     width = w_refs[0].shape[1]
-    per_chunk = LANES // n_chunks
+    me = lax.axis_index("sp")
+    step_idx = pl.program_id(0)
+
+    def target(off):
+        return lax.rem(me + off, n_dev)
+
+    @pl.when(step_idx == 0)
+    def _():
+        share_filters(n_dev, n_groups, n_chunks, units, (one_ref, two_ref), u_ref, share_ref, halo_ref, tail_ref, stage_ref, hold_ref, full_ref, sems)
+        halo_send(target, tail_ref, halo_ref, halo_sem).wait()
+
     for which in range(3):
         w = w_refs[which][...]
         bias = b_refs[which][...]
         halo = (dot32(halo_ref[...].astype(BF16), w) + bias).astype(BF16).astype(F32)
-        p_ref[0:8, :] = jnp.where(flag_ref[0] > 0, halo, 0.0)
+        p_ref[0:8, :] = jnp.where(me > 0, halo, 0.0)
         step = 2 * LANES
 
         @pl.loop(0, rows // step)
@@ -142,46 +198,62 @@
             else:
                 slot = 1 if which == 0 else 0
                 for d in range(width // LANES):
-                    turned = mixed[:, d * LANES : (d + 1) * LANES].astype(F32).T
-                    for k in range(n_chunks):
-                        sent_ref[k, d, slot, pl.ds(r, per_chunk, stride=n_rows), :] = turned[k * per_chunk : (k + 1) * per_chunk]
-
-
-def project(has_prev, u, halo, w_in, b_in, taps, n_dev, n_chunks):
+                    block = mixed[:, d * LANES : (d + 1) * LANES].astype(F32)
+                    turn_rows(block, sent_ref.at[:, d, slot], n_chunks, r, n_rows)
+
+    @pl.when(step_idx == pl.num_programs(0) - 1)
+    def _():
+        pltpu.make_async_copy(hold_ref.at[me], share_ref.at[me], sent_sem.at[0]).wait()
+        for off in range(1, n_dev):
+            share_send(me, target, hold_ref, share_ref, sent_sem, share_sem, off).wait()
+
+
+def project(u, filt_one, filt_two, w_in, b_in, taps, n_dev, n_groups, n_chunks, units):
     rows, depth = u.shape
     model = w_in.shape[1] // 3
     width = 2 * LANES
     steps = model // width
     n_rows = rows // LANES
-    per_chunk = LANES // n_chunks
-    chunk_rows = per_chunk * n_rows
-    w_specs = [pl.BlockSpec((depth, width), functools.partial(lambda off, j: (0, off + j), t * steps)) for t in range(3)]
-    b_specs = [pl.BlockSpec((1, width), functools.partial(lambda off, j: (0, off + j), t * steps)) for t in range(3)]
-    t_specs = [pl.BlockSpec((3, width), functools.partial(lambda off, j: (0, off + j), t * steps)) for t in range(3)]
+    n_chan = LANES // n_chunks
+    chunk_rows = n_chan * n_rows
+    any_spec = pl.BlockSpec(memory_space=pl.ANY)
+
+    def third(height):
+        return [pl.BlockSpec((height, width), functools.partial(lambda off, j: (0, off + j), t * steps)) for t in range(3)]
+
+    full_shape = (n_chunks, chunk_rows, LANES) if units < n_chan else (1, 8, LANES)
     return pl.pallas_call(
-        functools.partial(project_body, n_chunks),
+        functools.partial(project_body, n_dev, n_groups, n_chunks, units),
         grid=(steps,),
-        in_specs=[
-            pl.BlockSpec(memory_space=pltpu.SMEM),
-            pl.BlockSpec((rows, depth), lambda j: (0, 0)),
-            pl.BlockSpec((8, depth), lambda j: (0, 0)),
-            *w_specs,
-            *b_specs,
-            *t_specs,
-        ],
+        in_specs=[pl.BlockSpec((rows, depth), lambda j: (0, 0)), any_spec, any_spec, *third(depth), *third(1), *third(3)],
         out_specs=[
             pl.BlockSpec((n_chunks, 2, 2, chunk_rows, LANES), lambda j: (0, j, 0, 0, 0)),
             pl.BlockSpec((rows, width), lambda j: (0, j)),
+            any_spec,
         ],
         out_shape=[
             jax.ShapeDtypeStruct((n_chunks, n_dev, 2, chunk_rows, LANES), F32),
             jax.ShapeDtypeStruct((rows, model), BF16),
+            jax.ShapeDtypeStruct((n_dev, n_chunks, units * n_rows, LANES), F32),
         ],
-        scratch_shapes=[pltpu.VMEM((rows + 8, width), F32)],
-        cost_estimate=pl.CostEstimate(flops=2 * rows * depth * 3 * model, bytes_accessed=30 * 2**20, transcendentals=0),
-        compiler_params=pltpu.CompilerParams(dimension_semantics=("arbitrary",), vmem_limit_bytes=60 * 2**20),
+        scratch_shapes=[
+            pltpu.VMEM((rows + 8, width), F32),
+            pltpu.VMEM((8, depth), F32),
+            pltpu.VMEM((8, depth), F32),
+            pltpu.VMEM((2, rows, LANES), F32),
+            pltpu.VMEM((n_dev, n_chunks, units * n_rows, LANES), F32),
+            pltpu.VMEM(full_shape, F32),
+            pltpu.SemaphoreType.DMA((2,)),
+            pltpu.SemaphoreType.DMA((n_dev,)),
+            pltpu.SemaphoreType.DMA((n_dev,)),
+            pltpu.SemaphoreType.DMA((2,)),
+        ],
+        cost_estimate=pl.CostEstimate(flops=2 * rows * depth * 3 * model, bytes_accessed=50 * 2**20, transcendentals=0),
+        compiler_params=pltpu.CompilerParams(
+            dimension_semantics=("arbitrary",), collective_id=0, has_side_effects=True, vmem_limit_bytes=60 * 2**20
+        ),
         name="project",
-    )(has_prev, u, halo, w_in, w_in, w_in, b_in, b_in, b_in, taps, taps, taps)
+    )(u, filt_one, filt_two, w_in, w_in, w_in, b_in, b_in, b_in, taps, taps, taps)
 
 
 def spectrum_tools(group, n_high, tables, parts_ref):
@@ -247,7 +319,7 @@
     return spectrum, signal
 
 
-def exchange_body(n_dev, n_groups, group, skip_ref, share_ref, sent_ref, wide_ref, thin_ref, fwd_ref, inv_ref, last_ref, twist_ref, back_ref, got_ref, filt_ref, done_ref, parts_ref, spec_one_ref, spec_two_ref, sent_sem, got_sem, share_sem, filt_sem, back_sem, done_sem):
+def exchange_body(n_dev, n_groups, group, skip_one_ref, skip_two_ref, share_ref, sent_ref, wide_ref, thin_ref, fwd_ref, inv_ref, last_ref, twist_ref, back_ref, got_ref, filt_ref, done_ref, parts_ref, spec_one_ref, spec_two_ref, sent_sem, got_sem, share_sem, filt_sem, back_sem, done_sem):
     n_chunks, _, _, chunk_rows, _ = sent_ref.shape
     n_high = twist_ref.shape[1]
     per_src = n_high // n_dev
@@ -343,15 +415,15 @@
                 start = pl.multiple_of((first + g) * per_src, per_src)
                 return got_ref[k, :, which, pl.ds(start, per_src), :].reshape(n_high, LANES)
 
-            chan = k * n_chan + first
+            chan = me * LANES + k * n_chan + first
             spec_one_ref[...] = spectrum([load_h(0, g) for g in range(group)], False)
             spec_two_ref[...] = spectrum([load_h(1, g) for g in range(group)], False)
             values = [load_x(0, g) for g in range(group)]
             conv = signal(spectrum(values, True), spec_one_ref)
-            gated = [load_x(1, g) * (conv[g] + skip_ref[0, chan + g] * values[g]) for g in range(group)]
+            gated = [load_x(1, g) * (conv[g] + skip_one_ref[chan + g] * values[g]) for g in range(group)]
             conv = signal(spectrum(gated, False), spec_two_ref)
             for g in range(group):
-                done_ref[k, pl.ds(first + g, n_high, stride=n_chan), :] = conv[g] + skip_ref[1, chan + g] * gated[g]
+                done_ref[k, pl.ds(first + g, n_high, stride=n_chan), :] = conv[g] + skip_two_ref[chan + g] * gated[g]
 
         storing(k).start()
         for off in range(1, n_dev):
@@ -367,7 +439,7 @@
             sharing(k, off).wait_send()
 
 
-def exchange(skips, share, sent, tables, n_dev, n_groups, group=4):
+def exchange(skip_one, skip_two, share, sent, tables, n_dev, n_groups, group=4):
     n_chunks, _, _, chunk_rows, _ = sent.shape
     n_high = tables[-1].shape[1]
     n_chan = chunk_rows // (n_high // n_dev)
@@ -375,7 +447,7 @@
     vmem_spec = pl.BlockSpec(memory_space=pltpu.VMEM)
     return pl.pallas_call(
         functools.partial(exchange_body, n_dev, n_groups, group),
-        in_specs=[pl.BlockSpec(memory_space=pltpu.SMEM), any_spec, any_spec] + [vmem_spec] * len(tables),
+        in_specs=[pl.BlockSpec(memory_space=pltpu.SMEM)] * 2 + [any_spec, any_spec] + [vmem_spec] * len(tables),
         out_specs=any_spec,
         out_shape=jax.ShapeDtypeStruct((n_chunks, n_dev, chunk_rows, LANES), F32),
         scratch_shapes=[
@@ -393,9 +465,9 @@
             pltpu.SemaphoreType.DMA((n_chunks, n_dev)),
         ],
         cost_estimate=pl.CostEstimate(flops=10**11, bytes_accessed=40 * 2**20, transcendentals=0),
-        compiler_params=pltpu.CompilerParams(collective_id=0, has_side_effects=True, vmem_limit_bytes=60 * 2**20),
+        compiler_params=pltpu.CompilerParams(collective_id=1, has_side_effects=True, vmem_limit_bytes=60 * 2**20),
         name="exchange",
-    )(skips, share, sent, *tables)
+    )(skip_one, skip_two, share, sent, *tables)
 
 
 def finish_body(gate_ref, u_ref, w_ref, back_ref, out_ref, y_ref):
@@ -437,24 +509,12 @@
     if (2 * n_chan) % n_groups:
         raise ValueError("uneven groups")
     units = 2 * n_chan // n_groups
-    halo_perm = list(zip(range(n_dev - 1), range(1, n_dev)))
-
     def local_step(u_in, w_in, b_in, conv_taps, w_out, skip_one, skip_two, filt_one, filt_two):
-        rank = lax.axis_index("sp")
         u = u_in[0]
         rows = u.shape[0]
         tables = [jnp.asarray(t) for t in transform_tables(rows * n_dev)]
-
-        halo = lax.ppermute(u[-8:].astype(F32), "sp", halo_perm)
-        has_prev = (rank > 0).astype(jnp.int32)[None]
-        first_unit = lax.axis_index("dp") * units
-        place = jnp.stack([first_unit // n_chan, first_unit % n_chan])
-        share = turn_share(place, filt_one, filt_two, n_dev, n_chunks, units)
-        share, halo = lax.optimization_barrier((share, halo))
-        share = lax.all_to_all(share, "sp", 0, 0, tiled=True)
-        sent, gate = project(has_prev, u, halo, w_in, b_in[None], conv_taps, n_dev, n_chunks)
-        skips = lax.dynamic_slice_in_dim(jnp.stack([skip_one, skip_two]), rank * LANES, LANES, axis=1)
-        back = exchange(skips, share, sent, tables, n_dev, n_groups)
+        sent, gate, share = project(u, filt_one, filt_two, w_in, b_in[None], conv_taps, n_dev, n_groups, n_chunks, units)
+        back = exchange(skip_one, skip_two, share, sent, tables, n_dev, n_groups)
         back = back.reshape(n_chunks, n_dev, rows // LANES, LANES // n_chunks, LANES)
         return finish(gate, u, w_out, back)[None]
 

time: 413 us -> 398 us (0.964)
  waiting for transfers between devices: 33.5 us -> 0 us
  Pallas kernels: 367 us -> 398 us
  starting transfers between devices: 9.65 us -> 0 us
    all_to_all x1 -> x0, waiting for transfers between devices: 33.5 us -> none  [local_step(): share = lax.all_to_all(share, 'sp', 0, 0, tiled=True)]
    pallas_call x2 -> x1, Pallas kernels: 75.9 us -> 107 us  [project(): pl.pallas_call(functools.partial(project_body, n_dev, n_groups, n_chunks,...]
    all_to_all x1 -> x0, starting transfers between devices: 5.06 us -> none  [local_step(): share = lax.all_to_all(share, 'sp', 0, 0, tiled=True)]
    ppermute x1 -> x0, starting transfers between devices: 4.59 us -> none  [local_step(): halo = lax.ppermute(u[-8:].astype(F32), 'sp', halo_perm)]
  transfers between devices with their start and end apart: 2 -> 0, of which waited for: 1 -> 0; matrix products, arithmetic and copies ran while one was open for 0% -> 0% of each run, Pallas kernels for 18% -> 0%
where the time goes in v4:
time: 398 us
  Pallas kernels  398 us (100%)
    pallas_call x1, Pallas kernels, exchange(): pl.pallas_call(functools.partial(exchange_body, n_dev, n_groups, group),...  279 us
    pallas_call x1, Pallas kernels, project(): pl.pallas_call(functools.partial(project_body, n_dev, n_groups, n_chunks,...  107 us
    pallas_call x1, Pallas kernels, finish(): pl.pallas_call(finish_body, grid=(rows // tile,), in_specs=[pl.BlockSpec(...  12.3 us

profile of v4, /device:TPU:113, one launch (start us, length us, event | category | flops | bytes accessed | tf_op | source)
XLA Modules:
  0.0 397.7 jit_solution(17784487679299782215)
XLA Ops:
  0.0 106.5 %project.1 = (f32[8,8,2,256,128]{4,3,2,1,0:T(8,128)}, bf16[2048,1024]{1,0:T(8,128)(2,1)}, f32[8,8,256,128]{3,2,1,0:T(8,128)}) custom-call(bf16[2048,1024]{1,0:T(8,128)(2,1)} %bitcast.5, f32[2048,1024]{1,0:T(8,128)} %one_ref.1, f32[2048,1024]{1,0:T(8,128)} %two_ref.1, bf16[1024,3072]{1,0:T(8,128)(2,1)} %refs_2_.1, bf16[1024,3072]{1,0:T(8,128)(2,1)} %refs_2_.1, ...), custom_call_target="tpu_custom_call" | custom-call | flops 12884901888 | bytes 52428800 | tf_op jit(solution)/shard_map/project/pallas_call | solution.py:225
  106.5 0.0 copy-start
  106.6 278.8 %exchange.1 = f32[8,8,256,128]{3,2,1,0:T(8,128)} custom-call(f32[1024]{0:T(1024)} %skip_one_ref.1, f32[1024]{0:T(1024)} %skip_two_ref.1, f32[8,8,256,128]{3,2,1,0:T(8,128)} %get-tuple-element.9.share_ref, f32[8,8,2,256,128]{4,3,2,1,0:T(8,128)} %get-tuple-element.10.sent_ref, bf16[256,768]{1,0:T(8,128)(2,1)} %constant.12.clone.wide_ref, ...), custom_call_target="tpu_custom_call" | custom-call | flops 99999997952 | bytes 41943040 | tf_op jit(solution)/shard_map/exchange/pallas_call | solution.py:448
  385.4 0.0 copy-done
  385.4 12.3 %finish.1 = bf16[2048,1024]{1,0:T(8,128)(2,1)} custom-call(bf16[2048,1024]{1,0:T(8,128)(2,1)} %get-tuple-element.8.gate_ref, bf16[2048,1024]{1,0:T(8,128)(2,1)} %bitcast.6, bf16[1024,1024]{1,0:T(8,128)(2,1)S(1)} %copy-done, f32[8,8,16,16,128]{4,3,2,1,0:T(8,128)} %bitcast.4), custom_call_target="tpu_custom_call" | custom-call | flops 4294967296 | bytes 20971520 | tf_op jit(solution)/shard_map/finish/pallas_call | solution.py:487
Async XLA Ops:
  106.5 278.8 %copy-start = (bf16[1024,1024]{1,0:T(8,128)(2,1)S(1)}, bf16[1024,1024]{1,0:T(8,128)(2,1)}, u32[]{:S(2)}) copy-start(bf16[1024,1024]{1,0:T(8,128)(2,1)} %w_ref.1) | copy-start | bytes 6291460

commit v5 on v4

--- a/solution.py
+++ b/solution.py
@@ -1,4 +1,5 @@
 import functools
+import math
 import jax
 import jax.numpy as jnp
 import numpy as np
@@ -61,74 +62,83 @@
         into_ref[k, pl.ds(row, n_chan, stride=n_rows), :] = turned[k * n_chan : (k + 1) * n_chan]
 
 
-def share_filters(n_dev, n_groups, n_chunks, units, filt_refs, u_ref, share_ref, halo_ref, tail_ref, stage_ref, hold_ref, full_ref, sems):
-    stage_sem, sent_sem, share_sem, halo_sem = sems
+def spread_offsets(n_dev):
+    pairs = [off for near in range(2, n_dev, 4) for off in (near, n_dev - near)]
+    rest = [off for off in range(1, n_dev) if off not in pairs]
+    rest.sort(key=lambda off: -min(off, n_dev - off))
+    order = list(dict.fromkeys(pairs)) + rest
+    return order
+
+
+def share_filters(n_dev, n_groups, n_chunks, units, filt_refs, u_hbm_ref, u_ref, share_ref, halo_ref, tail_ref, stage_ref, hold_ref, full_ref, sems):
+    stage_sem, sent_sem, share_sem, halo_sem, u_sem = sems
     me, my_group = lax.axis_index("sp"), lax.axis_index("dp")
     rows = stage_ref.shape[1]
     n_rows = rows // LANES
     n_chan = LANES // n_chunks
     first_unit = my_group * units
     which_mine = first_unit // n_chan
-    per_dest = 2 if units == 2 * n_chan else 1
-    n_items = n_dev * per_dest
+    both = units == 2 * n_chan
+    items = [(off, which) for off in spread_offsets(n_dev) + [0] for which in ((0, 1) if both else (None,))]
 
     def target(off):
         return lax.rem(me + off, n_dev)
 
-    def load(item, start):
-        slot = lax.rem(item, 2)
-        dest = target(item // per_dest + 1)
-        cols = pl.ds(pl.multiple_of(dest * LANES, LANES), LANES)
-
-        def copy(ref):
-            return pltpu.make_async_copy(ref.at[:, cols], stage_ref.at[slot], stage_sem.at[slot])
-
-        if not start:
-            copy(filt_refs[0]).wait()
+    def loading(item, which):
+        cols = pl.ds(pl.multiple_of(target(items[item][0]) * LANES, LANES), LANES)
+        return pltpu.make_async_copy(filt_refs[which].at[:, cols], stage_ref.at[item % 2], stage_sem.at[item % 2])
+
+    def load(item):
+        if both:
+            loading(item, items[item][1]).start()
             return
-        which = lax.rem(item, 2) if per_dest == 2 else which_mine
-        for w, ref in enumerate(filt_refs):
-
-            @pl.when(which == w)
+        for which in range(2):
+
+            @pl.when(which_mine == which)
             def _():
-                copy(ref).start()
-
-    load(0, True)
-    tail_ref[...] = u_ref[u_ref.shape[0] - tail_ref.shape[0] :, :].astype(F32)
-
+                loading(item, which).start()
+
+    tail_rows = u_ref.at[pl.ds(rows - 16, 16), :]
+    tail_copy = pltpu.make_async_copy(u_hbm_ref.at[pl.ds(rows - 16, 16), :], tail_rows, u_sem.at[1])
+    head_copy = u_head(u_hbm_ref, u_ref, u_sem)
     barrier = pltpu.get_barrier_semaphore()
     for off in range(1, n_dev):
         pl.semaphore_signal(barrier, inc=1, device_id={"sp": target(off)}, device_id_type=pl.DeviceIdType.MESH)
-    pl.semaphore_wait(barrier, n_dev - 1)
-    halo_send(target, tail_ref, halo_ref, halo_sem).start()
-
-    @pl.loop(0, n_items)
-    def _(item):
-        slot = lax.rem(item, 2)
-        off = item // per_dest + 1
+    load(0)
+    tail_copy.start()
+    for item, (off, which) in enumerate(items):
+        if item + 1 < len(items):
+            load(item + 1)
+        if item == 0:
+            head_copy.start()
+        loading(item, 0).wait()
         dest = target(off)
-
-        @pl.when(item + 1 < n_items)
-        def _():
-            load(item + 1, True)
-
-        load(item, False)
         into = hold_ref.at[dest] if units >= n_chan else full_ref
-        base = lax.rem(item, per_dest) * (n_chan * n_rows)
-
-        @pl.loop(0, n_rows)
-        def _(r):
-            turn_rows(stage_ref[slot, pl.ds(pl.multiple_of(r * LANES, LANES), LANES), :], into, n_chunks, base + r, n_rows)
+        base = n_chan * n_rows if which == 1 else 0
+        together = math.gcd(n_rows, 4)
+
+        @pl.loop(0, n_rows // together)
+        def _(i):
+            for j in range(together):
+                r = i * together + j
+                turn_rows(stage_ref[item % 2, pl.ds(pl.multiple_of(r * LANES, LANES), LANES), :], into, n_chunks, base + r, n_rows)
 
         if units < n_chan:
             start = pl.multiple_of(lax.rem(first_unit, n_chan) * n_rows, n_rows)
             hold_ref[dest] = full_ref[:, pl.ds(start, units * n_rows), :]
-
-        @pl.when(jnp.logical_and(lax.rem(item, per_dest) == per_dest - 1, off < n_dev))
-        def _():
+        if item == 0:
+            tail_copy.wait()
+            tail_ref[...] = tail_rows[...].astype(F32)[8:]
+            pl.semaphore_wait(barrier, n_dev - 1)
+            halo_send(target, tail_ref, halo_ref, halo_sem).start()
+        if off and which != 0:
             share_send(me, target, hold_ref, share_ref, sent_sem, share_sem, off).start()
-
     pltpu.make_async_copy(hold_ref.at[me], share_ref.at[me], sent_sem.at[0]).start()
+
+
+def u_head(u_hbm_ref, u_ref, u_sem):
+    rows = u_ref.shape[0] - 16
+    return pltpu.make_async_copy(u_hbm_ref.at[pl.ds(0, rows), :], u_ref.at[pl.ds(0, rows), :], u_sem.at[0])
 
 
 def share_send(me, target, hold_ref, share_ref, sent_sem, share_sem, off):
@@ -154,10 +164,10 @@
     )
 
 
-def project_body(n_dev, n_groups, n_chunks, units, u_ref, one_ref, two_ref, *refs):
+def project_body(n_dev, n_groups, n_chunks, units, u_hbm_ref, one_ref, two_ref, *refs):
     w_refs, b_refs, tap_refs = refs[:3], refs[3:6], refs[6:9]
-    sent_ref, gate_ref, share_ref, p_ref, halo_ref, tail_ref, stage_ref, hold_ref, full_ref, *sems = refs[9:]
-    stage_sem, sent_sem, share_sem, halo_sem = sems
+    sent_ref, gate_ref, share_ref, u_ref, p_ref, halo_ref, tail_ref, stage_ref, hold_ref, full_ref, *sems = refs[9:]
+    stage_sem, sent_sem, share_sem, halo_sem, u_sem = sems
     rows = u_ref.shape[0]
     n_rows = rows // LANES
     width = w_refs[0].shape[1]
@@ -169,7 +179,8 @@
 
     @pl.when(step_idx == 0)
     def _():
-        share_filters(n_dev, n_groups, n_chunks, units, (one_ref, two_ref), u_ref, share_ref, halo_ref, tail_ref, stage_ref, hold_ref, full_ref, sems)
+        share_filters(n_dev, n_groups, n_chunks, units, (one_ref, two_ref), u_hbm_ref, u_ref, share_ref, halo_ref, tail_ref, stage_ref, hold_ref, full_ref, sems)
+        u_head(u_hbm_ref, u_ref, u_sem).wait()
         halo_send(target, tail_ref, halo_ref, halo_sem).wait()
 
     for which in range(3):
@@ -225,7 +236,7 @@
     return pl.pallas_call(
         functools.partial(project_body, n_dev, n_groups, n_chunks, units),
         grid=(steps,),
-        in_specs=[pl.BlockSpec((rows, depth), lambda j: (0, 0)), any_spec, any_spec, *third(depth), *third(1), *third(3)],
+        in_specs=[any_spec, any_spec, any_spec, *third(depth), *third(1), *third(3)],
         out_specs=[
             pl.BlockSpec((n_chunks, 2, 2, chunk_rows, LANES), lambda j: (0, j, 0, 0, 0)),
             pl.BlockSpec((rows, width), lambda j: (0, j)),
@@ -237,6 +248,7 @@
             jax.ShapeDtypeStruct((n_dev, n_chunks, units * n_rows, LANES), F32),
         ],
         scratch_shapes=[
+            pltpu.VMEM((rows, depth), BF16),
             pltpu.VMEM((rows + 8, width), F32),
             pltpu.VMEM((8, depth), F32),
             pltpu.VMEM((8, depth), F32),
@@ -246,6 +258,7 @@
             pltpu.SemaphoreType.DMA((2,)),
             pltpu.SemaphoreType.DMA((n_dev,)),
             pltpu.SemaphoreType.DMA((n_dev,)),
+            pltpu.SemaphoreType.DMA((2,)),
             pltpu.SemaphoreType.DMA((2,)),
         ],
         cost_estimate=pl.CostEstimate(flops=2 * rows * depth * 3 * model, bytes_accessed=50 * 2**20, transcendentals=0),

time: 398 us -> 393 us (0.987)
  Pallas kernels: 398 us -> 392 us
    pallas_call x1, Pallas kernels: 107 us -> 101 us  [project(): pl.pallas_call(functools.partial(project_body, n_dev, n_groups, n_chunks,...]
where the time goes in v5:
time: 393 us; the launch traced here: 392 us
  Pallas kernels  392 us (100%)
    pallas_call x1, Pallas kernels, exchange(): pl.pallas_call(functools.partial(exchange_body, n_dev, n_groups, group),...  279 us
    pallas_call x1, Pallas kernels, project(): pl.pallas_call(functools.partial(project_body, n_dev, n_groups, n_chunks,...  101 us
    pallas_call x1, Pallas kernels, finish(): pl.pallas_call(finish_body, grid=(rows // tile,), in_specs=[pl.BlockSpec(...  12.3 us

profile of v5, /device:TPU:113, one launch (start us, length us, event | category | flops | bytes accessed | tf_op | source)
XLA Modules:
  0.0 392.3 jit_solution(2873736544984421915)
XLA Ops:
  0.0 101.1 %project.1 = (f32[8,8,2,256,128]{4,3,2,1,0:T(8,128)}, bf16[2048,1024]{1,0:T(8,128)(2,1)}, f32[8,8,256,128]{3,2,1,0:T(8,128)}) custom-call(bf16[2048,1024]{1,0:T(8,128)(2,1)} %bitcast.5, f32[2048,1024]{1,0:T(8,128)} %one_ref.1, f32[2048,1024]{1,0:T(8,128)} %two_ref.1, bf16[1024,3072]{1,0:T(8,128)(2,1)} %refs_2_.1, bf16[1024,3072]{1,0:T(8,128)(2,1)} %refs_2_.1, ...), custom_call_target="tpu_custom_call" | custom-call | flops 12884901888 | bytes 52428800 | tf_op jit(solution)/shard_map/project/pallas_call | solution.py:236
  101.1 0.0 copy-start
  101.1 278.8 %exchange.1 = f32[8,8,256,128]{3,2,1,0:T(8,128)} custom-call(f32[1024]{0:T(1024)} %skip_one_ref.1, f32[1024]{0:T(1024)} %skip_two_ref.1, f32[8,8,256,128]{3,2,1,0:T(8,128)} %get-tuple-element.9.share_ref, f32[8,8,2,256,128]{4,3,2,1,0:T(8,128)} %get-tuple-element.10.sent_ref, bf16[256,768]{1,0:T(8,128)(2,1)} %constant.12.clone.wide_ref, ...), custom_call_target="tpu_custom_call" | custom-call | flops 99999997952 | bytes 41943040 | tf_op jit(solution)/shard_map/exchange/pallas_call | solution.py:461
  379.9 0.0 copy-done
  379.9 12.3 %finish.1 = bf16[2048,1024]{1,0:T(8,128)(2,1)} custom-call(bf16[2048,1024]{1,0:T(8,128)(2,1)} %get-tuple-element.8.gate_ref, bf16[2048,1024]{1,0:T(8,128)(2,1)} %bitcast.6, bf16[1024,1024]{1,0:T(8,128)(2,1)S(1)} %copy-done, f32[8,8,16,16,128]{4,3,2,1,0:T(8,128)} %bitcast.4), custom_call_target="tpu_custom_call" | custom-call | flops 4294967296 | bytes 20971520 | tf_op jit(solution)/shard_map/finish/pallas_call | solution.py:500
Async XLA Ops:
  101.1 278.8 %copy-start = (bf16[1024,1024]{1,0:T(8,128)(2,1)S(1)}, bf16[1024,1024]{1,0:T(8,128)(2,1)}, u32[]{:S(2)}) copy-start(bf16[1024,1024]{1,0:T(8,128)(2,1)} %w_ref.1) | copy-start | bytes 6291460

commit v6 on v5

--- a/solution.py
+++ b/solution.py
@@ -478,41 +478,93 @@
             pltpu.SemaphoreType.DMA((n_chunks, n_dev)),
         ],
         cost_estimate=pl.CostEstimate(flops=10**11, bytes_accessed=40 * 2**20, transcendentals=0),
-        compiler_params=pltpu.CompilerParams(collective_id=1, has_side_effects=True, vmem_limit_bytes=60 * 2**20),
+        compiler_params=pltpu.CompilerParams(collective_id=1, has_side_effects=True, vmem_limit_bytes=50 * 2**20),
         name="exchange",
     )(skip_one, skip_two, share, sent, *tables)
 
 
-def finish_body(gate_ref, u_ref, w_ref, back_ref, out_ref, y_ref):
-    n_chunks, n_src, n_rows, _, _ = back_ref.shape
-    for r in range(n_rows):
-        for s in range(n_src):
-            full = jnp.concatenate([back_ref[k, s, r] for k in range(n_chunks)], axis=0)
-            rows, cols = slice(r * LANES, (r + 1) * LANES), slice(s * LANES, (s + 1) * LANES)
-            y_ref[rows, cols] = (gate_ref[rows, cols].astype(F32) * full.T).astype(BF16)
-    out_ref[...] = (u_ref[...].astype(F32) + dot32(y_ref[...], w_ref[...])).astype(BF16)
+def finish_body(gate_ref, all_back_ref, u_ref, w_ref, out_ref, y_ref, back_bufs, back_sem):
+    _, n_chunks, n_src, n_rows, _, _ = back_bufs.shape
+    step = pl.program_id(0)
+
+    def fetch(idx, slot):
+        rows = pl.ds(pl.multiple_of(idx * n_rows, n_rows), n_rows)
+        return pltpu.make_async_copy(all_back_ref.at[:, :, rows], back_bufs.at[slot], back_sem.at[slot])
+
+    def gather(slot):
+        back_ref = back_bufs.at[slot]
+        for r in range(n_rows):
+            for s in range(n_src):
+                full = jnp.concatenate([back_ref[k, s, r] for k in range(n_chunks)], axis=0)
+                rows, cols = slice(r * LANES, (r + 1) * LANES), slice(s * LANES, (s + 1) * LANES)
+                y_ref[slot, rows, cols] = (gate_ref[rows, cols].astype(F32) * full.T).astype(BF16)
+
+    def emit(slot):
+        out_ref[...] = (u_ref[...].astype(F32) + dot32(y_ref[slot], w_ref[...])).astype(BF16)
+
+    last = pl.num_programs(0) - 1
+
+    @pl.when(step == 0)
+    def _():
+        fetch(0, 0).start()
+
+    for slot in range(2):
+        mine = lax.rem(step, 2) == slot
+
+        @pl.when(jnp.logical_and(mine, step + 1 < last))
+        def _():
+            fetch(step + 1, 1 - slot).start()
+
+        @pl.when(jnp.logical_and(mine, step < last))
+        def _():
+            fetch(step, slot).wait()
+
+        @pl.when(jnp.logical_and(mine, jnp.logical_and(step > 0, step < last)))
+        def _():
+            gather(slot)
+            emit(1 - slot)
+
+    @pl.when(step == 0)
+    def _():
+        gather(0)
+
+    @pl.when(step == last)
+    def _():
+        emit((last - 1) % 2)
 
 
 def finish(gate, u, w_out, back, n_rows=2):
     rows, model = u.shape
     n_chunks, n_src, _, per_chunk, _ = back.shape
     tile = n_rows * LANES
+    steps = rows // tile
+
+    def now(i):
+        return jnp.minimum(i, steps - 1)
+
+    def before(i):
+        return jnp.maximum(i - 1, 0)
+
     return pl.pallas_call(
         finish_body,
-        grid=(rows // tile,),
+        grid=(steps + 1,),
         in_specs=[
-            pl.BlockSpec((tile, model), lambda i: (i, 0)),
-            pl.BlockSpec((tile, model), lambda i: (i, 0)),
+            pl.BlockSpec((tile, model), lambda i: (now(i), 0)),
+            pl.BlockSpec(memory_space=pltpu.HBM),
+            pl.BlockSpec((tile, model), lambda i: (before(i), 0)),
             pl.BlockSpec(w_out.shape, lambda i: (0, 0)),
-            pl.BlockSpec((n_chunks, n_src, n_rows, per_chunk, LANES), lambda i: (0, 0, i, 0, 0)),
         ],
-        out_specs=pl.BlockSpec((tile, model), lambda i: (i, 0)),
+        out_specs=pl.BlockSpec((tile, model), lambda i: (before(i), 0)),
         out_shape=jax.ShapeDtypeStruct((rows, model), BF16),
-        scratch_shapes=[pltpu.VMEM((tile, model), BF16)],
+        scratch_shapes=[
+            pltpu.VMEM((2, tile, model), BF16),
+            pltpu.VMEM((2, n_chunks, n_src, n_rows, per_chunk, LANES), F32),
+            pltpu.SemaphoreType.DMA((2,)),
+        ],
         cost_estimate=pl.CostEstimate(flops=2 * rows * model * model, bytes_accessed=20 * 2**20, transcendentals=0),
-        compiler_params=pltpu.CompilerParams(dimension_semantics=("arbitrary",), vmem_limit_bytes=48 * 2**20),
+        compiler_params=pltpu.CompilerParams(dimension_semantics=("arbitrary",), vmem_limit_bytes=40 * 2**20),
         name="finish",
-    )(gate, u, w_out, back)
+    )(gate, back, u, w_out)
 
 
 def solution(mesh):

time: 393 us -> 390 us (level)
  no operation moved by 1% of the time
where the time goes in v6:
time: 390 us
  Pallas kernels  390 us (100%)
    pallas_call x1, Pallas kernels, exchange(): pl.pallas_call(functools.partial(exchange_body, n_dev, n_groups, group),...  278 us
    pallas_call x1, Pallas kernels, project(): pl.pallas_call(functools.partial(project_body, n_dev, n_groups, n_chunks,...  101 us
    pallas_call x1, Pallas kernels, finish(): pl.pallas_call(finish_body, grid=(steps + 1,), in_specs=[pl.BlockSpec((ti...  10.8 us

profile of v6, /device:TPU:113, one launch (start us, length us, event | category | flops | bytes accessed | tf_op | source)
XLA Modules:
  0.0 390.1 jit_solution(18173386054234307608)
XLA Ops:
  0.0 0.0 copy-start.3
  0.0 0.0 copy-start.4
  0.0 0.0 copy-start.5
  0.0 0.0 copy-start.6
  0.0 0.0 copy-start.7
  0.0 0.0 copy-start.8
  0.0 0.0 copy-start.9
  0.1 0.0 copy-start.10
  0.1 101.2 %project.1 = (f32[8,8,2,256,128]{4,3,2,1,0:T(8,128)}, bf16[2048,1024]{1,0:T(8,128)(2,1)}, f32[8,8,256,128]{3,2,1,0:T(8,128)}) custom-call(bf16[2048,1024]{1,0:T(8,128)(2,1)} %bitcast.4, f32[2048,1024]{1,0:T(8,128)} %one_ref.1, f32[2048,1024]{1,0:T(8,128)} %two_ref.1, bf16[1024,3072]{1,0:T(8,128)(2,1)} %refs_2_.1, bf16[1024,3072]{1,0:T(8,128)(2,1)} %refs_2_.1, ...), custom_call_target="tpu_custom_call" | custom-call | flops 12884901888 | bytes 52428800 | tf_op jit(solution)/shard_map/project/pallas_call | solution.py:236
  101.2 0.0 copy-done.3
  101.3 0.0 copy-done.4
  101.3 0.0 copy-done.5
  101.3 0.0 copy-done.6
  101.3 0.0 copy-done.7
  101.3 0.0 copy-done.8
  101.3 0.0 copy-done.9
  101.3 0.0 copy-done.10
  101.3 0.0 copy-start
  101.3 0.0 copy-start.1
  101.3 0.0 copy-start.2
  101.4 277.9 %exchange.1 = f32[8,8,256,128]{3,2,1,0:T(8,128)} custom-call(f32[1024]{0:T(1024)S(1)} %copy-done.3, f32[1024]{0:T(1024)S(1)} %copy-done.4, f32[8,8,256,128]{3,2,1,0:T(8,128)} %get-tuple-element.9.share_ref, f32[8,8,2,256,128]{4,3,2,1,0:T(8,128)} %get-tuple-element.10.sent_ref, bf16[256,768]{1,0:T(8,128)(2,1)S(1)} %copy-done.7, ...), custom_call_target="tpu_custom_call" | custom-call | flops 99999997952 | bytes 41943040 | tf_op jit(solution)/shard_map/exchange/pallas_call | solution.py:461
  379.3 0.0 copy-done
  379.3 0.0 copy-done.1
  379.3 0.0 copy-done.2
  379.3 10.8 %finish.1 = bf16[2048,1024]{1,0:T(8,128)(2,1)} custom-call(bf16[2048,1024]{1,0:T(8,128)(2,1)S(1)} %copy-done.1, f32[8,8,16,16,128]{4,3,2,1,0:T(8,128)} %bitcast.6, bf16[2048,1024]{1,0:T(8,128)(2,1)S(1)} %bitcast.5, bf16[1024,1024]{1,0:T(8,128)(2,1)S(1)} %copy-done.2), custom_call_target="tpu_custom_call" | custom-call | flops 4294967296 | bytes 20971520 | tf_op jit(solution)/shard_map/finish/pallas_call | solution.py:548
Async XLA Ops:
  0.0 101.2 %copy-start.3 = (f32[1024]{0:T(1024)S(1)}, f32[1024]{0:T(1024)}, u32[]{:S(2)}) copy-start(f32[1024]{0:T(1024)} %skip_one_ref.1) | copy-start | bytes 12292
  0.0 101.3 %copy-start.4 = (f32[1024]{0:T(1024)S(1)}, f32[1024]{0:T(1024)}, u32[]{:S(2)}) copy-start(f32[1024]{0:T(1024)} %skip_two_ref.1) | copy-start | bytes 12292
  0.0 101.3 %copy-start.5 = (bf16[768,256]{1,0:T(8,128)(2,1)S(1)}, bf16[768,256]{1,0:T(8,128)(2,1)}, u32[]{:S(2)}) copy-start(bf16[768,256]{1,0:T(8,128)(2,1)} %constant.15.clone.inv_ref) | copy-start | bytes 1179652
  0.0 101.3 %copy-start.6 = (bf16[768,256]{1,0:T(8,128)(2,1)S(1)}, bf16[768,256]{1,0:T(8,128)(2,1)}, u32[]{:S(2)}) copy-start(bf16[768,256]{1,0:T(8,128)(2,1)} %constant.14.clone.fwd_ref) | copy-start | bytes 1179652
  0.0 101.3 %copy-start.7 = (bf16[256,768]{1,0:T(8,128)(2,1)S(1)}, bf16[256,768]{1,0:T(8,128)(2,1)}, u32[]{:S(2)}) copy-start(bf16[256,768]{1,0:T(8,128)(2,1)} %constant.12.clone.wide_ref) | copy-start | bytes 1179652
  0.0 101.3 %copy-start.8 = (bf16[384,256]{1,0:T(8,128)(2,1)S(1)}, bf16[384,256]{1,0:T(8,128)(2,1)}, u32[]{:S(2)}) copy-start(bf16[384,256]{1,0:T(8,128)(2,1)} %constant.16.clone.last_ref) | copy-start | bytes 589828
  0.0 101.3 %copy-start.9 = (bf16[256,384]{1,0:T(8,128)(2,1)S(1)}, bf16[256,384]{1,0:T(8,128)(2,1)}, u32[]{:S(2)}) copy-start(bf16[256,384]{1,0:T(8,128)(2,1)} %constant.13.clone.thin_ref) | copy-start | bytes 589828
  0.1 101.3 %copy-start.10 = (f32[2,128,128]{2,1,0:T(8,128)S(1)}, f32[2,128,128]{2,1,0:T(8,128)}, u32[]{:S(2)}) copy-start(f32[2,128,128]{2,1,0:T(8,128)} %constant.17.clone.twist_ref) | copy-start | bytes 393220
  101.3 277.9 %copy-start = (bf16[1,2048,1024]{2,1,0:T(8,128)(2,1)S(1)}, bf16[1,2048,1024]{2,1,0:T(8,128)(2,1)}, u32[]{:S(2)}) copy-start(bf16[1,2048,1024]{2,1,0:T(8,128)(2,1)} %param.15) | copy-start | bytes 12582916
  101.3 277.9 %copy-start.1 = (bf16[2048,1024]{1,0:T(8,128)(2,1)S(1)}, bf16[2048,1024]{1,0:T(8,128)(2,1)}, u32[]{:S(2)}) copy-start(bf16[2048,1024]{1,0:T(8,128)(2,1)} %get-tuple-element.8.gate_ref) | copy-start | bytes 12582916
  101.3 277.9 %copy-start.2 = (bf16[1024,1024]{1,0:T(8,128)(2,1)S(1)}, bf16[1024,1024]{1,0:T(8,128)(2,1)}, u32[]{:S(2)}) copy-start(bf16[1024,1024]{1,0:T(8,128)(2,1)} %w_ref.1) | copy-start | bytes 6291460

commit v7 on v0

v7 whole, which is shorter than its diff:
```python
import functools
import math
import jax
import jax.numpy as jnp
import numpy as np
from jax import lax
from jax.experimental import pallas as pl
from jax.experimental.pallas import tpu as pltpu
from jax.sharding import PartitionSpec as P

LANES = 128
F32 = jnp.float32
BF16 = jnp.bfloat16


def split_table(table, n_parts=3):
    parts, rest = [], np.asarray(table, np.float64)
    for _ in range(n_parts):
        part = rest.astype(jnp.bfloat16)
        parts.append(part)
        rest = rest - part.astype(np.float64)
    return parts


def transform_tables(seq_len):
    n_high = seq_len // LANES
    quarter = np.arange(n_high)[:, None] + 0.25
    high = 2.0 * np.pi * quarter * np.arange(n_high)[None, :] / n_high
    twist = 2.0 * np.pi * quarter * np.arange(LANES)[None, :] / seq_len
    low = 2.0 * np.pi * np.outer(np.arange(LANES), np.arange(LANES)) / LANES
    first = np.concatenate([np.cos(high), -np.sin(high)], axis=0)
    last = np.concatenate([np.cos(high.T), -np.sin(high.T)], axis=1)
    er, ei = np.cos(low), -np.sin(low)
    fwd = np.block([[er, ei], [-ei, er]])
    inv = np.block([[er, -ei], [ei, er]])
    a, b, c = split_table(first)
    first_wide = np.concatenate([a, a, a, b, b, c], axis=1)
    first_thin = np.concatenate([a, b, c], axis=1)
    fwd_parts = np.concatenate(split_table(fwd), axis=0)
    inv_parts = np.concatenate(split_table(inv), axis=0)
    last_parts = np.concatenate(split_table(last), axis=0)
    twist_tab = np.stack([np.cos(twist), -np.sin(twist)]).astype(np.float32)
    return first_wide, first_thin, fwd_parts, inv_parts, last_parts, twist_tab


def split3(x):
    hi = x.astype(BF16)
    rest = x - hi.astype(F32)
    mid = rest.astype(BF16)
    low = (rest - mid.astype(F32)).astype(BF16)
    return hi, mid, low


def dot32(a, b):
    return jnp.dot(a, b, preferred_element_type=F32)


def turn_rows(block, into_ref, n_chunks, row, n_rows):
    turned = block.T
    n_chan = LANES // n_chunks
    for k in range(n_chunks):
        into_ref[k, pl.ds(row, n_chan, stride=n_rows), :] = turned[k * n_chan : (k + 1) * n_chan]


def spread_offsets(n_dev):
    pairs = [off for near in range(2, n_dev, 4) for off in (near, n_dev - near)]
    rest = [off for off in range(1, n_dev) if off not in pairs]
    rest.sort(key=lambda off: -min(off, n_dev - off))
    return list(dict.fromkeys(pairs)) + rest


def spectrum_tools(group, n_high, tables, parts_ref):
    wide_ref, thin_ref, fwd_ref, inv_ref, last_ref, twist_ref = tables
    wide = 2 * LANES
    scale = 1.0 / (n_high * LANES)

    def complex_dot(tab_ref):
        return (
            dot32(parts_ref[:, 2 * wide :], tab_ref[:wide])
            + dot32(parts_ref[:, wide : 2 * wide], tab_ref[:wide])
            + dot32(parts_ref[:, :wide], tab_ref[wide : 2 * wide])
            + dot32(parts_ref[:, wide : 2 * wide], tab_ref[wide : 2 * wide])
            + dot32(parts_ref[:, :wide], tab_ref[2 * wide :])
            + dot32(parts_ref[:, :wide], tab_ref[:wide])
        )

    def store_parts(g, real, imag):
        for t, (re, im) in enumerate(zip(split3(real), split3(imag))):
            parts_ref[g * n_high : (g + 1) * n_high, 2 * t * LANES : (2 * t + 1) * LANES] = re
            parts_ref[g * n_high : (g + 1) * n_high, (2 * t + 1) * LANES : (2 * t + 2) * LANES] = im

    def spectrum(signals, exact):
        tr, ti = twist_ref[0], twist_ref[1]
        for g in range(0, group, 2):
            pair = jnp.concatenate([signals[g], signals[g + 1]], axis=1)
            if exact:
                short = pair.astype(BF16)
                coarse = dot32(thin_ref[...], jnp.concatenate([short, short, short], axis=0))
            else:
                hi, mid, low = split3(pair)
                coarse = dot32(wide_ref[...], jnp.concatenate([hi, mid, low, hi, mid, hi], axis=0))
            for j in range(2):
                re = coarse[:n_high, j * LANES : (j + 1) * LANES]
                im = coarse[n_high:, j * LANES : (j + 1) * LANES]
                store_parts(g + j, re * tr - im * ti, re * ti + im * tr)
        return complex_dot(fwd_ref)

    def signal(spec_a, spec_b):
        tr, ti = twist_ref[0], twist_ref[1]
        for g in range(group):
            rows = slice(g * n_high, (g + 1) * n_high)
            ar, ai = spec_a[rows, :LANES], spec_a[rows, LANES:]
            br, bi = spec_b[rows, :LANES], spec_b[rows, LANES:]
            store_parts(g, ar * br - ai * bi, ar * bi + ai * br)
        fine = complex_dot(inv_ref)
        results = []
        for g in range(0, group, 2):
            halves = []
            for j in range(2):
                rows = slice((g + j) * n_high, (g + j + 1) * n_high)
                re, im = fine[rows, :LANES] * scale, fine[rows, LANES:] * scale
                halves.append(jnp.concatenate([re * tr + im * ti, im * tr - re * ti], axis=0))
            hi, mid, low = split3(jnp.concatenate(halves, axis=1))
            d_hi = dot32(last_ref[...], hi)
            d_mid = dot32(last_ref[: 2 * n_high], mid)
            d_low = dot32(last_ref[:n_high], low)
            small = d_hi[2 * n_high :] + d_mid[n_high:] + d_low
            total = d_hi[:n_high] + ((d_hi[n_high : 2 * n_high] + d_mid[:n_high]) + small)
            results += [total[:, :LANES], total[:, LANES:]]
        return results

    return spectrum, signal


def hyena_body(n_dev, n_groups, units, group, u_hbm_ref, one_ref, two_ref, w_hbm_ref, *refs):
    consts_in, refs = refs[:10], refs[10:]
    consts, const_sem, refs = refs[4:14], refs[14], refs[:4] + refs[15:]
    skip_one_ref, skip_two_ref, bias_ref, taps_ref, *tables = consts
    sent_ref, gate_ref, got_ref, back_ref = refs[:4]
    u_ref, w_ref, p_ref, stage_ref, turned_ref, mixed_ref, halo_ref, tail_ref = refs[4:12]
    filt_ref, block_ref, done_ref, parts_ref, spec_one_ref, spec_two_ref = refs[12:18]
    (u_sem, w_sem, stage_sem, out_sem, halo_sem, hold_sem, share_sem, group_sem, filt_sem, sent_sem, got_sem, block_sem, done_sem, back_sem) = refs[18:]
    me, my_group = lax.axis_index("sp"), lax.axis_index("dp")
    rows, depth = u_ref.shape
    n_rows = rows // LANES
    n_chunks = n_dev
    n_chan = LANES // n_chunks
    n_high = n_dev * n_rows
    model = w_hbm_ref.shape[1] // 3
    width = w_ref.shape[2]
    steps = model // width
    share_rows = units * n_rows
    first_unit = my_group * units
    which_mine = first_unit // n_chan
    mesh_id = pl.DeviceIdType.MESH

    def target(off):
        return lax.rem(me + off, n_dev)

    def own_rows(first):
        return pl.ds(pl.multiple_of(first * share_rows, share_rows), share_rows)


    def loading(item, off, which):
        cols = pl.ds(pl.multiple_of(target(off) * LANES, LANES), LANES)
        return pltpu.make_async_copy((one_ref, two_ref)[which].at[:, cols], stage_ref.at[item % 2], stage_sem.at[item % 2])

    def weights(which, step):
        cols = pl.ds(pl.multiple_of(which * model + step * width, width), width)
        slot = lax.rem(which + step, 2)
        return pltpu.make_async_copy(w_hbm_ref.at[:, cols], w_ref.at[slot], w_sem.at[slot])

    def u_part(start, size, idx):
        return pltpu.make_async_copy(u_hbm_ref.at[pl.ds(start, size), :], u_ref.at[pl.ds(start, size), :], u_sem.at[idx])

    def halo_send():
        return pltpu.make_async_remote_copy(tail_ref, halo_ref, halo_sem.at[0], halo_sem.at[1], device_id={"sp": target(1)}, device_id_type=mesh_id)

    def hold_of(dest):
        return done_ref.at[dest, :, pl.ds(0, share_rows), :]

    def share_send(off):
        dest = target(off)
        return pltpu.make_async_remote_copy(
            hold_of(dest), filt_ref.at[:, me, own_rows(my_group), :], hold_sem.at[off], share_sem.at[off], device_id={"sp": dest}, device_id_type=mesh_id
        )

    def group_send(k, off):
        mine = filt_ref.at[k, :, own_rows(my_group), :]
        return pltpu.make_async_remote_copy(
            mine, mine, group_sem.at[k], filt_sem.at[k], device_id={"dp": lax.rem(my_group + off, n_groups)}, device_id_type=mesh_id
        )

    def other_groups(k):
        same_size = filt_ref.at[k, :, pl.ds(0, (n_groups - 1) * share_rows), :]
        return pltpu.make_async_copy(same_size, same_size, filt_sem.at[k])

    def turned_out(slot, step):
        return pltpu.make_async_copy(turned_ref.at[slot], sent_ref.at[:, pl.ds(step * (width // LANES), width // LANES), slot], out_sem.at[slot])

    def mixed_out(step):
        cols = pl.ds(pl.multiple_of(step * width, width), width)
        return pltpu.make_async_copy(mixed_ref, gate_ref.at[:, cols], out_sem.at[2])

    def sending(k, off):
        dest = target(off)
        return pltpu.make_async_remote_copy(
            sent_ref.at[k, dest], got_ref.at[k, me], sent_sem.at[k, off], got_sem.at[k, off], device_id={"sp": dest}, device_id_type=mesh_id
        )

    def block_in(k, off):
        src = lax.rem(me - off + n_dev, n_dev)
        from_ref = got_ref if off else sent_ref
        return pltpu.make_async_copy(from_ref.at[k, src], block_ref.at[src], block_sem.at[off])

    def returning(k, off):
        dest = target(off)
        return pltpu.make_async_remote_copy(
            done_ref.at[k, dest], back_ref.at[k, me], done_sem.at[k, off], back_sem.at[k, off], device_id={"sp": dest}, device_id_type=mesh_id
        )

    def storing(k):
        return pltpu.make_async_copy(done_ref.at[k, me], back_ref.at[k, me], done_sem.at[k, 0])

    def constant(idx):
        return pltpu.make_async_copy(consts_in[idx], consts[idx], const_sem.at[idx])


    barrier = pltpu.get_barrier_semaphore()
    for off in range(1, n_dev):
        pl.semaphore_signal(barrier, inc=1, device_id={"sp": target(off)}, device_id_type=mesh_id)
    for off in range(1, n_groups):
        pl.semaphore_signal(barrier, inc=1, device_id={"dp": lax.rem(my_group + off, n_groups)}, device_id_type=mesh_id)

    order = spread_offsets(n_dev) + [0]

    def load(item):
        for which in range(2):

            @pl.when(which_mine == which)
            def _():
                loading(item, order[item], which).start()

    load(0)
    u_part(rows - 16, 16, 1).start()
    for item, off in enumerate(order):
        if item + 1 < len(order):
            load(item + 1)
        if item == 0:
            u_part(0, rows - 16, 0).start()
            weights(0, 0).start()
            for idx in range(len(consts)):
                constant(idx).start()
        loading(item, off, 0).wait()
        if units < n_chan:
            into = turned_ref.at[0, :, 0]
        elif off:
            into = done_ref.at[target(off)]
        else:
            into = filt_ref.at[:, me, own_rows(my_group), :]
        together = math.gcd(n_rows, 4)

        @pl.loop(0, n_rows // together)
        def _(i):
            for j in range(together):
                r = i * together + j
                turn_rows(stage_ref[item % 2, pl.ds(pl.multiple_of(r * LANES, LANES), LANES), :], into, n_chunks, r, n_rows)

        if units < n_chan:
            start = pl.multiple_of(lax.rem(first_unit, n_chan) * n_rows, n_rows)
            share = turned_ref[0, :, 0, pl.ds(start, share_rows), :]
            if off:
                done_ref[target(off), :, pl.ds(0, share_rows), :] = share
            else:
                filt_ref[:, me, own_rows(my_group), :] = share
        if item == 0:
            u_part(rows - 16, 16, 1).wait()
            tail_ref[...] = u_ref[pl.ds(rows - 16, 16), :].astype(F32)[8:]
            pl.semaphore_wait(barrier, n_dev + n_groups - 2)
            halo_send().start()
        if off:
            share_send(off).start()


    for idx in range(len(consts)):
        constant(idx).wait()
    u_part(0, rows - 16, 0).wait()
    halo_send().wait()

    @pl.loop(0, steps)
    def _(step):
        for which in range(3):
            if which < 2:
                weights(which + 1, step).start()
            else:

                @pl.when(step + 1 < steps)
                def _():
                    weights(0, step + 1).start()

            weights(which, step).wait()
            w_now = w_ref.at[lax.rem(which + step, 2)]
            cols = pl.ds(pl.multiple_of(which * model + step * width, width), width)
            bias = bias_ref[:, cols]
            halo = (dot32(halo_ref[...].astype(BF16), w_now[...]) + bias).astype(BF16).astype(F32)
            p_ref[0:8, :] = jnp.where(me > 0, halo, 0.0)
            tile = 2 * LANES

            @pl.loop(0, rows // tile)
            def _(i):
                start = pl.multiple_of(i * tile, tile)
                proj = dot32(u_ref[pl.ds(start, tile), :], w_now[...]) + bias
                p_ref[pl.ds(start + 8, tile), :] = proj.astype(BF16).astype(F32)

            c0, c1, c2 = (taps_ref[t : t + 1, cols] for t in range(3))
            slot = 1 if which == 0 else 0

            @pl.when(step > 0)
            def _():
                if which == 1:
                    mixed_out(step - 1).wait()
                else:
                    turned_out(slot, step - 1).wait()

            @pl.loop(0, n_rows)
            def _(r):
                start = pl.multiple_of(r * LANES, LANES)
                window = p_ref[pl.ds(start, LANES + 8), :]
                mixed = c0 * window[8:] + c1 * window[7:-1] + c2 * window[6:-2]
                mixed = mixed.astype(BF16)
                if which == 1:
                    mixed_ref[pl.ds(start, LANES), :] = mixed
                else:
                    for d in range(width // LANES):
                        block = mixed[:, d * LANES : (d + 1) * LANES].astype(F32)
                        turn_rows(block, turned_ref.at[slot, :, d], n_chunks, r, n_rows)

            if which == 1:
                mixed_out(step).start()
            else:
                turned_out(slot, step).start()

    turned_out(0, steps - 1).wait()
    turned_out(1, steps - 1).wait()
    mixed_out(steps - 1).wait()

    @pl.loop(0, n_chunks)
    def _(k):
        for off in range(1, n_dev):
            sending(k, off).start()


    for off in range(1, n_dev):
        share_send(off).wait()

    @pl.loop(0, n_chunks)
    def _(k):
        for off in range(1, n_groups):
            group_send(k, off).start()


    spectrum, signal = spectrum_tools(group, n_high, tables, parts_ref)

    @pl.loop(0, n_chunks)
    def _(k):
        block_in(k, 0).start()
        for off in range(1, n_dev):
            sending(k, off).wait_recv()
            block_in(k, off).start()
        other_groups(k).wait()
        for off in range(n_dev):
            block_in(k, off).wait()

        @pl.loop(0, n_chan // group)
        def _(i):
            first = i * group

            def load_h(which, g):
                start = pl.multiple_of((which * n_chan + first + g) * n_rows, n_rows)
                return filt_ref[k, :, pl.ds(start, n_rows), :].reshape(n_high, LANES)

            def load_x(which, g):
                start = pl.multiple_of((first + g) * n_rows, n_rows)
                return block_ref[:, which, pl.ds(start, n_rows), :].reshape(n_high, LANES)

            chan = me * LANES + k * n_chan + first
            spec_one_ref[...] = spectrum([load_h(0, g) for g in range(group)], False)
            spec_two_ref[...] = spectrum([load_h(1, g) for g in range(group)], False)
            values = [load_x(0, g) for g in range(group)]
            conv = signal(spectrum(values, True), spec_one_ref)
            gated = [load_x(1, g) * (conv[g] + skip_one_ref[chan + g] * values[g]) for g in range(group)]
            conv = signal(spectrum(gated, False), spec_two_ref)
            for g in range(group):
                result = conv[g] + skip_two_ref[chan + g] * gated[g]
                done_ref[k, :, pl.ds(first + g, n_rows, stride=n_chan), :] = result.reshape(n_dev, n_rows, LANES)

        storing(k).start()
        for off in range(1, n_dev):
            returning(k, off).start()

    @pl.loop(0, n_chunks)
    def _(k):
        for off in range(1, n_dev):
            sending(k, off).wait_send()
            returning(k, off).wait()
        storing(k).wait()
        for off in range(1, n_groups):
            group_send(k, off).wait_send()


def hyena(skip_one, skip_two, u, filt_one, filt_two, w_in, bias, taps, tables, n_dev, n_groups, units, group=4):
    rows, depth = u.shape
    model = w_in.shape[1] // 3
    width = 2 * LANES
    n_rows = rows // LANES
    n_chunks = n_dev
    n_high = n_dev * n_rows
    chunk_rows = LANES // n_chunks * n_rows
    hbm_spec = pl.BlockSpec(memory_space=pltpu.HBM)
    consts = (bias, taps, *tables)
    dma = pltpu.SemaphoreType.DMA
    return pl.pallas_call(
        functools.partial(hyena_body, n_dev, n_groups, units, group),
        in_specs=[hbm_spec] * (6 + len(consts)),
        out_specs=[hbm_spec] * 4,
        out_shape=[
            jax.ShapeDtypeStruct((n_chunks, n_dev, 2, chunk_rows, LANES), F32),
            jax.ShapeDtypeStruct((rows, model), BF16),
            jax.ShapeDtypeStruct((n_chunks, n_dev, 2, chunk_rows, LANES), F32),
            jax.ShapeDtypeStruct((n_chunks, n_dev, chunk_rows, LANES), F32),
        ],
        scratch_shapes=[
            pltpu.SMEM(skip_one.shape, F32),
            pltpu.SMEM(skip_two.shape, F32),
            *[pltpu.VMEM(c.shape, c.dtype) for c in consts],
            dma((2 + len(consts),)),
            pltpu.VMEM((rows, depth), BF16),
            pltpu.VMEM((2, depth, width), BF16),
            pltpu.VMEM((rows + 8, width), F32),
            pltpu.VMEM((2, rows, LANES), F32),
            pltpu.VMEM((2, n_chunks, width // LANES, chunk_rows, LANES), F32),
            pltpu.VMEM((rows, width), BF16),
            pltpu.VMEM((8, depth), F32),
            pltpu.VMEM((8, depth), F32),
            pltpu.VMEM((n_chunks, n_dev, 2 * chunk_rows, LANES), F32),
            pltpu.VMEM((n_dev, 2, chunk_rows, LANES), F32),
            pltpu.VMEM((n_chunks, n_dev, chunk_rows, LANES), F32),
            pltpu.VMEM((group * n_high, 6 * LANES), BF16),
            pltpu.VMEM((group * n_high, 2 * LANES), F32),
            pltpu.VMEM((group * n_high, 2 * LANES), F32),
            dma((2,)),
            dma((2,)),
            dma((2,)),
            dma((3,)),
            dma((2,)),
            dma((n_dev,)),
            dma((n_dev,)),
            dma((n_chunks,)),
            dma((n_chunks,)),
            dma((n_chunks, n_dev)),
            dma((n_chunks, n_dev)),
            dma((n_dev,)),
            dma((n_chunks, n_dev)),
            dma((n_chunks, n_dev)),
        ],
        cost_estimate=pl.CostEstimate(flops=10**11, bytes_accessed=100 * 2**20, transcendentals=0),
        compiler_params=pltpu.CompilerParams(collective_id=0, has_side_effects=True, vmem_limit_bytes=54 * 2**20),
        name="hyena",
    )(u, filt_one, filt_two, w_in, skip_one, skip_two, *consts)


def finish_body(all_gate_ref, all_back_ref, u_ref, w_ref, out_ref, y_ref, gate_bufs, back_bufs, back_sem):
    _, n_chunks, n_src, n_rows, _, _ = back_bufs.shape
    step = pl.program_id(0)

    def fetch(idx, slot):
        rows = pl.ds(pl.multiple_of(idx * n_rows, n_rows), n_rows)
        tile = pl.ds(pl.multiple_of(idx * n_rows * LANES, n_rows * LANES), n_rows * LANES)
        return (
            pltpu.make_async_copy(all_back_ref.at[:, :, rows], back_bufs.at[slot], back_sem.at[slot, 0]),
            pltpu.make_async_copy(all_gate_ref.at[tile, :], gate_bufs.at[slot], back_sem.at[slot, 1]),
        )

    def gather(slot):
        back_ref, gate_ref = back_bufs.at[slot], gate_bufs.at[slot]
        for r in range(n_rows):
            for s in range(n_src):
                full = jnp.concatenate([back_ref[k, s, r] for k in range(n_chunks)], axis=0)
                rows, cols = slice(r * LANES, (r + 1) * LANES), slice(s * LANES, (s + 1) * LANES)
                y_ref[slot, rows, cols] = (gate_ref[rows, cols].astype(F32) * full.T).astype(BF16)

    def emit(slot):
        out_ref[...] = (u_ref[...].astype(F32) + dot32(y_ref[slot], w_ref[...])).astype(BF16)

    last = pl.num_programs(0) - 1

    @pl.when(step == 0)
    def _():
        for copy in fetch(0, 0):
            copy.start()

    for slot in range(2):
        mine = lax.rem(step, 2) == slot

        @pl.when(jnp.logical_and(mine, step + 1 < last))
        def _():
            for copy in fetch(step + 1, 1 - slot):
                copy.start()

        @pl.when(jnp.logical_and(mine, step < last))
        def _():
            for copy in fetch(step, slot):
                copy.wait()

        @pl.when(jnp.logical_and(mine, jnp.logical_and(step > 0, step < last)))
        def _():
            gather(slot)
            emit(1 - slot)

    @pl.when(step == 0)
    def _():
        gather(0)

    @pl.when(step == last)
    def _():
        emit((last - 1) % 2)


def finish(gate, u, w_out, back, n_rows=2):
    rows, model = u.shape
    n_chunks, n_src, _, per_chunk, _ = back.shape
    tile = n_rows * LANES
    steps = rows // tile

    def before(i):
        return jnp.maximum(i - 1, 0)

    return pl.pallas_call(
        finish_body,
        grid=(steps + 1,),
        in_specs=[
            pl.BlockSpec(memory_space=pltpu.HBM),
            pl.BlockSpec(memory_space=pltpu.HBM),
            pl.BlockSpec((tile, model), lambda i: (before(i), 0)),
            pl.BlockSpec(w_out.shape, lambda i: (0, 0)),
        ],
        out_specs=pl.BlockSpec((tile, model), lambda i: (before(i), 0)),
        out_shape=jax.ShapeDtypeStruct((rows, model), BF16),
        scratch_shapes=[
            pltpu.VMEM((2, tile, model), BF16),
            pltpu.VMEM((2, tile, model), BF16),
            pltpu.VMEM((2, n_chunks, n_src, n_rows, per_chunk, LANES), F32),
            pltpu.SemaphoreType.DMA((2, 2)),
        ],
        cost_estimate=pl.CostEstimate(flops=2 * rows * model * model, bytes_accessed=20 * 2**20, transcendentals=0),
        compiler_params=pltpu.CompilerParams(dimension_semantics=("arbitrary",), vmem_limit_bytes=48 * 2**20),
        name="finish",
    )(gate, back, u, w_out)


def solution(mesh):
    n_dev, n_groups = mesh.shape["sp"], mesh.shape["dp"]
    n_chunks = n_dev
    n_chan = LANES // n_chunks
    if n_groups < 2 or (2 * n_chan) % n_groups:
        raise ValueError("uneven groups")
    units = 2 * n_chan // n_groups

    def local_step(u_in, w_in, b_in, conv_taps, w_out, skip_one, skip_two, filt_one, filt_two):
        u = u_in[0]
        rows = u.shape[0]
        tables = [jnp.asarray(t) for t in transform_tables(rows * n_dev)]
        _, gate, _, back = hyena(skip_one, skip_two, u, filt_one, filt_two, w_in, b_in[None], conv_taps, tables, n_dev, n_groups, units)
        back = back.reshape(n_chunks, n_dev, rows // LANES, LANES // n_chunks, LANES)
        return finish(gate, u, w_out, back)[None]

    seq_spec = P("dp", "sp", None)
    filt_spec = P("sp", None)
    return jax.shard_map(
        local_step,
        mesh=mesh,
        in_specs=(seq_spec, P(), P(), P(), P(), P(), P(), filt_spec, filt_spec),
        out_specs=seq_spec,
        check_vma=False,
    )
```

time: 5430 us -> 384 us (0.07)
  matrix products: 1850 us -> 0 us
  waiting for transfers between devices: 1300 us -> 0 us
  blocking collectives: 948 us -> 0 us
  local copies, waits for them, and re-layouts: 946 us -> 0.01 us
  Pallas kernels: 0 us -> 384 us
  other arithmetic: 306 us -> 0 us
  starting transfers between devices: 61.3 us -> 0 us
    another operation x51 -> x0, matrix products: 1820 us -> none  [the longest x24 937 us: to_spectrum(): return jnp.fft.fft(lax.complex(pair_parts[0], pair_parts[1]), axis=2)]
    all_to_all x8 -> x0, waiting for transfers between devices: 1230 us -> none  [the longest x4 1050 us: to_spectrum(): lax.all_to_all(jnp.stack([coarse.real, coarse.imag]), 'sp', 2, 3, tiled=T...]
    all_to_all x4 -> x0, blocking collectives: 948 us -> none  [the longest x2 751 us: from_spectrum(): lax.all_to_all(jnp.stack([fine_part.real, fine_part.imag]), 'sp', 3, 2, t...]
    another operation x18 -> x0, local copies, waits for them, and re-layouts: 445 us -> none  [the longest x4 143 us: to_spectrum(): jnp.stack([coarse.real, coarse.imag])]
    pallas_call x0 -> x2, Pallas kernels: none -> 384 us  [the longest x1 371 us: hyena(): pl.pallas_call(functools.partial(hyena_body, n_dev, n_groups, units, grou...]
    slice x23 -> x0, local copies, waits for them, and re-layouts: 234 us -> none  [the longest x12 162 us: to_spectrum(): return jnp.fft.fft(lax.complex(pair_parts[0], pair_parts[1]), axis=2)]
    another operation x16 -> x0, other arithmetic: 200 us -> none  [the longest x4 71.7 us: from_spectrum(): jnp.stack([fine_part.real, fine_part.imag])]
    all_to_all x10 -> x0, local copies, waits for them, and re-layouts: 173 us -> none  [the longest x4 93.4 us: to_spectrum(): lax.all_to_all(jnp.stack([coarse.real, coarse.imag]), 'sp', 2, 3, tiled=T...]
  transfers between devices with their start and end apart: 9 -> 0, of which waited for: 8 -> 0; matrix products, arithmetic and copies ran while one was open for 10% -> 0% of each run, Pallas kernels for 0% -> 0%
where the time goes in v7:
time: 384 us
  Pallas kernels  384 us (100%)
    pallas_call x1, Pallas kernels, hyena(): pl.pallas_call(functools.partial(hyena_body, n_dev, n_groups, units, grou...  371 us
    pallas_call x1, Pallas kernels, finish(): pl.pallas_call(finish_body, grid=(steps + 1,), in_specs=[pl.BlockSpec(mem...  13.1 us

profile of v7, /device:TPU:113, one launch (start us, length us, event | category | flops | bytes accessed | tf_op | source)
XLA Modules:
  0.0 383.6 jit_solution(6932911004606961930)
XLA Ops:
  0.0 0.0 copy-start
  0.0 370.5 %hyena.1 = (f32[8,8,2,256,128]{4,3,2,1,0:T(8,128)}, bf16[2048,1024]{1,0:T(8,128)(2,1)}, f32[8,8,2,256,128]{4,3,2,1,0:T(8,128)}, f32[8,8,256,128]{3,2,1,0:T(8,128)}) custom-call(bf16[2048,1024]{1,0:T(8,128)(2,1)} %bitcast.5, f32[2048,1024]{1,0:T(8,128)} %one_ref.1, f32[2048,1024]{1,0:T(8,128)} %two_ref.1, bf16[1024,3072]{1,0:T(8,128)(2,1)} %w_hbm_ref.1, ...), custom_call_target="tpu_custom_call" | custom-call | flops 99999997952 | bytes 104857600 | tf_op jit(solution)/shard_map/hyena/pallas_call | solution.py:422
  370.5 0.0 copy-done
  370.5 13.1 %finish.1 = bf16[2048,1024]{1,0:T(8,128)(2,1)} custom-call(bf16[2048,1024]{1,0:T(8,128)(2,1)} %get-tuple-element.7.all_gate_ref, f32[8,8,16,16,128]{4,3,2,1,0:T(8,128)} %bitcast.4, bf16[2048,1024]{1,0:T(8,128)(2,1)} %bitcast.6, bf16[1024,1024]{1,0:T(8,128)(2,1)S(1)} %copy-done), custom_call_target="tpu_custom_call" | custom-call | flops 4294967296 | bytes 20971520 | tf_op jit(solution)/shard_map/finish/pallas_call | solution.py:538
Async XLA Ops:
  0.0 370.5 %copy-start = (bf16[1024,1024]{1,0:T(8,128)(2,1)S(1)}, bf16[1024,1024]{1,0:T(8,128)(2,1)}, u32[]{:S(2)}) copy-start(bf16[1024,1024]{1,0:T(8,128)(2,1)} %w_ref.1) | copy-start | bytes 6291460

commit v8 on v7

--- a/solution.py
+++ b/solution.py
@@ -132,14 +132,14 @@
     return spectrum, signal
 
 
-def hyena_body(n_dev, n_groups, units, group, u_hbm_ref, one_ref, two_ref, w_hbm_ref, *refs):
+def hyena_body(n_dev, n_groups, units, group, u_hbm_ref, one_ref, two_ref, w_hbm_ref, w_out_ref, *refs):
     consts_in, refs = refs[:10], refs[10:]
-    consts, const_sem, refs = refs[4:14], refs[14], refs[:4] + refs[15:]
+    consts, const_sem, refs = refs[5:15], refs[15], refs[:5] + refs[16:]
     skip_one_ref, skip_two_ref, bias_ref, taps_ref, *tables = consts
-    sent_ref, gate_ref, got_ref, back_ref = refs[:4]
-    u_ref, w_ref, p_ref, stage_ref, turned_ref, mixed_ref, halo_ref, tail_ref = refs[4:12]
-    filt_ref, block_ref, done_ref, parts_ref, spec_one_ref, spec_two_ref = refs[12:18]
-    (u_sem, w_sem, stage_sem, out_sem, halo_sem, hold_sem, share_sem, group_sem, filt_sem, sent_sem, got_sem, block_sem, done_sem, back_sem) = refs[18:]
+    sent_ref, gate_ref, got_ref, back_ref, sum_ref = refs[:5]
+    u_ref, w_ref, p_ref, stage_ref, turned_ref, mixed_ref, halo_ref, tail_ref = refs[5:13]
+    filt_ref, block_ref, done_ref, parts_ref, spec_one_ref, spec_two_ref, gated_ref, w_pair_ref = refs[13:21]
+    (u_sem, w_sem, stage_sem, out_sem, halo_sem, hold_sem, share_sem, group_sem, filt_sem, sent_sem, got_sem, block_sem, done_sem, back_sem, pair_sem) = refs[21:]
     me, my_group = lax.axis_index("sp"), lax.axis_index("dp")
     rows, depth = u_ref.shape
     n_rows = rows // LANES
@@ -199,8 +199,7 @@
         return pltpu.make_async_copy(turned_ref.at[slot], sent_ref.at[:, pl.ds(step * (width // LANES), width // LANES), slot], out_sem.at[slot])
 
     def mixed_out(step):
-        cols = pl.ds(pl.multiple_of(step * width, width), width)
-        return pltpu.make_async_copy(mixed_ref, gate_ref.at[:, cols], out_sem.at[2])
+        return pltpu.make_async_copy(mixed_ref, gate_ref.at[:, pl.ds(step * (width // LANES), width // LANES)], out_sem.at[2])
 
     def sending(k, off):
         dest = target(off)
@@ -328,12 +327,15 @@
                 window = p_ref[pl.ds(start, LANES + 8), :]
                 mixed = c0 * window[8:] + c1 * window[7:-1] + c2 * window[6:-2]
                 mixed = mixed.astype(BF16)
-                if which == 1:
-                    mixed_ref[pl.ds(start, LANES), :] = mixed
-                else:
-                    for d in range(width // LANES):
-                        block = mixed[:, d * LANES : (d + 1) * LANES].astype(F32)
+                for d in range(width // LANES):
+                    block = mixed[:, d * LANES : (d + 1) * LANES].astype(F32)
+                    if which != 1:
                         turn_rows(block, turned_ref.at[slot, :, d], n_chunks, r, n_rows)
+                        continue
+                    turned = block.T.astype(BF16)
+                    for k in range(n_chunks):
+                        at = pl.ds(pl.multiple_of(r * n_chan, n_chan), n_chan)
+                        mixed_ref[k, d, at, :] = turned[k * n_chan : (k + 1) * n_chan]
 
             if which == 1:
                 mixed_out(step).start()
@@ -402,13 +404,60 @@
     def _(k):
         for off in range(1, n_dev):
             sending(k, off).wait_send()
+        for off in range(1, n_groups):
+            group_send(k, off).wait_send()
+
+
+    tile = filt_ref.shape[2]
+    n_tiles = rows // tile
+
+    @pl.loop(0, n_tiles)
+    def _(q):
+        for e in range(model // LANES):
+            part = u_ref[pl.ds(pl.multiple_of(q * tile, tile), tile), e * LANES : (e + 1) * LANES]
+            filt_ref[e, q] = part.astype(F32)
+
+    def returned(k):
+        for off in range(1, n_dev):
             returning(k, off).wait()
         storing(k).wait()
-        for off in range(1, n_groups):
-            group_send(k, off).wait_send()
-
-
-def hyena(skip_one, skip_two, u, filt_one, filt_two, w_in, bias, taps, tables, n_dev, n_groups, units, group=4):
+
+    def pair_in(k, j):
+        return (
+            pltpu.make_async_copy(back_ref.at[k], block_ref.at[:, j], pair_sem.at[j, 0]),
+            pltpu.make_async_copy(gate_ref.at[k], mixed_ref.at[:, j], pair_sem.at[j, 1]),
+            pltpu.make_async_copy(w_out_ref.at[:, k], w_pair_ref.at[j], pair_sem.at[j, 2]),
+        )
+
+    @pl.loop(0, n_chunks // 2 - 1)
+    def _(p):
+        for j in range(2):
+            returned(2 * p + j)
+            for copy in pair_in(2 * p + j, j):
+                copy.start()
+        for j in range(2):
+            for copy in pair_in(2 * p + j, j):
+                copy.wait()
+
+        @pl.loop(0, n_tiles)
+        def _(q):
+            for t in range(tile // LANES):
+                for j in range(2):
+                    at = pl.ds(pl.multiple_of((q * (tile // LANES) + t) * n_chan, n_chan), n_chan)
+                    gated = block_ref[:, j, at, :] * mixed_ref[:, j, at, :].astype(F32)
+                    gated_ref[t * LANES : (t + 1) * LANES, j * LANES : (j + 1) * LANES] = gated.reshape(LANES, LANES).T.astype(BF16)
+            added = dot32(gated_ref[...], w_pair_ref[...].reshape(2 * LANES, model))
+            for e in range(model // LANES):
+                filt_ref[e, q] = filt_ref[e, q] + added[:, e * LANES : (e + 1) * LANES]
+
+    sum_out = pltpu.make_async_copy(filt_ref.at[:, pl.ds(0, n_tiles)], sum_ref, pair_sem.at[0, 0])
+    sum_out.start()
+    for k in range(n_chunks - 2, n_chunks):
+        returned(k)
+    sum_out.wait()
+
+
+def hyena(skip_one, skip_two, u, filt_one, filt_two, w_in, w_out, bias, taps, tables, n_dev, n_groups, units, group=4):
     rows, depth = u.shape
     model = w_in.shape[1] // 3
     width = 2 * LANES
@@ -421,13 +470,14 @@
     dma = pltpu.SemaphoreType.DMA
     return pl.pallas_call(
         functools.partial(hyena_body, n_dev, n_groups, units, group),
-        in_specs=[hbm_spec] * (6 + len(consts)),
-        out_specs=[hbm_spec] * 4,
+        in_specs=[hbm_spec] * (7 + len(consts)),
+        out_specs=[hbm_spec] * 5,
         out_shape=[
             jax.ShapeDtypeStruct((n_chunks, n_dev, 2, chunk_rows, LANES), F32),
-            jax.ShapeDtypeStruct((rows, model), BF16),
+            jax.ShapeDtypeStruct((n_chunks, n_dev, chunk_rows, LANES), BF16),
             jax.ShapeDtypeStruct((n_chunks, n_dev, 2, chunk_rows, LANES), F32),
             jax.ShapeDtypeStruct((n_chunks, n_dev, chunk_rows, LANES), F32),
+            jax.ShapeDtypeStruct((n_chunks, rows // (2 * chunk_rows), 2 * chunk_rows, LANES), F32),
         ],
         scratch_shapes=[
             pltpu.SMEM(skip_one.shape, F32),
@@ -439,7 +489,7 @@
             pltpu.VMEM((rows + 8, width), F32),
             pltpu.VMEM((2, rows, LANES), F32),
             pltpu.VMEM((2, n_chunks, width // LANES, chunk_rows, LANES), F32),
-            pltpu.VMEM((rows, width), BF16),
+            pltpu.VMEM((n_chunks, width // LANES, chunk_rows, LANES), BF16),
             pltpu.VMEM((8, depth), F32),
             pltpu.VMEM((8, depth), F32),
             pltpu.VMEM((n_chunks, n_dev, 2 * chunk_rows, LANES), F32),
@@ -448,6 +498,8 @@
             pltpu.VMEM((group * n_high, 6 * LANES), BF16),
             pltpu.VMEM((group * n_high, 2 * LANES), F32),
             pltpu.VMEM((group * n_high, 2 * LANES), F32),
+            pltpu.VMEM((2 * chunk_rows, 2 * LANES), BF16),
+            pltpu.VMEM((2, n_dev, LANES // n_chunks, model), BF16),
             dma((2,)),
             dma((2,)),
             dma((2,)),
@@ -462,100 +514,49 @@
             dma((n_dev,)),
             dma((n_chunks, n_dev)),
             dma((n_chunks, n_dev)),
+            dma((2, 3)),
         ],
         cost_estimate=pl.CostEstimate(flops=10**11, bytes_accessed=100 * 2**20, transcendentals=0),
         compiler_params=pltpu.CompilerParams(collective_id=0, has_side_effects=True, vmem_limit_bytes=54 * 2**20),
         name="hyena",
-    )(u, filt_one, filt_two, w_in, skip_one, skip_two, *consts)
-
-
-def finish_body(all_gate_ref, all_back_ref, u_ref, w_ref, out_ref, y_ref, gate_bufs, back_bufs, back_sem):
-    _, n_chunks, n_src, n_rows, _, _ = back_bufs.shape
-    step = pl.program_id(0)
-
-    def fetch(idx, slot):
-        rows = pl.ds(pl.multiple_of(idx * n_rows, n_rows), n_rows)
-        tile = pl.ds(pl.multiple_of(idx * n_rows * LANES, n_rows * LANES), n_rows * LANES)
-        return (
-            pltpu.make_async_copy(all_back_ref.at[:, :, rows], back_bufs.at[slot], back_sem.at[slot, 0]),
-            pltpu.make_async_copy(all_gate_ref.at[tile, :], gate_bufs.at[slot], back_sem.at[slot, 1]),
-        )
-
-    def gather(slot):
-        back_ref, gate_ref = back_bufs.at[slot], gate_bufs.at[slot]
-        for r in range(n_rows):
-            for s in range(n_src):
-                full = jnp.concatenate([back_ref[k, s, r] for k in range(n_chunks)], axis=0)
-                rows, cols = slice(r * LANES, (r + 1) * LANES), slice(s * LANES, (s + 1) * LANES)
-                y_ref[slot, rows, cols] = (gate_ref[rows, cols].astype(F32) * full.T).astype(BF16)
-
-    def emit(slot):
-        out_ref[...] = (u_ref[...].astype(F32) + dot32(y_ref[slot], w_ref[...])).astype(BF16)
-
-    last = pl.num_programs(0) - 1
-
-    @pl.when(step == 0)
-    def _():
-        for copy in fetch(0, 0):
-            copy.start()
-
-    for slot in range(2):
-        mine = lax.rem(step, 2) == slot
-
-        @pl.when(jnp.logical_and(mine, step + 1 < last))
-        def _():
-            for copy in fetch(step + 1, 1 - slot):
-                copy.start()
-
-        @pl.when(jnp.logical_and(mine, step < last))
-        def _():
-            for copy in fetch(step, slot):
-                copy.wait()
-
-        @pl.when(jnp.logical_and(mine, jnp.logical_and(step > 0, step < last)))
-        def _():
-            gather(slot)
-            emit(1 - slot)
-
-    @pl.when(step == 0)
-    def _():
-        gather(0)
-
-    @pl.when(step == last)
-    def _():
-        emit((last - 1) % 2)
-
-
-def finish(gate, u, w_out, back, n_rows=2):
-    rows, model = u.shape
-    n_chunks, n_src, _, per_chunk, _ = back.shape
+    )(u, filt_one, filt_two, w_in, w_out, skip_one, skip_two, *consts)
+
+
+def finish_body(sum_ref, gate_ref, back_ref, w_ref, out_ref, gated_ref):
+    n_rows = back_ref.shape[2]
+    for r in range(n_rows):
+        for j in range(2):
+            gated = back_ref[j, :, r] * gate_ref[j, :, r].astype(F32)
+            gated_ref[r * LANES : (r + 1) * LANES, j * LANES : (j + 1) * LANES] = gated.reshape(LANES, LANES).T.astype(BF16)
+    w_pair = jnp.concatenate([w_ref[:, j].reshape(LANES, w_ref.shape[3]) for j in range(2)], axis=0)
+    added = dot32(gated_ref[...], w_pair)
+    for e in range(sum_ref.shape[0]):
+        cols = slice(e * LANES, (e + 1) * LANES)
+        out_ref[:, cols] = (sum_ref[e] + added[:, cols]).astype(BF16)
+
+
+def finish(partial, gate, back, w_out, n_rows=2):
+    n_chunks, n_src, all_rows, n_chan, _ = back.shape
+    rows, model = all_rows * LANES, w_out.shape[3]
     tile = n_rows * LANES
-    steps = rows // tile
-
-    def before(i):
-        return jnp.maximum(i - 1, 0)
-
+    last = n_chunks // 2 - 1
+    pair = pl.BlockSpec((2, n_src, n_rows, n_chan, LANES), lambda i: (last, 0, i, 0, 0))
     return pl.pallas_call(
         finish_body,
-        grid=(steps + 1,),
+        grid=(rows // tile,),
         in_specs=[
-            pl.BlockSpec(memory_space=pltpu.HBM),
-            pl.BlockSpec(memory_space=pltpu.HBM),
-            pl.BlockSpec((tile, model), lambda i: (before(i), 0)),
-            pl.BlockSpec(w_out.shape, lambda i: (0, 0)),
+            pl.BlockSpec((model // LANES, tile, LANES), lambda i: (0, i, 0)),
+            pair,
+            pair,
+            pl.BlockSpec((n_src, 2, n_chan, model), lambda i: (0, last, 0, 0)),
         ],
-        out_specs=pl.BlockSpec((tile, model), lambda i: (before(i), 0)),
+        out_specs=pl.BlockSpec((tile, model), lambda i: (i, 0)),
         out_shape=jax.ShapeDtypeStruct((rows, model), BF16),
-        scratch_shapes=[
-            pltpu.VMEM((2, tile, model), BF16),
-            pltpu.VMEM((2, tile, model), BF16),
-            pltpu.VMEM((2, n_chunks, n_src, n_rows, per_chunk, LANES), F32),
-            pltpu.SemaphoreType.DMA((2, 2)),
-        ],
-        cost_estimate=pl.CostEstimate(flops=2 * rows * model * model, bytes_accessed=20 * 2**20, transcendentals=0),
-        compiler_params=pltpu.CompilerParams(dimension_semantics=("arbitrary",), vmem_limit_bytes=48 * 2**20),
+        scratch_shapes=[pltpu.VMEM((tile, 2 * LANES), BF16)],
+        cost_estimate=pl.CostEstimate(flops=4 * rows * model * LANES, bytes_accessed=16 * 2**20, transcendentals=0),
+        compiler_params=pltpu.CompilerParams(dimension_semantics=("arbitrary",), vmem_limit_bytes=56 * 2**20),
         name="finish",
-    )(gate, back, u, w_out)
+    )(partial, gate, back, w_out)
 
 
 def solution(mesh):
@@ -570,9 +571,12 @@
         u = u_in[0]
         rows = u.shape[0]
         tables = [jnp.asarray(t) for t in transform_tables(rows * n_dev)]
-        _, gate, _, back = hyena(skip_one, skip_two, u, filt_one, filt_two, w_in, b_in[None], conv_taps, tables, n_dev, n_groups, units)
-        back = back.reshape(n_chunks, n_dev, rows // LANES, LANES // n_chunks, LANES)
-        return finish(gate, u, w_out, back)[None]
+        w_blocks = w_out.reshape(n_dev, n_chunks, n_chan, w_out.shape[1])
+        _, gate, _, back, partial = hyena(
+            skip_one, skip_two, u, filt_one, filt_two, w_in, w_blocks, b_in[None], conv_taps, tables, n_dev, n_groups, units
+        )
+        by_row = (n_chunks, n_dev, rows // LANES, n_chan, LANES)
+        return finish(partial.reshape(-1, rows, LANES), gate.reshape(by_row), back.reshape(by_row), w_blocks)[None]
 
     seq_spec = P("dp", "sp", None)
     filt_spec = P("sp", None)

time: 384 us -> 382 us (level)
  Pallas kernels: 384 us -> 380 us
where the time goes in v8:
time: 382 us; the launch traced here: 380 us
  Pallas kernels  380 us (99%)
    pallas_call x1, Pallas kernels, hyena(): pl.pallas_call(functools.partial(hyena_body, n_dev, n_groups, units, grou...  370 us
    pallas_call x1, Pallas kernels, finish(): pl.pallas_call(finish_body, grid=(rows // tile,), in_specs=[pl.BlockSpec(...  9.42 us

profile of v8, /device:TPU:113, one launch (start us, length us, event | category | flops | bytes accessed | tf_op | source)
XLA Modules:
  0.0 379.8 jit_solution(18430891809453368262)
XLA Ops:
  0.0 370.4 %hyena.1 = (f32[8,8,2,256,128]{4,3,2,1,0:T(8,128)}, bf16[8,8,256,128]{3,2,1,0:T(8,128)(2,1)}, f32[8,8,2,256,128]{4,3,2,1,0:T(8,128)}, f32[8,8,256,128]{3,2,1,0:T(8,128)}, f32[8,4,512,128]{3,2,1,0:T(8,128)}) custom-call(bf16[2048,1024]{1,0:T(8,128)(2,1)} %bitcast.12, f32[2048,1024]{1,0:T(8,128)} %one_ref.1, f32[2048,1024]{1,0:T(8,128)} %two_ref.1, ...), custom_call_target="tpu_custom_call" | custom-call | flops 99999997952 | bytes 104857600 | tf_op jit(solution)/shard_map/hyena/pallas_call | solution.py:471
  370.4 9.4 %finish.1 = bf16[2048,1024]{1,0:T(8,128)(2,1)} custom-call(f32[8,2048,128]{2,1,0:T(8,128)} %bitcast.8, bf16[8,8,16,16,128]{4,3,2,1,0:T(8,128)(2,1)} %bitcast.9, f32[8,8,16,16,128]{4,3,2,1,0:T(8,128)} %bitcast.7, bf16[8,8,16,1024]{3,2,1,0:T(8,128)(2,1)} %bitcast.11), custom_call_target="tpu_custom_call" | custom-call | flops 1073741824 | bytes 16777216 | tf_op jit(solution)/shard_map/finish/pallas_call | solution.py:544

commit v9 on v8

--- a/solution.py
+++ b/solution.py
@@ -139,7 +139,7 @@
     sent_ref, gate_ref, got_ref, back_ref, sum_ref = refs[:5]
     u_ref, w_ref, p_ref, stage_ref, turned_ref, mixed_ref, halo_ref, tail_ref = refs[5:13]
     filt_ref, block_ref, done_ref, parts_ref, spec_one_ref, spec_two_ref, gated_ref, w_pair_ref = refs[13:21]
-    (u_sem, w_sem, stage_sem, out_sem, halo_sem, hold_sem, share_sem, group_sem, filt_sem, sent_sem, got_sem, block_sem, done_sem, back_sem, pair_sem) = refs[21:]
+    (u_sem, w_sem, stage_sem, out_sem, halo_sem, hold_sem, share_sem, group_sem, filt_sem, sent_sem, got_sem, block_sem, done_sem, back_sem, pair_sem, sum_sem) = refs[21:]
     me, my_group = lax.axis_index("sp"), lax.axis_index("dp")
     rows, depth = u_ref.shape
     n_rows = rows // LANES
@@ -429,7 +429,12 @@
             pltpu.make_async_copy(w_out_ref.at[:, k], w_pair_ref.at[j], pair_sem.at[j, 2]),
         )
 
-    @pl.loop(0, n_chunks // 2 - 1)
+    n_pairs = n_chunks // 2 - 1
+
+    def sum_out(q):
+        return pltpu.make_async_copy(filt_ref.at[:, q], sum_ref.at[:, q], sum_sem.at[q])
+
+    @pl.loop(0, n_pairs)
     def _(p):
         for j in range(2):
             returned(2 * p + j)
@@ -450,11 +455,18 @@
             for e in range(model // LANES):
                 filt_ref[e, q] = filt_ref[e, q] + added[:, e * LANES : (e + 1) * LANES]
 
-    sum_out = pltpu.make_async_copy(filt_ref.at[:, pl.ds(0, n_tiles)], sum_ref, pair_sem.at[0, 0])
-    sum_out.start()
+            @pl.when(p == n_pairs - 1)
+            def _():
+                sum_out(q).start()
+
     for k in range(n_chunks - 2, n_chunks):
         returned(k)
-    sum_out.wait()
+
+    @pl.loop(0, n_tiles)
+    def _(q):
+        if n_pairs == 0:
+            sum_out(q).start()
+        sum_out(q).wait()
 
 
 def hyena(skip_one, skip_two, u, filt_one, filt_two, w_in, w_out, bias, taps, tables, n_dev, n_groups, units, group=4):
@@ -515,6 +527,7 @@
             dma((n_chunks, n_dev)),
             dma((n_chunks, n_dev)),
             dma((2, 3)),
+            dma((rows // (2 * chunk_rows),)),
         ],
         cost_estimate=pl.CostEstimate(flops=10**11, bytes_accessed=100 * 2**20, transcendentals=0),
         compiler_params=pltpu.CompilerParams(collective_id=0, has_side_effects=True, vmem_limit_bytes=54 * 2**20),
@@ -522,39 +535,79 @@
     )(u, filt_one, filt_two, w_in, w_out, skip_one, skip_two, *consts)
 
 
-def finish_body(sum_ref, gate_ref, back_ref, w_ref, out_ref, gated_ref):
-    n_rows = back_ref.shape[2]
-    for r in range(n_rows):
-        for j in range(2):
-            gated = back_ref[j, :, r] * gate_ref[j, :, r].astype(F32)
-            gated_ref[r * LANES : (r + 1) * LANES, j * LANES : (j + 1) * LANES] = gated.reshape(LANES, LANES).T.astype(BF16)
-    w_pair = jnp.concatenate([w_ref[:, j].reshape(LANES, w_ref.shape[3]) for j in range(2)], axis=0)
-    added = dot32(gated_ref[...], w_pair)
-    for e in range(sum_ref.shape[0]):
-        cols = slice(e * LANES, (e + 1) * LANES)
-        out_ref[:, cols] = (sum_ref[e] + added[:, cols]).astype(BF16)
+def finish_body(n_rows, sum_hbm_ref, gate_hbm_ref, back_hbm_ref, w_hbm_ref, out_hbm_ref, *refs):
+    sum_ref, gate_ref, back_ref, w_ref, out_ref, gated_ref, in_sem, w_sem, out_sem = refs
+    first = gate_hbm_ref.shape[0] - 2
+    tile = n_rows * LANES
+    n_tiles = out_ref.shape[0] // tile
+
+    def rows_of(i):
+        return pl.ds(pl.multiple_of(i * tile, tile), tile)
+
+    def tile_in(i):
+        narrow = pl.ds(i * n_rows, n_rows)
+        return (
+            pltpu.make_async_copy(sum_hbm_ref.at[:, rows_of(i)], sum_ref.at[:, rows_of(i)], in_sem.at[i, 0]),
+            pltpu.make_async_copy(gate_hbm_ref.at[pl.ds(first, 2), :, narrow], gate_ref.at[:, :, narrow], in_sem.at[i, 1]),
+            pltpu.make_async_copy(back_hbm_ref.at[pl.ds(first, 2), :, narrow], back_ref.at[:, :, narrow], in_sem.at[i, 2]),
+        )
+
+    def tile_out(i):
+        return pltpu.make_async_copy(out_ref.at[rows_of(i)], out_hbm_ref.at[rows_of(i)], out_sem.at[i])
+
+    w_in = pltpu.make_async_copy(w_hbm_ref.at[:, pl.ds(first, 2)], w_ref, w_sem)
+    w_in.start()
+
+    @pl.loop(0, n_tiles)
+    def _(i):
+        for copy in tile_in(i):
+            copy.start()
+
+    w_in.wait()
+
+    @pl.loop(0, n_tiles)
+    def _(i):
+        for copy in tile_in(i):
+            copy.wait()
+        for r in range(n_rows):
+            for j in range(2):
+                gated = back_ref[j, :, i * n_rows + r] * gate_ref[j, :, i * n_rows + r].astype(F32)
+                gated_ref[r * LANES : (r + 1) * LANES, j * LANES : (j + 1) * LANES] = gated.reshape(LANES, LANES).T.astype(BF16)
+        w_pair = jnp.concatenate([w_ref[:, j].reshape(LANES, w_ref.shape[3]) for j in range(2)], axis=0)
+        added = dot32(gated_ref[...], w_pair)
+        for e in range(sum_ref.shape[0]):
+            cols = slice(e * LANES, (e + 1) * LANES)
+            out_ref[rows_of(i), cols] = (sum_ref[e, rows_of(i)] + added[:, cols]).astype(BF16)
+        tile_out(i).start()
+
+    @pl.loop(0, n_tiles)
+    def _(i):
+        tile_out(i).wait()
 
 
 def finish(partial, gate, back, w_out, n_rows=2):
-    n_chunks, n_src, all_rows, n_chan, _ = back.shape
+    _, n_src, all_rows, n_chan, _ = back.shape
     rows, model = all_rows * LANES, w_out.shape[3]
-    tile = n_rows * LANES
-    last = n_chunks // 2 - 1
-    pair = pl.BlockSpec((2, n_src, n_rows, n_chan, LANES), lambda i: (last, 0, i, 0, 0))
+    n_tiles = all_rows // n_rows
+    hbm_spec = pl.BlockSpec(memory_space=pltpu.HBM)
     return pl.pallas_call(
-        finish_body,
-        grid=(rows // tile,),
-        in_specs=[
-            pl.BlockSpec((model // LANES, tile, LANES), lambda i: (0, i, 0)),
-            pair,
-            pair,
-            pl.BlockSpec((n_src, 2, n_chan, model), lambda i: (0, last, 0, 0)),
+        functools.partial(finish_body, n_rows),
+        in_specs=[hbm_spec] * 4,
+        out_specs=hbm_spec,
+        out_shape=jax.ShapeDtypeStruct((rows, model), BF16),
+        scratch_shapes=[
+            pltpu.VMEM(partial.shape, F32),
+            pltpu.VMEM((2,) + gate.shape[1:], BF16),
+            pltpu.VMEM((2,) + back.shape[1:], F32),
+            pltpu.VMEM((n_src, 2, n_chan, model), BF16),
+            pltpu.VMEM((rows, model), BF16),
+            pltpu.VMEM((n_rows * LANES, 2 * LANES), BF16),
+            pltpu.SemaphoreType.DMA((n_tiles, 3)),
+            pltpu.SemaphoreType.DMA,
+            pltpu.SemaphoreType.DMA((n_tiles,)),
         ],
-        out_specs=pl.BlockSpec((tile, model), lambda i: (i, 0)),
-        out_shape=jax.ShapeDtypeStruct((rows, model), BF16),
-        scratch_shapes=[pltpu.VMEM((tile, 2 * LANES), BF16)],
         cost_estimate=pl.CostEstimate(flops=4 * rows * model * LANES, bytes_accessed=16 * 2**20, transcendentals=0),
-        compiler_params=pltpu.CompilerParams(dimension_semantics=("arbitrary",), vmem_limit_bytes=56 * 2**20),
+        compiler_params=pltpu.CompilerParams(vmem_limit_bytes=56 * 2**20),
         name="finish",
     )(partial, gate, back, w_out)
 

time: 382 us -> 378 us (0.990)
  no operation moved by 1% of the time
where the time goes in v9:
time: 378 us; the launch traced here: 377 us
  Pallas kernels  377 us (100%)
    pallas_call x1, Pallas kernels, hyena(): pl.pallas_call(functools.partial(hyena_body, n_dev, n_groups, units, grou...  370 us

profile of v9, /device:TPU:113, one launch (start us, length us, event | category | flops | bytes accessed | tf_op | source)
XLA Modules:
  0.0 377.3 jit_solution(6736285644257134604)
XLA Ops:
  0.0 370.4 %hyena.1 = (f32[8,8,2,256,128]{4,3,2,1,0:T(8,128)}, bf16[8,8,256,128]{3,2,1,0:T(8,128)(2,1)}, f32[8,8,2,256,128]{4,3,2,1,0:T(8,128)}, f32[8,8,256,128]{3,2,1,0:T(8,128)}, f32[8,4,512,128]{3,2,1,0:T(8,128)}) custom-call(bf16[2048,1024]{1,0:T(8,128)(2,1)} %bitcast.12, f32[2048,1024]{1,0:T(8,128)} %one_ref.1, f32[2048,1024]{1,0:T(8,128)} %two_ref.1, ...), custom_call_target="tpu_custom_call" | custom-call | flops 99999997952 | bytes 104857600 | tf_op jit(solution)/shard_map/hyena/pallas_call | solution.py:483
  370.5 6.8 %finish.1 = bf16[2048,1024]{1,0:T(8,128)(2,1)} custom-call(f32[8,2048,128]{2,1,0:T(8,128)} %bitcast.8, bf16[8,8,16,16,128]{4,3,2,1,0:T(8,128)(2,1)} %bitcast.9, f32[8,8,16,16,128]{4,3,2,1,0:T(8,128)} %bitcast.7, bf16[8,8,16,1024]{3,2,1,0:T(8,128)(2,1)} %bitcast.11), custom_call_target="tpu_custom_call" | custom-call | flops 1073741824 | bytes 16777216 | tf_op jit(solution)/shard_map/finish/pallas_call | solution.py:593

commit v10 on v9

--- a/solution.py
+++ b/solution.py
@@ -62,11 +62,8 @@
         into_ref[k, pl.ds(row, n_chan, stride=n_rows), :] = turned[k * n_chan : (k + 1) * n_chan]
 
 
-def spread_offsets(n_dev):
-    pairs = [off for near in range(2, n_dev, 4) for off in (near, n_dev - near)]
-    rest = [off for off in range(1, n_dev) if off not in pairs]
-    rest.sort(key=lambda off: -min(off, n_dev - off))
-    return list(dict.fromkeys(pairs)) + rest
+def far_first(n_dev):
+    return sorted(range(1, n_dev), key=lambda off: -min(off, n_dev - off))
 
 
 def spectrum_tools(group, n_high, tables, parts_ref):
@@ -231,7 +228,7 @@
     for off in range(1, n_groups):
         pl.semaphore_signal(barrier, inc=1, device_id={"dp": lax.rem(my_group + off, n_groups)}, device_id_type=mesh_id)
 
-    order = spread_offsets(n_dev) + [0]
+    order = far_first(n_dev) + [0]
 
     def load(item):
         for which in range(2):
@@ -348,7 +345,7 @@
 
     @pl.loop(0, n_chunks)
     def _(k):
-        for off in range(1, n_dev):
+        for off in far_first(n_dev):
             sending(k, off).start()
 
 
@@ -397,7 +394,7 @@
                 done_ref[k, :, pl.ds(first + g, n_rows, stride=n_chan), :] = result.reshape(n_dev, n_rows, LANES)
 
         storing(k).start()
-        for off in range(1, n_dev):
+        for off in far_first(n_dev):
             returning(k, off).start()
 
     @pl.loop(0, n_chunks)

time: 378 us -> 377 us (level)
  no operation moved by 1% of the time
where the time goes in v10:
time: 377 us; the launch traced here: 376 us
  Pallas kernels  376 us (100%)
    pallas_call x1, Pallas kernels, hyena(): pl.pallas_call(functools.partial(hyena_body, n_dev, n_groups, units, grou...  369 us

profile of v10, /device:TPU:113, one launch (start us, length us, event | category | flops | bytes accessed | tf_op | source)
XLA Modules:
  0.0 376.0 jit_solution(16499825741817643229)
XLA Ops:
  0.0 369.2 %hyena.1 = (f32[8,8,2,256,128]{4,3,2,1,0:T(8,128)}, bf16[8,8,256,128]{3,2,1,0:T(8,128)(2,1)}, f32[8,8,2,256,128]{4,3,2,1,0:T(8,128)}, f32[8,8,256,128]{3,2,1,0:T(8,128)}, f32[8,4,512,128]{3,2,1,0:T(8,128)}) custom-call(bf16[2048,1024]{1,0:T(8,128)(2,1)} %bitcast.12, f32[2048,1024]{1,0:T(8,128)} %one_ref.1, f32[2048,1024]{1,0:T(8,128)} %two_ref.1, ...), custom_call_target="tpu_custom_call" | custom-call | flops 99999997952 | bytes 104857600 | tf_op jit(solution)/shard_map/hyena/pallas_call | solution.py:480
  369.2 6.8 %finish.1 = bf16[2048,1024]{1,0:T(8,128)(2,1)} custom-call(f32[8,2048,128]{2,1,0:T(8,128)} %bitcast.8, bf16[8,8,16,16,128]{4,3,2,1,0:T(8,128)(2,1)} %bitcast.9, f32[8,8,16,16,128]{4,3,2,1,0:T(8,128)} %bitcast.7, bf16[8,8,16,1024]{3,2,1,0:T(8,128)(2,1)} %bitcast.11), custom_call_target="tpu_custom_call" | custom-call | flops 1073741824 | bytes 16777216 | tf_op jit(solution)/shard_map/finish/pallas_call | solution.py:590

commit v11 on v10

--- a/solution.py
+++ b/solution.py
@@ -131,12 +131,12 @@
 
 def hyena_body(n_dev, n_groups, units, group, u_hbm_ref, one_ref, two_ref, w_hbm_ref, w_out_ref, *refs):
     consts_in, refs = refs[:10], refs[10:]
-    consts, const_sem, refs = refs[5:15], refs[15], refs[:5] + refs[16:]
+    consts, const_sem, refs = refs[6:16], refs[16], refs[:6] + refs[17:]
     skip_one_ref, skip_two_ref, bias_ref, taps_ref, *tables = consts
-    sent_ref, gate_ref, got_ref, back_ref, sum_ref = refs[:5]
-    u_ref, w_ref, p_ref, stage_ref, turned_ref, mixed_ref, halo_ref, tail_ref = refs[5:13]
-    filt_ref, block_ref, done_ref, parts_ref, spec_one_ref, spec_two_ref, gated_ref, w_pair_ref = refs[13:21]
-    (u_sem, w_sem, stage_sem, out_sem, halo_sem, hold_sem, share_sem, group_sem, filt_sem, sent_sem, got_sem, block_sem, done_sem, back_sem, pair_sem, sum_sem) = refs[21:]
+    sent_ref, gate_ref, got_ref, back_ref, sum_ref, most_ref = refs[:6]
+    u_ref, w_ref, p_ref, stage_ref, turned_ref, mixed_ref, halo_ref, tail_ref = refs[6:14]
+    filt_ref, block_ref, done_ref, parts_ref, spec_one_ref, spec_two_ref, gated_ref, w_pair_ref = refs[14:22]
+    (u_sem, w_sem, stage_sem, out_sem, halo_sem, hold_sem, share_sem, group_sem, filt_sem, sent_sem, got_sem, block_sem, done_sem, back_sem, pair_sem, sum_sem, most_sem, piece_sem, piece_got_sem) = refs[22:]
     me, my_group = lax.axis_index("sp"), lax.axis_index("dp")
     rows, depth = u_ref.shape
     n_rows = rows // LANES
@@ -217,6 +217,29 @@
 
     def storing(k):
         return pltpu.make_async_copy(done_ref.at[k, me], back_ref.at[k, me], done_sem.at[k, 0])
+
+    last_pair = n_chunks - 2
+    tile = filt_ref.shape[2]
+    n_tiles = rows // tile
+    piece = tile // LANES * n_chan
+
+    def piece_of(q):
+        return pl.ds(pl.multiple_of(q * piece, piece), piece)
+
+    def returning_rows(q, off):
+        dest = target(off)
+        return pltpu.make_async_remote_copy(
+            done_ref.at[pl.ds(last_pair, 2), dest, piece_of(q)],
+            back_ref.at[pl.ds(last_pair, 2), me, piece_of(q)],
+            piece_sem.at[q, off],
+            piece_got_sem.at[q, off],
+            device_id={"sp": dest},
+            device_id_type=mesh_id,
+        )
+
+    def storing_rows(q):
+        last = pl.ds(last_pair, 2)
+        return pltpu.make_async_copy(done_ref.at[last, me, piece_of(q)], back_ref.at[last, me, piece_of(q)], piece_sem.at[q, 0])
 
     def constant(idx):
         return pltpu.make_async_copy(consts_in[idx], consts[idx], const_sem.at[idx])
@@ -393,9 +416,18 @@
                 result = conv[g] + skip_two_ref[chan + g] * gated[g]
                 done_ref[k, :, pl.ds(first + g, n_rows, stride=n_chan), :] = result.reshape(n_dev, n_rows, LANES)
 
-        storing(k).start()
+        @pl.when(k < last_pair)
+        def _():
+            storing(k).start()
+            for off in far_first(n_dev):
+                returning(k, off).start()
+
+
+    @pl.loop(0, n_tiles)
+    def _(q):
+        storing_rows(q).start()
         for off in far_first(n_dev):
-            returning(k, off).start()
+            returning_rows(q, off).start()
 
     @pl.loop(0, n_chunks)
     def _(k):
@@ -405,36 +437,36 @@
             group_send(k, off).wait_send()
 
 
-    tile = filt_ref.shape[2]
-    n_tiles = rows // tile
-
     @pl.loop(0, n_tiles)
     def _(q):
         for e in range(model // LANES):
             part = u_ref[pl.ds(pl.multiple_of(q * tile, tile), tile), e * LANES : (e + 1) * LANES]
             filt_ref[e, q] = part.astype(F32)
 
-    def returned(k):
-        for off in range(1, n_dev):
-            returning(k, off).wait()
-        storing(k).wait()
-
     def pair_in(k, j):
         return (
             pltpu.make_async_copy(back_ref.at[k], block_ref.at[:, j], pair_sem.at[j, 0]),
             pltpu.make_async_copy(gate_ref.at[k], mixed_ref.at[:, j], pair_sem.at[j, 1]),
-            pltpu.make_async_copy(w_out_ref.at[:, k], w_pair_ref.at[j], pair_sem.at[j, 2]),
-        )
-
-    n_pairs = n_chunks // 2 - 1
-
-    def sum_out(q):
-        return pltpu.make_async_copy(filt_ref.at[:, q], sum_ref.at[:, q], sum_sem.at[q])
-
-    @pl.loop(0, n_pairs)
+            w_pair_in(k, j),
+        )
+
+    def w_pair_in(k, j):
+        return pltpu.make_async_copy(w_out_ref.at[:, k], w_pair_ref.at[j], pair_sem.at[j, 2])
+
+    def product(q):
+        for t in range(tile // LANES):
+            for j in range(2):
+                at = pl.ds(pl.multiple_of((q * (tile // LANES) + t) * n_chan, n_chan), n_chan)
+                gated = block_ref[:, j, at, :] * mixed_ref[:, j, at, :].astype(F32)
+                gated_ref[t * LANES : (t + 1) * LANES, j * LANES : (j + 1) * LANES] = gated.reshape(LANES, LANES).T.astype(BF16)
+        return dot32(gated_ref[...], w_pair_ref[...].reshape(2 * LANES, model))
+
+    @pl.loop(0, n_chunks // 2 - 1)
     def _(p):
         for j in range(2):
-            returned(2 * p + j)
+            storing(2 * p + j).wait()
+            for off in range(1, n_dev):
+                returning(2 * p + j, off).wait()
             for copy in pair_in(2 * p + j, j):
                 copy.start()
         for j in range(2):
@@ -443,27 +475,57 @@
 
         @pl.loop(0, n_tiles)
         def _(q):
-            for t in range(tile // LANES):
-                for j in range(2):
-                    at = pl.ds(pl.multiple_of((q * (tile // LANES) + t) * n_chan, n_chan), n_chan)
-                    gated = block_ref[:, j, at, :] * mixed_ref[:, j, at, :].astype(F32)
-                    gated_ref[t * LANES : (t + 1) * LANES, j * LANES : (j + 1) * LANES] = gated.reshape(LANES, LANES).T.astype(BF16)
-            added = dot32(gated_ref[...], w_pair_ref[...].reshape(2 * LANES, model))
+            added = product(q)
             for e in range(model // LANES):
                 filt_ref[e, q] = filt_ref[e, q] + added[:, e * LANES : (e + 1) * LANES]
 
-            @pl.when(p == n_pairs - 1)
-            def _():
-                sum_out(q).start()
-
-    for k in range(n_chunks - 2, n_chunks):
-        returned(k)
-
-    @pl.loop(0, n_tiles)
+    sum_out = pltpu.make_async_copy(filt_ref.at[:, n_tiles - 1], sum_ref, sum_sem)
+    sum_out.start()
+
+    def rows_of(q):
+        return pl.ds(pl.multiple_of(q * tile, tile), tile)
+
+    def most_out(q):
+        return pltpu.make_async_copy(u_ref.at[rows_of(q)], most_ref.at[rows_of(q)], most_sem.at[q])
+
+    def rows_in(q, j):
+        k = last_pair + j
+        return (
+            pltpu.make_async_copy(back_ref.at[k, :, piece_of(q)], block_ref.at[:, j, piece_of(q)], pair_sem.at[j, 0]),
+            pltpu.make_async_copy(gate_ref.at[k, :, piece_of(q)], mixed_ref.at[:, j, piece_of(q)], pair_sem.at[j, 1]),
+        )
+
+    if n_tiles > 1:
+        for j in range(2):
+            w_pair_in(last_pair + j, j).start()
+        for j in range(2):
+            w_pair_in(last_pair + j, j).wait()
+
+    @pl.loop(0, n_tiles - 1)
     def _(q):
-        if n_pairs == 0:
-            sum_out(q).start()
-        sum_out(q).wait()
+        storing_rows(q).wait()
+        for off in range(1, n_dev):
+            returning_rows(q, off).wait()
+        for j in range(2):
+            for copy in rows_in(q, j):
+                copy.start()
+        for j in range(2):
+            for copy in rows_in(q, j):
+                copy.wait()
+        added = product(q)
+        for e in range(model // LANES):
+            cols = slice(e * LANES, (e + 1) * LANES)
+            u_ref[rows_of(q), cols] = (filt_ref[e, q] + added[:, cols]).astype(BF16)
+        most_out(q).start()
+
+    storing_rows(n_tiles - 1).wait()
+    for off in range(1, n_dev):
+        returning_rows(n_tiles - 1, off).wait()
+    sum_out.wait()
+
+    @pl.loop(0, n_tiles - 1)
+    def _(q):
+        most_out(q).wait()
 
 
 def hyena(skip_one, skip_two, u, filt_one, filt_two, w_in, w_out, bias, taps, tables, n_dev, n_groups, units, group=4):
@@ -474,19 +536,21 @@
     n_chunks = n_dev
     n_high = n_dev * n_rows
     chunk_rows = LANES // n_chunks * n_rows
+    tile = 2 * chunk_rows
     hbm_spec = pl.BlockSpec(memory_space=pltpu.HBM)
     consts = (bias, taps, *tables)
     dma = pltpu.SemaphoreType.DMA
     return pl.pallas_call(
         functools.partial(hyena_body, n_dev, n_groups, units, group),
         in_specs=[hbm_spec] * (7 + len(consts)),
-        out_specs=[hbm_spec] * 5,
+        out_specs=[hbm_spec] * 6,
         out_shape=[
             jax.ShapeDtypeStruct((n_chunks, n_dev, 2, chunk_rows, LANES), F32),
             jax.ShapeDtypeStruct((n_chunks, n_dev, chunk_rows, LANES), BF16),
             jax.ShapeDtypeStruct((n_chunks, n_dev, 2, chunk_rows, LANES), F32),
             jax.ShapeDtypeStruct((n_chunks, n_dev, chunk_rows, LANES), F32),
-            jax.ShapeDtypeStruct((n_chunks, rows // (2 * chunk_rows), 2 * chunk_rows, LANES), F32),
+            jax.ShapeDtypeStruct((model // LANES, tile, LANES), F32),
+            jax.ShapeDtypeStruct((rows, model), BF16),
         ],
         scratch_shapes=[
             pltpu.SMEM(skip_one.shape, F32),
@@ -524,7 +588,10 @@
             dma((n_chunks, n_dev)),
             dma((n_chunks, n_dev)),
             dma((2, 3)),
-            dma((rows // (2 * chunk_rows),)),
+            dma,
+            dma((rows // tile,)),
+            dma((rows // tile, n_dev)),
+            dma((rows // tile, n_dev)),
         ],
         cost_estimate=pl.CostEstimate(flops=10**11, bytes_accessed=100 * 2**20, transcendentals=0),
         compiler_params=pltpu.CompilerParams(collective_id=0, has_side_effects=True, vmem_limit_bytes=54 * 2**20),
@@ -532,81 +599,92 @@
     )(u, filt_one, filt_two, w_in, w_out, skip_one, skip_two, *consts)
 
 
-def finish_body(n_rows, sum_hbm_ref, gate_hbm_ref, back_hbm_ref, w_hbm_ref, out_hbm_ref, *refs):
-    sum_ref, gate_ref, back_ref, w_ref, out_ref, gated_ref, in_sem, w_sem, out_sem = refs
+def finish_body(n_rows, most_hbm_ref, sum_hbm_ref, gate_hbm_ref, back_hbm_ref, w_hbm_ref, out_hbm_ref, *refs):
+    sum_ref, gate_ref, back_ref, w_ref, out_ref, gated_ref, in_sem, w_sem, most_sem, out_sem = refs
     first = gate_hbm_ref.shape[0] - 2
+    rows = out_ref.shape[0]
+    first_row = rows - sum_ref.shape[1]
     tile = n_rows * LANES
-    n_tiles = out_ref.shape[0] // tile
-
-    def rows_of(i):
-        return pl.ds(pl.multiple_of(i * tile, tile), tile)
+    n_tiles = sum_ref.shape[1] // tile
+    n_most = first_row // sum_ref.shape[1]
 
     def tile_in(i):
-        narrow = pl.ds(i * n_rows, n_rows)
+        at = pl.ds(i * tile, tile)
+        narrow, wide = pl.ds(i * n_rows, n_rows), pl.ds(first_row // LANES + i * n_rows, n_rows)
         return (
-            pltpu.make_async_copy(sum_hbm_ref.at[:, rows_of(i)], sum_ref.at[:, rows_of(i)], in_sem.at[i, 0]),
-            pltpu.make_async_copy(gate_hbm_ref.at[pl.ds(first, 2), :, narrow], gate_ref.at[:, :, narrow], in_sem.at[i, 1]),
-            pltpu.make_async_copy(back_hbm_ref.at[pl.ds(first, 2), :, narrow], back_ref.at[:, :, narrow], in_sem.at[i, 2]),
-        )
+            pltpu.make_async_copy(sum_hbm_ref.at[:, at], sum_ref.at[:, at], in_sem.at[i, 0]),
+            pltpu.make_async_copy(gate_hbm_ref.at[pl.ds(first, 2), :, wide], gate_ref.at[:, :, narrow], in_sem.at[i, 1]),
+            pltpu.make_async_copy(back_hbm_ref.at[pl.ds(first, 2), :, wide], back_ref.at[:, :, narrow], in_sem.at[i, 2]),
+        )
+
+    def most(i, out):
+        at = pl.ds(i * sum_ref.shape[1], sum_ref.shape[1])
+        if out:
+            return pltpu.make_async_copy(out_ref.at[at], out_hbm_ref.at[at], most_sem.at[i])
+        return pltpu.make_async_copy(most_hbm_ref.at[at], out_ref.at[at], most_sem.at[i])
 
     def tile_out(i):
-        return pltpu.make_async_copy(out_ref.at[rows_of(i)], out_hbm_ref.at[rows_of(i)], out_sem.at[i])
+        at = pl.ds(first_row + i * tile, tile)
+        return pltpu.make_async_copy(out_ref.at[at], out_hbm_ref.at[at], out_sem.at[i])
 
     w_in = pltpu.make_async_copy(w_hbm_ref.at[:, pl.ds(first, 2)], w_ref, w_sem)
     w_in.start()
-
-    @pl.loop(0, n_tiles)
-    def _(i):
+    for i in range(n_tiles):
         for copy in tile_in(i):
             copy.start()
-
+    for i in range(n_most):
+        most(i, False).start()
     w_in.wait()
-
-    @pl.loop(0, n_tiles)
-    def _(i):
+    w_pair = jnp.concatenate([w_ref[:, j].reshape(LANES, w_ref.shape[3]) for j in range(2)], axis=0)
+    for i in range(n_tiles):
         for copy in tile_in(i):
             copy.wait()
         for r in range(n_rows):
             for j in range(2):
                 gated = back_ref[j, :, i * n_rows + r] * gate_ref[j, :, i * n_rows + r].astype(F32)
                 gated_ref[r * LANES : (r + 1) * LANES, j * LANES : (j + 1) * LANES] = gated.reshape(LANES, LANES).T.astype(BF16)
-        w_pair = jnp.concatenate([w_ref[:, j].reshape(LANES, w_ref.shape[3]) for j in range(2)], axis=0)
         added = dot32(gated_ref[...], w_pair)
         for e in range(sum_ref.shape[0]):
             cols = slice(e * LANES, (e + 1) * LANES)
-            out_ref[rows_of(i), cols] = (sum_ref[e, rows_of(i)] + added[:, cols]).astype(BF16)
+            out_ref[first_row + i * tile : first_row + (i + 1) * tile, cols] = (sum_ref[e, i * tile : (i + 1) * tile] + added[:, cols]).astype(BF16)
         tile_out(i).start()
-
-    @pl.loop(0, n_tiles)
-    def _(i):
+    for i in range(n_most):
+        most(i, False).wait()
+        most(i, True).start()
+    for i in range(n_tiles):
         tile_out(i).wait()
-
-
-def finish(partial, gate, back, w_out, n_rows=2):
-    _, n_src, all_rows, n_chan, _ = back.shape
-    rows, model = all_rows * LANES, w_out.shape[3]
-    n_tiles = all_rows // n_rows
+    for i in range(n_most):
+        most(i, True).wait()
+
+
+def finish(most, partial, gate, back, w_out, n_rows=2):
+    _, n_src, _, n_chan, _ = back.shape
+    rows, model = most.shape
+    last_rows = partial.shape[1]
+    n_tiles = last_rows // (n_rows * LANES)
     hbm_spec = pl.BlockSpec(memory_space=pltpu.HBM)
+    returned = (2, n_src, last_rows // LANES, n_chan, LANES)
     return pl.pallas_call(
         functools.partial(finish_body, n_rows),
-        in_specs=[hbm_spec] * 4,
+        in_specs=[hbm_spec] * 5,
         out_specs=hbm_spec,
         out_shape=jax.ShapeDtypeStruct((rows, model), BF16),
         scratch_shapes=[
             pltpu.VMEM(partial.shape, F32),
-            pltpu.VMEM((2,) + gate.shape[1:], BF16),
-            pltpu.VMEM((2,) + back.shape[1:], F32),
+            pltpu.VMEM(returned, BF16),
+            pltpu.VMEM(returned, F32),
             pltpu.VMEM((n_src, 2, n_chan, model), BF16),
             pltpu.VMEM((rows, model), BF16),
             pltpu.VMEM((n_rows * LANES, 2 * LANES), BF16),
             pltpu.SemaphoreType.DMA((n_tiles, 3)),
             pltpu.SemaphoreType.DMA,
+            pltpu.SemaphoreType.DMA((max(1, rows // last_rows - 1),)),
             pltpu.SemaphoreType.DMA((n_tiles,)),
         ],
-        cost_estimate=pl.CostEstimate(flops=4 * rows * model * LANES, bytes_accessed=16 * 2**20, transcendentals=0),
+        cost_estimate=pl.CostEstimate(flops=4 * last_rows * model * LANES, bytes_accessed=11 * 2**20, transcendentals=0),
         compiler_params=pltpu.CompilerParams(vmem_limit_bytes=56 * 2**20),
         name="finish",
-    )(partial, gate, back, w_out)
+    )(most, partial, gate, back, w_out)
 
 
 def solution(mesh):
@@ -622,11 +700,11 @@
         rows = u.shape[0]
         tables = [jnp.asarray(t) for t in transform_tables(rows * n_dev)]
         w_blocks = w_out.reshape(n_dev, n_chunks, n_chan, w_out.shape[1])
-        _, gate, _, back, partial = hyena(
+        _, gate, _, back, partial, most = hyena(
             skip_one, skip_two, u, filt_one, filt_two, w_in, w_blocks, b_in[None], conv_taps, tables, n_dev, n_groups, units
         )
         by_row = (n_chunks, n_dev, rows // LANES, n_chan, LANES)
-        return finish(partial.reshape(-1, rows, LANES), gate.reshape(by_row), back.reshape(by_row), w_blocks)[None]
+        return finish(most, partial, gate.reshape(by_row), back.reshape(by_row), w_blocks)[None]
 
     seq_spec = P("dp", "sp", None)
     filt_spec = P("sp", None)

time: 377 us -> 377 us (level)
  no operation moved by 1% of the time
where the time goes in v11:
time: 377 us; the launch traced here: 376 us
  Pallas kernels  376 us (100%)
    pallas_call x1, Pallas kernels, hyena(): pl.pallas_call(functools.partial(hyena_body, n_dev, n_groups, units, grou...  371 us

profile of v11, /device:TPU:113, one launch (start us, length us, event | category | flops | bytes accessed | tf_op | source)
XLA Modules:
  0.0 376.0 jit_solution(2261740559868160079)
XLA Ops:
  0.0 370.8 %hyena.1 = (f32[8,8,2,256,128]{4,3,2,1,0:T(8,128)}, bf16[8,8,256,128]{3,2,1,0:T(8,128)(2,1)}, f32[8,8,2,256,128]{4,3,2,1,0:T(8,128)}, f32[8,8,256,128]{3,2,1,0:T...) custom-call(bf16[2048,1024]{1,0:T(8,128)(2,1)} %bitcast.10, f32[2048,1024]{1,0:T(8,128)} %one_ref.1, ...), custom_call_target="tpu_custom_call" | custom-call | flops 99999997952 | bytes 104857600 | tf_op jit(solution)/shard_map/hyena/pallas_call | solution.py:543
  370.8 5.2 %finish.1 = bf16[2048,1024]{1,0:T(8,128)(2,1)} custom-call(bf16[2048,1024]{1,0:T(8,128)(2,1)} %get-tuple-element.9.most_hbm_ref, f32[8,512,128]{2,1,0:T(8,128)} %get-tuple-element.10.sum_hbm_ref, bf16[8,8,16,16,128]{4,3,2,1,0:T(8,128)(2,1)} %bitcast.7, f32[8,8,16,16,128]{4,3,2,1,0:T(8,128)} %bitcast.6, bf16[8,8,16,1024]{3,2,1,0:T(8,128)(2,1)} %bitcast.9), custom_call_target="tpu_custom_call" | custom-call | flops 268435456 | bytes 11534336 | tf_op jit(solution)/shard_map/finish/pallas_call | solution.py:667

commit v12 on v11

--- a/solution.py
+++ b/solution.py
@@ -64,6 +64,15 @@
 
 def far_first(n_dev):
     return sorted(range(1, n_dev), key=lambda off: -min(off, n_dev - off))
+
+
+def send_spans(n_chunks):
+    half = n_chunks // 2
+    return [(k, 1) for k in range(half)] + [(k, 2) for k in range(half, n_chunks, 2)] if half % 2 == 0 else [(k, 1) for k in range(n_chunks)]
+
+
+def row_spans(n_tiles):
+    return [(0, n_tiles - 2), (n_tiles - 2, 1), (n_tiles - 1, 1)] if n_tiles > 2 else [(q, 1) for q in range(n_tiles)]
 
 
 def spectrum_tools(group, n_high, tables, parts_ref):
@@ -198,10 +207,10 @@
     def mixed_out(step):
         return pltpu.make_async_copy(mixed_ref, gate_ref.at[:, pl.ds(step * (width // LANES), width // LANES)], out_sem.at[2])
 
-    def sending(k, off):
-        dest = target(off)
+    def sending(k, off, span):
+        dest, chunks = target(off), pl.ds(k, span)
         return pltpu.make_async_remote_copy(
-            sent_ref.at[k, dest], got_ref.at[k, me], sent_sem.at[k, off], got_sem.at[k, off], device_id={"sp": dest}, device_id_type=mesh_id
+            sent_ref.at[chunks, dest], got_ref.at[chunks, me], sent_sem.at[k, off], got_sem.at[k, off], device_id={"sp": dest}, device_id_type=mesh_id
         )
 
     def block_in(k, off):
@@ -212,34 +221,39 @@
     def returning(k, off):
         dest = target(off)
         return pltpu.make_async_remote_copy(
-            done_ref.at[k, dest], back_ref.at[k, me], done_sem.at[k, off], back_sem.at[k, off], device_id={"sp": dest}, device_id_type=mesh_id
+            done_ref.at[pl.ds(k, 2), dest],
+            back_ref.at[pl.ds(k, 2), me],
+            done_sem.at[k, off],
+            back_sem.at[k, off],
+            device_id={"sp": dest},
+            device_id_type=mesh_id,
         )
 
     def storing(k):
-        return pltpu.make_async_copy(done_ref.at[k, me], back_ref.at[k, me], done_sem.at[k, 0])
+        return pltpu.make_async_copy(done_ref.at[pl.ds(k, 2), me], back_ref.at[pl.ds(k, 2), me], done_sem.at[k, 0])
 
     last_pair = n_chunks - 2
     tile = filt_ref.shape[2]
     n_tiles = rows // tile
     piece = tile // LANES * n_chan
 
-    def piece_of(q):
-        return pl.ds(pl.multiple_of(q * piece, piece), piece)
-
-    def returning_rows(q, off):
+    def piece_of(part):
+        return pl.ds(part[0] * piece, part[1] * piece)
+
+    def returning_rows(part, off):
         dest = target(off)
         return pltpu.make_async_remote_copy(
-            done_ref.at[pl.ds(last_pair, 2), dest, piece_of(q)],
-            back_ref.at[pl.ds(last_pair, 2), me, piece_of(q)],
-            piece_sem.at[q, off],
-            piece_got_sem.at[q, off],
+            done_ref.at[pl.ds(last_pair, 2), dest, piece_of(part)],
+            back_ref.at[pl.ds(last_pair, 2), me, piece_of(part)],
+            piece_sem.at[part[0], off],
+            piece_got_sem.at[part[0], off],
             device_id={"sp": dest},
             device_id_type=mesh_id,
         )
 
-    def storing_rows(q):
+    def storing_rows(part):
         last = pl.ds(last_pair, 2)
-        return pltpu.make_async_copy(done_ref.at[last, me, piece_of(q)], back_ref.at[last, me, piece_of(q)], piece_sem.at[q, 0])
+        return pltpu.make_async_copy(done_ref.at[last, me, piece_of(part)], back_ref.at[last, me, piece_of(part)], piece_sem.at[part[0], 0])
 
     def constant(idx):
         return pltpu.make_async_copy(consts_in[idx], consts[idx], const_sem.at[idx])
@@ -366,10 +380,10 @@
     turned_out(1, steps - 1).wait()
     mixed_out(steps - 1).wait()
 
-    @pl.loop(0, n_chunks)
-    def _(k):
+    spans = send_spans(n_chunks)
+    for k, span in spans:
         for off in far_first(n_dev):
-            sending(k, off).start()
+            sending(k, off, span).start()
 
 
     for off in range(1, n_dev):
@@ -386,8 +400,19 @@
     @pl.loop(0, n_chunks)
     def _(k):
         block_in(k, 0).start()
+        for span in (1, 2):
+            firsts = [first for first, size in spans if size == span]
+            if firsts:
+                begins = jnp.logical_and(k >= firsts[0], k <= firsts[-1])
+                if span == 2:
+                    begins = jnp.logical_and(begins, lax.rem(k - firsts[0], 2) == 0)
+
+                @pl.when(begins)
+                def _():
+                    for off in range(1, n_dev):
+                        sending(k, off, span).wait_recv()
+
         for off in range(1, n_dev):
-            sending(k, off).wait_recv()
             block_in(k, off).start()
         other_groups(k).wait()
         for off in range(n_dev):
@@ -416,23 +441,25 @@
                 result = conv[g] + skip_two_ref[chan + g] * gated[g]
                 done_ref[k, :, pl.ds(first + g, n_rows, stride=n_chan), :] = result.reshape(n_dev, n_rows, LANES)
 
-        @pl.when(k < last_pair)
+        @pl.when(jnp.logical_and(k < last_pair, lax.rem(k, 2) == 1))
         def _():
-            storing(k).start()
+            storing(k - 1).start()
             for off in far_first(n_dev):
-                returning(k, off).start()
-
-
-    @pl.loop(0, n_tiles)
-    def _(q):
-        storing_rows(q).start()
+                returning(k - 1, off).start()
+
+
+    parts = row_spans(n_tiles)
+    for part in parts:
+        storing_rows(part).start()
         for off in far_first(n_dev):
-            returning_rows(q, off).start()
+            returning_rows(part, off).start()
+
+    for k, span in spans:
+        for off in range(1, n_dev):
+            sending(k, off, span).wait_send()
 
     @pl.loop(0, n_chunks)
     def _(k):
-        for off in range(1, n_dev):
-            sending(k, off).wait_send()
         for off in range(1, n_groups):
             group_send(k, off).wait_send()
 
@@ -463,10 +490,10 @@
 
     @pl.loop(0, n_chunks // 2 - 1)
     def _(p):
+        storing(2 * p).wait()
+        for off in range(1, n_dev):
+            returning(2 * p, off).wait()
         for j in range(2):
-            storing(2 * p + j).wait()
-            for off in range(1, n_dev):
-                returning(2 * p + j, off).wait()
             for copy in pair_in(2 * p + j, j):
                 copy.start()
         for j in range(2):
@@ -488,11 +515,11 @@
     def most_out(q):
         return pltpu.make_async_copy(u_ref.at[rows_of(q)], most_ref.at[rows_of(q)], most_sem.at[q])
 
-    def rows_in(q, j):
-        k = last_pair + j
+    def rows_in(part, j):
+        k, at = last_pair + j, piece_of(part)
         return (
-            pltpu.make_async_copy(back_ref.at[k, :, piece_of(q)], block_ref.at[:, j, piece_of(q)], pair_sem.at[j, 0]),
-            pltpu.make_async_copy(gate_ref.at[k, :, piece_of(q)], mixed_ref.at[:, j, piece_of(q)], pair_sem.at[j, 1]),
+            pltpu.make_async_copy(back_ref.at[k, :, at], block_ref.at[:, j, at], pair_sem.at[j, 0]),
+            pltpu.make_async_copy(gate_ref.at[k, :, at], mixed_ref.at[:, j, at], pair_sem.at[j, 1]),
         )
 
     if n_tiles > 1:
@@ -501,26 +528,28 @@
         for j in range(2):
             w_pair_in(last_pair + j, j).wait()
 
-    @pl.loop(0, n_tiles - 1)
-    def _(q):
-        storing_rows(q).wait()
+    for part in parts[:-1]:
+        storing_rows(part).wait()
         for off in range(1, n_dev):
-            returning_rows(q, off).wait()
+            returning_rows(part, off).wait()
         for j in range(2):
-            for copy in rows_in(q, j):
+            for copy in rows_in(part, j):
                 copy.start()
         for j in range(2):
-            for copy in rows_in(q, j):
+            for copy in rows_in(part, j):
                 copy.wait()
-        added = product(q)
-        for e in range(model // LANES):
-            cols = slice(e * LANES, (e + 1) * LANES)
-            u_ref[rows_of(q), cols] = (filt_ref[e, q] + added[:, cols]).astype(BF16)
-        most_out(q).start()
-
-    storing_rows(n_tiles - 1).wait()
+
+        @pl.loop(part[0], part[0] + part[1])
+        def _(q):
+            added = product(q)
+            for e in range(model // LANES):
+                cols = slice(e * LANES, (e + 1) * LANES)
+                u_ref[rows_of(q), cols] = (filt_ref[e, q] + added[:, cols]).astype(BF16)
+            most_out(q).start()
+
+    storing_rows(parts[-1]).wait()
     for off in range(1, n_dev):
-        returning_rows(n_tiles - 1, off).wait()
+        returning_rows(parts[-1], off).wait()
     sum_out.wait()
 
     @pl.loop(0, n_tiles - 1)

time: 377 us -> 376 us (level)
  no operation moved by 1% of the time
where the time goes in v12:
time: 376 us
  Pallas kernels  376 us (100%)
    pallas_call x1, Pallas kernels, hyena(): pl.pallas_call(functools.partial(hyena_body, n_dev, n_groups, units, grou...  370 us

profile of v12, /device:TPU:113, one launch (start us, length us, event | category | flops | bytes accessed | tf_op | source)
XLA Modules:
  0.0 375.7 jit_solution(10486809955818302117)
XLA Ops:
  0.0 370.5 %hyena.1 = (f32[8,8,2,256,128]{4,3,2,1,0:T(8,128)}, bf16[8,8,256,128]{3,2,1,0:T(8,128)(2,1)}, f32[8,8,2,256,128]{4,3,2,1,0:T(8,128)}, f32[8,8,256,128]{3,2,1,0:T...) custom-call(bf16[2048,1024]{1,0:T(8,128)(2,1)} %bitcast.10, f32[2048,1024]{1,0:T(8,128)} %one_ref.1, ...), custom_call_target="tpu_custom_call" | custom-call | flops 99999997952 | bytes 104857600 | tf_op jit(solution)/shard_map/hyena/pallas_call | solution.py:572
  370.5 5.2 %finish.1 = bf16[2048,1024]{1,0:T(8,128)(2,1)} custom-call(bf16[2048,1024]{1,0:T(8,128)(2,1)} %get-tuple-element.9.most_hbm_ref, f32[8,512,128]{2,1,0:T(8,128)} %get-tuple-element.10.sum_hbm_ref, bf16[8,8,16,16,128]{4,3,2,1,0:T(8,128)(2,1)} %bitcast.7, f32[8,8,16,16,128]{4,3,2,1,0:T(8,128)} %bitcast.6, bf16[8,8,16,1024]{3,2,1,0:T(8,128)(2,1)} %bitcast.9), custom_call_target="tpu_custom_call" | custom-call | flops 268435456 | bytes 11534336 | tf_op jit(solution)/shard_map/finish/pallas_call | solution.py:696

commit v13 on v12

--- a/solution.py
+++ b/solution.py
@@ -67,8 +67,7 @@
 
 
 def send_spans(n_chunks):
-    half = n_chunks // 2
-    return [(k, 1) for k in range(half)] + [(k, 2) for k in range(half, n_chunks, 2)] if half % 2 == 0 else [(k, 1) for k in range(n_chunks)]
+    return [(k, 1) for k in range(n_chunks - 2)] + [(n_chunks - 2, 2)]
 
 
 def row_spans(n_tiles):
@@ -215,8 +214,8 @@
 
     def block_in(k, off):
         src = lax.rem(me - off + n_dev, n_dev)
-        from_ref = got_ref if off else sent_ref
-        return pltpu.make_async_copy(from_ref.at[k, src], block_ref.at[src], block_sem.at[off])
+        from_ref, slot = (got_ref if off else sent_ref), lax.rem(k, 2)
+        return pltpu.make_async_copy(from_ref.at[k, src], block_ref.at[slot, src], block_sem.at[slot, off])
 
     def returning(k, off):
         dest = target(off)
@@ -397,23 +396,23 @@
 
     spectrum, signal = spectrum_tools(group, n_high, tables, parts_ref)
 
+    def fetch(k):
+        block_in(k, 0).start()
+        for first, span in spans:
+
+            @pl.when(k == first)
+            def _():
+                for off in range(1, n_dev):
+                    sending(first, off, span).wait_recv()
+
+        for off in range(1, n_dev):
+            block_in(k, off).start()
+
+    fetch(jnp.int32(0))
+
     @pl.loop(0, n_chunks)
     def _(k):
-        block_in(k, 0).start()
-        for span in (1, 2):
-            firsts = [first for first, size in spans if size == span]
-            if firsts:
-                begins = jnp.logical_and(k >= firsts[0], k <= firsts[-1])
-                if span == 2:
-                    begins = jnp.logical_and(begins, lax.rem(k - firsts[0], 2) == 0)
-
-                @pl.when(begins)
-                def _():
-                    for off in range(1, n_dev):
-                        sending(k, off, span).wait_recv()
-
-        for off in range(1, n_dev):
-            block_in(k, off).start()
+        slot = lax.rem(k, 2)
         other_groups(k).wait()
         for off in range(n_dev):
             block_in(k, off).wait()
@@ -422,13 +421,17 @@
         def _(i):
             first = i * group
 
+            @pl.when(jnp.logical_and(i == n_chan // group - 1, k + 1 < n_chunks))
+            def _():
+                fetch(k + 1)
+
             def load_h(which, g):
                 start = pl.multiple_of((which * n_chan + first + g) * n_rows, n_rows)
                 return filt_ref[k, :, pl.ds(start, n_rows), :].reshape(n_high, LANES)
 
             def load_x(which, g):
                 start = pl.multiple_of((first + g) * n_rows, n_rows)
-                return block_ref[:, which, pl.ds(start, n_rows), :].reshape(n_high, LANES)
+                return block_ref[slot, :, which, pl.ds(start, n_rows), :].reshape(n_high, LANES)
 
             chan = me * LANES + k * n_chan + first
             spec_one_ref[...] = spectrum([load_h(0, g) for g in range(group)], False)
@@ -472,7 +475,7 @@
 
     def pair_in(k, j):
         return (
-            pltpu.make_async_copy(back_ref.at[k], block_ref.at[:, j], pair_sem.at[j, 0]),
+            pltpu.make_async_copy(back_ref.at[k], block_ref.at[0, :, j], pair_sem.at[j, 0]),
             pltpu.make_async_copy(gate_ref.at[k], mixed_ref.at[:, j], pair_sem.at[j, 1]),
             w_pair_in(k, j),
         )
@@ -484,7 +487,7 @@
         for t in range(tile // LANES):
             for j in range(2):
                 at = pl.ds(pl.multiple_of((q * (tile // LANES) + t) * n_chan, n_chan), n_chan)
-                gated = block_ref[:, j, at, :] * mixed_ref[:, j, at, :].astype(F32)
+                gated = block_ref[0, :, j, at, :] * mixed_ref[:, j, at, :].astype(F32)
                 gated_ref[t * LANES : (t + 1) * LANES, j * LANES : (j + 1) * LANES] = gated.reshape(LANES, LANES).T.astype(BF16)
         return dot32(gated_ref[...], w_pair_ref[...].reshape(2 * LANES, model))
 
@@ -518,7 +521,7 @@
     def rows_in(part, j):
         k, at = last_pair + j, piece_of(part)
         return (
-            pltpu.make_async_copy(back_ref.at[k, :, at], block_ref.at[:, j, at], pair_sem.at[j, 0]),
+            pltpu.make_async_copy(back_ref.at[k, :, at], block_ref.at[0, :, j, at], pair_sem.at[j, 0]),
             pltpu.make_async_copy(gate_ref.at[k, :, at], mixed_ref.at[:, j, at], pair_sem.at[j, 1]),
         )
 
@@ -595,7 +598,7 @@
             pltpu.VMEM((8, depth), F32),
             pltpu.VMEM((8, depth), F32),
             pltpu.VMEM((n_chunks, n_dev, 2 * chunk_rows, LANES), F32),
-            pltpu.VMEM((n_dev, 2, chunk_rows, LANES), F32),
+            pltpu.VMEM((2, n_dev, 2, chunk_rows, LANES), F32),
             pltpu.VMEM((n_chunks, n_dev, chunk_rows, LANES), F32),
             pltpu.VMEM((group * n_high, 6 * LANES), BF16),
             pltpu.VMEM((group * n_high, 2 * LANES), F32),
@@ -613,7 +616,7 @@
             dma((n_chunks,)),
             dma((n_chunks, n_dev)),
             dma((n_chunks, n_dev)),
-            dma((n_dev,)),
+            dma((2, n_dev)),
             dma((n_chunks, n_dev)),
             dma((n_chunks, n_dev)),
             dma((2, 3)),

time: 376 us -> 376 us (level)
  no operation moved by 1% of the time
where the time goes in v13:
time: 376 us; the launch traced here: 375 us
  Pallas kernels  375 us (100%)
    pallas_call x1, Pallas kernels, hyena(): pl.pallas_call(functools.partial(hyena_body, n_dev, n_groups, units, grou...  370 us

profile of v13, /device:TPU:113, one launch (start us, length us, event | category | flops | bytes accessed | tf_op | source)
XLA Modules:
  0.0 375.1 jit_solution(13304515725217686132)
XLA Ops:
  0.0 369.9 %hyena.1 = (f32[8,8,2,256,128]{4,3,2,1,0:T(8,128)}, bf16[8,8,256,128]{3,2,1,0:T(8,128)(2,1)}, f32[8,8,2,256,128]{4,3,2,1,0:T(8,128)}, f32[8,8,256,128]{3,2,1,0:T...) custom-call(bf16[2048,1024]{1,0:T(8,128)(2,1)} %bitcast.10, f32[2048,1024]{1,0:T(8,128)} %one_ref.1, ...), custom_call_target="tpu_custom_call" | custom-call | flops 99999997952 | bytes 104857600 | tf_op jit(solution)/shard_map/hyena/pallas_call | solution.py:575
  369.9 5.2 %finish.1 = bf16[2048,1024]{1,0:T(8,128)(2,1)} custom-call(bf16[2048,1024]{1,0:T(8,128)(2,1)} %get-tuple-element.9.most_hbm_ref, f32[8,512,128]{2,1,0:T(8,128)} %get-tuple-element.10.sum_hbm_ref, bf16[8,8,16,16,128]{4,3,2,1,0:T(8,128)(2,1)} %bitcast.7, f32[8,8,16,16,128]{4,3,2,1,0:T(8,128)} %bitcast.6, bf16[8,8,16,1024]{3,2,1,0:T(8,128)(2,1)} %bitcast.9), custom_call_target="tpu_custom_call" | custom-call | flops 268435456 | bytes 11534336 | tf_op jit(solution)/shard_map/finish/pallas_call | solution.py:699

commit v14 on v13

--- a/solution.py
+++ b/solution.py
@@ -662,13 +662,18 @@
     w_in = pltpu.make_async_copy(w_hbm_ref.at[:, pl.ds(first, 2)], w_ref, w_sem)
     w_in.start()
     for i in range(n_tiles):
+        if i == n_tiles - 1:
+            for m in range(n_most):
+                most(m, False).start()
         for copy in tile_in(i):
             copy.start()
-    for i in range(n_most):
-        most(i, False).start()
     w_in.wait()
     w_pair = jnp.concatenate([w_ref[:, j].reshape(LANES, w_ref.shape[3]) for j in range(2)], axis=0)
     for i in range(n_tiles):
+        if i == n_tiles - 1:
+            for m in range(n_most):
+                most(m, False).wait()
+                most(m, True).start()
         for copy in tile_in(i):
             copy.wait()
         for r in range(n_rows):
@@ -680,9 +685,6 @@
             cols = slice(e * LANES, (e + 1) * LANES)
             out_ref[first_row + i * tile : first_row + (i + 1) * tile, cols] = (sum_ref[e, i * tile : (i + 1) * tile] + added[:, cols]).astype(BF16)
         tile_out(i).start()
-    for i in range(n_most):
-        most(i, False).wait()
-        most(i, True).start()
     for i in range(n_tiles):
         tile_out(i).wait()
     for i in range(n_most):

time: 376 us -> 376 us (level)
  no operation moved by 1% of the time
where the time goes in v14:
time: 376 us; the launch traced here: 375 us
  Pallas kernels  375 us (100%)
    pallas_call x1, Pallas kernels, hyena(): pl.pallas_call(functools.partial(hyena_body, n_dev, n_groups, units, grou...  370 us

profile of v14, /device:TPU:113, one launch (start us, length us, event | category | flops | bytes accessed | tf_op | source)
XLA Modules:
  0.0 374.9 jit_solution(8894711792731183810)
XLA Ops:
  0.0 369.9 %hyena.1 = (f32[8,8,2,256,128]{4,3,2,1,0:T(8,128)}, bf16[8,8,256,128]{3,2,1,0:T(8,128)(2,1)}, f32[8,8,2,256,128]{4,3,2,1,0:T(8,128)}, f32[8,8,256,128]{3,2,1,0:T...) custom-call(bf16[2048,1024]{1,0:T(8,128)(2,1)} %bitcast.10, f32[2048,1024]{1,0:T(8,128)} %one_ref.1, ...), custom_call_target="tpu_custom_call" | custom-call | flops 99999997952 | bytes 104857600 | tf_op jit(solution)/shard_map/hyena/pallas_call | solution.py:575
  369.9 5.0 %finish.1 = bf16[2048,1024]{1,0:T(8,128)(2,1)} custom-call(bf16[2048,1024]{1,0:T(8,128)(2,1)} %get-tuple-element.9.most_hbm_ref, f32[8,512,128]{2,1,0:T(8,128)} %get-tuple-element.10.sum_hbm_ref, bf16[8,8,16,16,128]{4,3,2,1,0:T(8,128)(2,1)} %bitcast.7, f32[8,8,16,16,128]{4,3,2,1,0:T(8,128)} %bitcast.6, bf16[8,8,16,1024]{3,2,1,0:T(8,128)(2,1)} %bitcast.9), custom_call_target="tpu_custom_call" | custom-call | flops 268435456 | bytes 11534336 | tf_op jit(solution)/shard_map/finish/pallas_call | solution.py:701
